TPU v7x, 256 devices: a 4x2x16 block of a 4x16x16 slice. The times are simulated.
256 devices in a mesh: group: 2 (over y), tensor: 32 (over z, core), seq: 4 (over x).
Axes of the slice: x: 4, y: 2, z: 16, core: 2. Of those that a mesh axis runs over, the one named last changes fastest.
The devices are a block of a 4x16x16 slice.
Arguments:
- mixer_input: bfloat16 [2048, 8192], P(('group', 'seq'), 'tensor'), parts along dimension 0, may hold values from -6 to 6
- state_maps: bfloat16 [2048, 256], P(('group', 'seq')), parts along dimension 0, may hold values from -6 to 6
- gate_input: bfloat16 [2048, 8192], P(('group', 'seq'), 'tensor'), parts along dimension 0, may hold values from -6 to 6
- step_raw: float32 [128, 2048], P('tensor', ('group', 'seq')), parts along dimension 1, may hold values from -10 to 10, as said below
- decay_log: float32 [128], P('tensor'), may hold values from -4 to -2
- skip_gain: float32 [128], P('tensor'), may hold values from 0.5 to 1.5
- conv_input: bfloat16 [4, 8192], P(None, 'tensor'), may hold values from -3 to 3
- conv_maps: bfloat16 [4, 256], replicated, may hold values from -3 to 3
- norm_gain: float32 [8192], P('tensor'), may hold values from 0.1 to 1.9
- out_weight: bfloat16 [8192, 8192], P('tensor'), may hold values from -0.125 to 0.125
Outputs:
- mixed: bfloat16 [2048, 8192], P(('group', 'seq'), 'tensor'), parts along dimension 0
There are 2 independent parts, one for each index of `group`. A program takes and returns all parts, laid end to end along the dimension named above; an argument that names none is the same for every part. Nothing has to cross between parts.
Inputs may be any that keep to these rules, and one draw needn't show every extreme that they name: `step_raw`: Real-valued step parameters before softplus.
All inputs are finite; a program needn't handle non-finite values.
Results may differ from a plain program's by a relative error of at most 0.008.
Values may be sent and summed in bfloat16 or wider, within the bound.
No kernel may reach another device: no remote copies, remote signals or barrier semaphores. Data moves between devices by JAX's collectives and lax.ppermute only.
A program may use at most 64 MiB of HBM per device.

v0:
```python
import jax
import jax.numpy as jnp
from jax import lax
from jax.sharding import PartitionSpec as P

SPAN = 256


PRECISE = lax.Precision.HIGHEST


def shifted(shard, axis, by):
    devices = lax.axis_size(axis)
    pairs = [(i, i + by) for i in range(devices) if 0 <= i + by < devices]
    return lax.ppermute(shard, axis, pairs)


def in_one_piece(arrays, axis, dim, along):
    columns = [a.reshape(*a.shape[:along], -1) for a in arrays]
    both = jnp.concatenate(columns, axis=along)
    out, at, done = (lax.all_gather(both, axis, axis=dim, tiled=True), 0, [])
    for a, column in zip(arrays, columns):
        piece = out[..., at : at + column.shape[along]]
        done.append(piece.reshape(*piece.shape[:along], *a.shape[along:]))
        at += column.shape[along]
    return tuple(done)


def causal_conv(leading, values, kernel):
    padded = jnp.concatenate([leading, values], axis=0).astype(jnp.float32)
    summed = jnp.zeros(values.shape, jnp.float32)
    for offset in range(kernel.shape[0]):
        summed = (
            summed + kernel[offset].astype(jnp.float32) * padded[offset : offset + values.shape[0]]
        )
    return jax.nn.silu(summed).astype(jnp.bfloat16)


def local(
    mixer_input,
    state_maps,
    gate_input,
    step_raw,
    decay_log,
    skip_gain,
    conv_input,
    conv_maps,
    norm_gain,
    out_weight,
):
    tokens, channels = mixer_input.shape
    resident_heads = decay_log.shape[0]
    head_dim = channels // resident_heads
    state_dim = state_maps.shape[1] // 2
    lead_rows = conv_input.shape[0] - 1
    blocks = tokens // SPAN
    tail_rows = jnp.concatenate(
        [mixer_input[tokens - lead_rows :], state_maps[tokens - lead_rows :]], axis=1
    )
    leading = shifted(tail_rows, "seq", 1)
    conv_out = causal_conv(leading[:, :channels], mixer_input, conv_input)
    maps_out = causal_conv(leading[:, channels:], state_maps, conv_maps)
    b_blocks = maps_out[:, :state_dim].reshape(blocks, SPAN, state_dim)
    c_blocks = maps_out[:, state_dim:].reshape(blocks, SPAN, state_dim)
    scores = jnp.einsum("ktn,ksn->kts", c_blocks, b_blocks, preferred_element_type=jnp.float32)
    step_size = jax.nn.softplus(step_raw)
    step_blocks = step_size.reshape(resident_heads, blocks, SPAN)
    log_decay = -jnp.exp(decay_log)[:, None] * step_size
    cumulative = jnp.cumsum(log_decay.reshape(resident_heads, blocks, SPAN), axis=2)
    causal = lax.broadcasted_iota(jnp.int32, (SPAN, SPAN), 0) >= lax.broadcasted_iota(
        jnp.int32, (SPAN, SPAN), 1
    )
    logarithm_spacing = jnp.where(
        causal, cumulative[:, :, :, None] - cumulative[:, :, None, :], 0.0
    )
    weights = jnp.where(
        causal, scores[None] * jnp.exp(logarithm_spacing) * step_blocks[:, :, None, :], 0.0
    ).astype(jnp.bfloat16)
    value_blocks = conv_out.reshape(blocks, SPAN, resident_heads, head_dim)
    inside = jnp.einsum(
        "hkts,kshp->kthp", weights, value_blocks, preferred_element_type=jnp.float32
    )
    tail_weight = jnp.exp(cumulative[:, :, -1:] - cumulative) * step_blocks
    weighted = value_blocks.astype(jnp.float32) * tail_weight.transpose(1, 2, 0)[:, :, :, None]
    block_states = jnp.einsum(
        "kshp,ksn->khpn", weighted, b_blocks.astype(jnp.float32), precision=PRECISE
    )

    def advance(carried_in, element):
        state_now, prefix = carried_in
        decay_now, block_add = element
        return (
            (decay_now[:, None, None] * state_now + block_add, prefix * decay_now),
            (state_now, prefix),
        )

    zero_state = jnp.zeros((resident_heads, head_dim, state_dim), jnp.float32)
    start_carry = (zero_state, jnp.ones((resident_heads,), jnp.float32))
    (local_end, device_decay), (local_before, prefixes) = lax.scan(
        advance, start_carry, (jnp.exp(cumulative[:, :, -1]).T, block_states)
    )
    table_decay, table_state = in_one_piece((device_decay[None], local_end[None]), "seq", 0, 2)
    position = lax.axis_index("seq")

    def fold_source(source, state_now):
        return jnp.where(
            source < position,
            table_decay[source][:, None, None] * state_now + table_state[source],
            state_now,
        )

    incoming = lax.fori_loop(0, lax.axis_size("seq"), fold_source, zero_state)
    carried = local_before + prefixes[:, :, None, None] * incoming[None]
    growth = jnp.exp(cumulative).transpose(1, 2, 0)[:, :, :, None]
    carried_part = (
        jnp.einsum("ktn,khpn->kthp", c_blocks.astype(jnp.float32), carried, precision=PRECISE)
        * growth
    )
    scanned = (
        inside + carried_part + skip_gain[None, None, :, None] * value_blocks.astype(jnp.float32)
    )
    gate_values = jax.nn.silu(gate_input.astype(jnp.float32)).reshape(
        tokens, resident_heads, head_dim
    )
    gated_values = scanned.reshape(tokens, resident_heads, head_dim) * gate_values
    inverse_root_mean = lax.rsqrt(
        jnp.mean(gated_values * gated_values, axis=2, keepdims=True) + 1e-05
    )
    normed = ((gated_values * inverse_root_mean).reshape(tokens, channels) * norm_gain).astype(
        jnp.bfloat16
    )
    owned_rows = lax.psum_scatter(
        lax.dot_general(
            out_weight, normed, (((0,), (1,)), ((), ())), preferred_element_type=jnp.float32
        ),
        "tensor",
        scatter_dimension=0,
        tiled=True,
    )
    return owned_rows.T.astype(jnp.bfloat16)


def solution(mesh):
    placed = (
        P(("group", "seq"), "tensor"),
        P(("group", "seq"), None),
        P(("group", "seq"), "tensor"),
        P("tensor", ("group", "seq")),
        P("tensor"),
        P("tensor"),
        P(None, "tensor"),
        P(),
        P("tensor"),
        P("tensor", None),
    )
    return jax.shard_map(
        local, mesh=mesh, in_specs=placed, out_specs=P(("group", "seq"), "tensor"), check_vma=False
    )
```

profile of v0, /device:TPU:34, one launch (start us, length us, event | category | flops | bytes accessed | tf_op | source)
XLA Modules:
  0.0 184.6 jit_solution(4198889494481503857)
XLA Ops:
  6.6 0.7 slice.83
  7.2 0.7 slice.84
  7.9 3.6 %collective-permute-start = (bf16[3,512]{1,0:T(4,128)(2,1)S(1)}, bf16[3,512]{1,0:T(4,128)(2,1)S(1)}, u32[]{:S(2)}, u32[]{:S(2)}) collective-permute-start(bf16[3,512]{1,0:T(4,128)(2,1)S(1)} %pad_maximum_fusion.1), channel_id=1, source_target_pairs={{0,1},{1,2},{2,3},{4,5},{5,6},{6,7},{8,9},{9,10},{10,11},{12,13},{... | collective-permute-start | bytes 9224 | tf_op jit(solution)/shard_map/ppermute | solution.py:15
  11.5 0.7 exponential_negate_fusion
  12.2 0.8 compare_select_fusion
  12.9 1.2 reduce-window.6
  14.2 0.1 copy.70
  14.4 0.8 slice_convert_fusion.7
  15.2 0.8 slice_convert_fusion.3
  16.4 1.0 convert_multiply_fusion
  17.4 0.8 multiply_bitcast_fusion
  18.4 0.1 copy.62
  18.6 0.1 copy.68
  18.7 11.5 %collective-permute-done = bf16[3,512]{1,0:T(4,128)(2,1)S(1)} collective-permute-done((bf16[3,512]{1,0:T(4,128)(2,1)S(1)}, bf16[3,512]{1,0:T(4,128)(2,1)S(1)}, u32[]{:S(2)}, u32[]{:S(2)}) %collective-permute-start) | collective-permute-done | bytes 3104 | tf_op jit(solution)/shard_map/ppermute | solution.py:15
  30.2 1.0 maximum_convert_fusion
  31.2 0.2 convert_multiply_fusion.1
  31.6 0.1 copy.63
  31.8 0.2 multiply_convert_fusion.1
  32.0 0.2 fusion.26
  32.2 0.3 fusion.22
  32.6 0.1 pad_maximum_fusion
  32.7 15.3 %all_gather.3 = f32[4,4,8193]{2,1,0:T(4,128)S(1)} all-gather(f32[1,4,8193]{2,1,0:T(4,128)S(1)} %pad_maximum_fusion), channel_id=1, replica_groups=mesh['group'=2,'tensor'=32,'seq'=4] {'seq'}, dimensions={0}, use_global_device_ids=true | all-gather | bytes 655440 | tf_op jit(solution)/shard_map/all_gather | solution.py:21
  48.2 0.3 slice.124
  48.5 0.4 reshape.246
  48.9 0.5 while.9
  49.4 0.3 fusion.1
  49.7 0.5 fusion.20
  50.2 0.1 copy.67
  50.4 0.1 copy.69
  50.5 6.7 %convolution_bitcast_fusion = f32[8192,256]{0,1:T(8,128)} fusion(bf16[256,8192]{1,0:T(8,128)(2,1)} %param.21, f32[256,256]{1,0:T(8,128)S(1)} %copy.69, f32[256,256]{1,0:T(8,128)S(1)} %copy.67, f32[256]{0:T(256)S(1)} %copy-done.1, bf16[256,256]{1,0:T(8,128)(2,1)S(1)} %copy-done), kind=kOutput, calls=%fused_computation.3 | convolution fusion | flops 1074331648 | bytes 13239296 | tf_op jit(solution)/shard_map/dot_general | solution.py:133
  57.3 118.8 %reduce-scatter.2.cloned.1.call-done = f32[256,256]{0,1:T(8,128)} async-done(((f32[8192,256]{0,1:T(8,128)}), f32[256,256]{0,1:T(8,128)}) %reduce-scatter.2.cloned.1.call-update) | async-done | bytes 262160 | tf_op jit(solution)/shard_map/reduce_scatter | solution.py:132
  176.1 1.6 convert_bitcast_fusion
  (40 shorter events, 1.6 us)
Async XLA Ops:
  6.5 169.5 %reduce-scatter.2.cloned.1.call-start = ((), (), s32[]{:S(2)}) async-start(), calls=%async_computation.1 | async-start | bytes 8650752 | tf_op jit(solution)/shard_map/reduce_scatter | solution.py:132
  7.9 22.3 %collective-permute-start = (bf16[3,512]{1,0:T(4,128)(2,1)S(1)}, bf16[3,512]{1,0:T(4,128)(2,1)S(1)}, u32[]{:S(2)}, u32[]{:S(2)}) collective-permute-start(bf16[3,512]{1,0:T(4,128)(2,1)S(1)} %pad_maximum_fusion.1), channel_id=1, source_target_pairs={{0,1},{1,2},{2,3},{4,5},{5,6},{6,7},{8,9},{9,10},{10,11},{12,13},{... | collective-permute-start | bytes 9224 | tf_op jit(solution)/shard_map/ppermute | solution.py:15
  31.8 17.9 %copy-start.2 = (f32[4]{0:T(128)S(1)}, f32[4]{0:T(128)}, u32[]{:S(2)}) copy-start(f32[4]{0:T(128)} %param.17) | copy-start | bytes 52
  48.2 2.4 %copy-start = (bf16[256,256]{1,0:T(8,128)(2,1)S(1)}, bf16[256,256]{1,0:T(8,128)(2,1)}, u32[]{:S(2)}) copy-start(bf16[256,256]{1,0:T(8,128)(2,1)} %param.14) | copy-start | bytes 393220
  48.2 2.4 %copy-start.1 = (f32[256]{0:T(256)S(1)}, f32[256]{0:T(256)}, u32[]{:S(2)}) copy-start(f32[256]{0:T(256)} %param.20) | copy-start | bytes 3076
Sparse Core Ops, SparseCore 0:
  57.4 118.6 reduce-scatter.1
where the time goes:
time: 185 us
  waiting for transfers between devices  130 us (70%)
  blocking collectives  15.3 us (8%)
  between operations  13.7 us (7%)
  other arithmetic  9.75 us (5%)
  matrix products  7.96 us (4%)
  local copies, waits for them, and re-layouts  3.83 us (2%)
  starting transfers between devices  3.57 us (2%)
    reduce_scatter x1, waiting for transfers between devices, local(): lax.psum_scatter(lax.dot_general(out_weight, normed, (((0,), (1,)), ((),...  119 us
    all_gather x1, blocking collectives, in_one_piece(): out, at, done = (lax.all_gather(both, axis, axis=dim, tiled=True), 0, [])  15.3 us
    ppermute x1, waiting for transfers between devices, shifted(): return lax.ppermute(shard, axis, pairs)  11.5 us
    dot_general x1, matrix products, local(): lax.dot_general(out_weight, normed, (((0,), (1,)), ((), ())), preferred_e...  6.71 us
  transfers between devices with their start and end apart: 2, of which 2 were waited for; matrix products, arithmetic and copies ran while one was open for 4% of the time, Pallas kernels for 0%

commit v1 on v0

v1 whole, which is shorter than its diff:
```python
import functools

import jax
import jax.numpy as jnp
from jax import lax
from jax.experimental import pallas as pl
from jax.experimental.pallas import tpu as pltpu
from jax.sharding import PartitionSpec as P

SPAN = 256
CORES = 2


PRECISE = lax.Precision.HIGHEST


def shifted(shard, axis, by):
    devices = lax.axis_size(axis)
    pairs = [(i, i + by) for i in range(devices) if 0 <= i + by < devices]
    return lax.ppermute(shard, axis, pairs)


def to_other_core(shard):
    devices = lax.axis_size("tensor")
    return lax.ppermute(shard, "tensor", [(i, i ^ 1) for i in range(devices)])


def to_chip(shard, by):
    devices = lax.axis_size("tensor")
    return lax.ppermute(
        shard, "tensor", [(i, (i + CORES * by) % devices) for i in range(devices)]
    )


def causal_conv(leading, values, kernel):
    padded = jnp.concatenate([leading, values], axis=0).astype(jnp.float32)
    summed = jnp.zeros(values.shape, jnp.float32)
    for offset in range(kernel.shape[0]):
        summed = (
            summed + kernel[offset].astype(jnp.float32) * padded[offset : offset + values.shape[0]]
        )
    return jax.nn.silu(summed).astype(jnp.bfloat16)


def product_kernel(blocks, own_values, other_values, own_weight, other_weight, out):
    out[0] = jnp.dot(
        own_values[...], own_weight[...], preferred_element_type=jnp.float32
    ) + jnp.dot(other_values[...], other_weight[...], preferred_element_type=jnp.float32)


def products(blocks, own_values, other_values, own_weight, other_weight, width):
    count = blocks.shape[0]
    rows, depth = own_values.shape
    whole = pl.BlockSpec((rows, depth), lambda i, at: (0, 0))
    column = pl.BlockSpec((depth, width), lambda i, at: (0, at[i]))
    return pl.pallas_call(
        product_kernel,
        grid_spec=pltpu.PrefetchScalarGridSpec(
            num_scalar_prefetch=1,
            grid=(count,),
            in_specs=[whole, whole, column, column],
            out_specs=pl.BlockSpec((1, rows, width), lambda i, at: (i, 0, 0)),
        ),
        out_shape=jax.ShapeDtypeStruct((count, rows, width), jnp.float32),
        compiler_params=pltpu.CompilerParams(vmem_limit_bytes=8 << 20),
        cost_estimate=pl.CostEstimate(
            flops=count * 4 * rows * depth * width,
            bytes_accessed=count * (4 * depth * width + 4 * rows * width),
            transcendentals=0,
        ),
    )(blocks, own_values, other_values, own_weight, other_weight)


def project(normed, out_weight, other_weight):
    devices = lax.axis_size("tensor")
    chips = devices // CORES
    me = lax.axis_index("tensor")
    width = out_weight.shape[1] // devices
    other = to_other_core(normed)
    far = chips // 2

    def block_of(by):
        return lax.rem(me + CORES * (by + chips), devices)

    order = [far, 1 - far]
    for step in range(1, far):
        order.append(far - step)
        if step + 1 < far:
            order.append(step + 1 - far)
    order.append(0)
    first = products(
        jnp.stack([block_of(by) for by in order[:2]]),
        normed, other, out_weight, other_weight, width,
    )
    rest = products(
        jnp.stack([block_of(by) for by in order[2:]]),
        normed, other, out_weight, other_weight, width,
    )
    part = {by: (first[i] if i < 2 else rest[i - 2]) for i, by in enumerate(order)}
    up = part[far].astype(jnp.bfloat16)
    down = part[1 - far].astype(jnp.bfloat16)
    for step in range(1, far):
        up = to_chip(up, 1)
        down = to_chip(down, -1)
        up = (up.astype(jnp.float32) + part[far - step]).astype(jnp.bfloat16)
        if step + 1 < far:
            down, up = lax.optimization_barrier((down, up))
            down = (down.astype(jnp.float32) + part[step + 1 - far]).astype(jnp.bfloat16)
    up = to_chip(up, 1)
    total = part[0] + down.astype(jnp.float32)
    return (total + up.astype(jnp.float32)).astype(jnp.bfloat16)


def local(
    mixer_input,
    state_maps,
    gate_input,
    step_raw,
    decay_log,
    skip_gain,
    conv_input,
    conv_maps,
    norm_gain,
    out_weight,
):
    tokens, channels = mixer_input.shape
    resident_heads = decay_log.shape[0]
    head_dim = channels // resident_heads
    state_dim = state_maps.shape[1] // 2
    lead_rows = conv_input.shape[0] - 1
    tail_rows = jnp.concatenate(
        [mixer_input[tokens - lead_rows :], state_maps[tokens - lead_rows :]], axis=1
    )
    leading = shifted(tail_rows, "seq", 1)
    other_weight = to_other_core(out_weight)
    conv_out = causal_conv(leading[:, :channels], mixer_input, conv_input)
    maps_out = causal_conv(leading[:, channels:], state_maps, conv_maps)
    b_maps = maps_out[:, :state_dim]
    c_maps = maps_out[:, state_dim:]
    scores = jnp.einsum("tn,sn->ts", c_maps, b_maps, preferred_element_type=jnp.float32)
    step_size = jax.nn.softplus(step_raw)
    log_decay = -jnp.exp(decay_log)[:, None] * step_size
    cumulative = jnp.cumsum(log_decay, axis=1)
    causal = lax.broadcasted_iota(jnp.int32, (SPAN, SPAN), 0) >= lax.broadcasted_iota(
        jnp.int32, (SPAN, SPAN), 1
    )
    logarithm_spacing = jnp.where(causal, cumulative[:, :, None] - cumulative[:, None, :], 0.0)
    weights = jnp.where(
        causal, scores[None] * jnp.exp(logarithm_spacing) * step_size[:, None, :], 0.0
    ).astype(jnp.bfloat16)
    values = conv_out.reshape(tokens, resident_heads, head_dim)
    inside = jnp.einsum("hts,shp->thp", weights, values, preferred_element_type=jnp.float32)
    tail_weight = jnp.exp(cumulative[:, -1:] - cumulative) * step_size
    weighted = values.astype(jnp.float32) * tail_weight.T[:, :, None]
    end_state = jnp.einsum("shp,sn->hpn", weighted, b_maps.astype(jnp.float32), precision=PRECISE)
    device_decay = jnp.exp(cumulative[:, -1])
    sent = jnp.concatenate(
        [end_state.reshape(channels, state_dim),
         jnp.broadcast_to(device_decay[:, None], (resident_heads, state_dim))], axis=0
    )
    behind = [shifted(sent, "seq", by) for by in range(1, lax.axis_size("seq"))]
    carried = jnp.zeros((resident_heads, head_dim, state_dim), jnp.float32)
    for message in behind[::-1]:
        state = message[:channels].reshape(resident_heads, head_dim, state_dim)
        carried = message[channels:, :1, None] * carried + state
    growth = jnp.exp(cumulative).T[:, :, None]
    carried_part = (
        jnp.einsum("tn,hpn->thp", c_maps.astype(jnp.float32), carried, precision=PRECISE) * growth
    )
    scanned = inside + carried_part + skip_gain[None, :, None] * values.astype(jnp.float32)
    gate_values = jax.nn.silu(gate_input.astype(jnp.float32)).reshape(
        tokens, resident_heads, head_dim
    )
    gated_values = scanned * gate_values
    inverse_root_mean = lax.rsqrt(
        jnp.mean(gated_values * gated_values, axis=2, keepdims=True) + 1e-05
    )
    normed = ((gated_values * inverse_root_mean).reshape(tokens, channels) * norm_gain).astype(
        jnp.bfloat16
    )
    return project(normed, out_weight, other_weight)


def solution(mesh):
    placed = (
        P(("group", "seq"), "tensor"),
        P(("group", "seq"), None),
        P(("group", "seq"), "tensor"),
        P("tensor", ("group", "seq")),
        P("tensor"),
        P("tensor"),
        P(None, "tensor"),
        P(),
        P("tensor"),
        P("tensor", None),
    )
    return jax.shard_map(
        local, mesh=mesh, in_specs=placed, out_specs=P(("group", "seq"), "tensor"), check_vma=False
    )
```

time: 185 us -> 141 us (0.76)
  waiting for transfers between devices: 130 us -> 89.5 us
  starting transfers between devices: 3.57 us -> 21.7 us
  blocking collectives: 15.3 us -> 0 us
  between operations: 13.7 us -> 0.36 us
  Pallas kernels: 0 us -> 11.1 us
  matrix products: 7.96 us -> 1.31 us
  local copies, waits for them, and re-layouts: 3.83 us -> 7.01 us
    reduce_scatter x1 -> x0, waiting for transfers between devices: 119 us -> none  [local(): lax.psum_scatter(lax.dot_general(out_weight, normed, (((0,), (1,)), ((),...]
    ppermute x0 -> x17, waiting for transfers between devices: none -> 67.3 us  [the longest x15 66.1 us: to_chip(): lax.ppermute(shard, 'tensor', [(i, (i + CORES * by) % devices) for i in r...]
    all_gather x1 -> x0, blocking collectives: 15.3 us -> none  [in_one_piece(): out, at, done = (lax.all_gather(both, axis, axis=dim, tiled=True), 0, [])]
    ppermute x0 -> x17, starting transfers between devices: none -> 14.2 us  [the longest x15 13.9 us: to_chip(): lax.ppermute(shard, 'tensor', [(i, (i + CORES * by) % devices) for i in r...]
    pallas_call x0 -> x2, Pallas kernels: none -> 11.1 us  [products(): pl.pallas_call(product_kernel, grid_spec=pltpu.PrefetchScalarGridSpec(num...]
    ppermute x1 -> x4, waiting for transfers between devices: 11.5 us -> 22.2 us  [shifted(): return lax.ppermute(shard, axis, pairs)]
    dot_general x5 -> x4, matrix products: 7.96 us -> 1.31 us  [the longest x1 0.49 us: local(): jnp.einsum('hts,shp->thp', weights, values, preferred_element_type=jnp.fl...]
    unnamed x7 -> x9, local copies, waits for them, and re-layouts: 0.09 us -> 4.39 us
  transfers between devices with their start and end apart: 2 -> 21, of which waited for: 2 -> 16; matrix products, arithmetic and copies ran while one was open for 4% -> 7% of each run, Pallas kernels for 0% -> 6%
where the time goes in v1:
time: 141 us; the launch traced here: 140 us
  waiting for transfers between devices  89.5 us (63%)
  starting transfers between devices  21.7 us (15%)
  Pallas kernels  11.1 us (8%)
  other arithmetic  9.03 us (6%)
  local copies, waits for them, and re-layouts  7.01 us (5%)
    ppermute x15, waiting for transfers between devices, to_chip(): lax.ppermute(shard, 'tensor', [(i, (i + CORES * by) % devices) for i in r...  66.1 us
    ppermute x4, waiting for transfers between devices, shifted(): return lax.ppermute(shard, axis, pairs)  22.2 us
    ppermute x15, starting transfers between devices, to_chip(): lax.ppermute(shard, 'tensor', [(i, (i + CORES * by) % devices) for i in r...  13.9 us
    pallas_call x2, Pallas kernels, products(): pl.pallas_call(product_kernel, grid_spec=pltpu.PrefetchScalarGridSpec(num...  11.1 us
    ppermute x4, starting transfers between devices, shifted(): return lax.ppermute(shard, axis, pairs)  7.5 us
    unnamed x9, local copies, waits for them, and re-layouts  4.39 us
  transfers between devices with their start and end apart: 21, of which 16 were waited for; matrix products, arithmetic and copies ran while one was open for 7% of the time, Pallas kernels for 6%

profile of v1, /device:TPU:34, one launch (start us, length us, event | category | flops | bytes accessed | tf_op | source)
XLA Modules:
  0.0 140.0 jit_solution(12682548855516987453)
XLA Ops:
  1.4 3.6 %collective-permute-start = (bf16[3,512]{1,0:T(4,128)(2,1)S(1)}, bf16[3,512]{1,0:T(4,128)(2,1)S(1)}, u32[]{:S(2)}, u32[]{:S(2)}) collective-permute-start(bf16[3,512]{1,0:T(4,128)(2,1)S(1)} %pad_maximum_fusion.1), channel_id=1, source_target_pairs={{0,1},{1,2},{2,3},{4,5},{5,6},{6,7},{8,9},{9,10},{10,11},{12,13},{... | collective-permute-start | bytes 9224 | tf_op jit(solution)/shard_map/ppermute | solution.py:20
  5.1 0.8 slice_convert_fusion.7
  6.6 0.8 broadcast_multiply_fusion.1
  7.4 1.2 reduce-window.6
  9.2 0.8 slice_convert_fusion.3
  10.0 0.8 multiply_bitcast_fusion
  10.8 1.0 convert_multiply_fusion
  12.0 11.7 %collective-permute-done = bf16[3,512]{1,0:T(4,128)(2,1)S(1)} collective-permute-done((bf16[3,512]{1,0:T(4,128)(2,1)S(1)}, bf16[3,512]{1,0:T(4,128)(2,1)S(1)}, u32[]{:S(2)}, u32[]{:S(2)}) %collective-permute-start) | collective-permute-done | bytes 3104 | tf_op jit(solution)/shard_map/ppermute | solution.py:20
  23.7 1.0 maximum_convert_fusion
  26.3 1.3 collective-permute-start.2
  27.6 2.0 %collective-permute-start.1 = (f32[260,128]{1,0:T(8,128)S(1)}, f32[260,128]{1,0:T(8,128)S(1)}, u32[]{:S(2)}, u32[]{:S(2)}) collective-permute-start(f32[260,128]{1,0:T(8,128)S(1)} %pad_maximum_fusion), channel_id=1, source_target_pairs={{0,1},{1,2},{2,3},{4,5},{5,6},{6,7},{8,9},{9,10},{10,11},{12,13},{... | collective-permute-start | bytes 399368 | tf_op jit(solution)/shard_map/ppermute | solution.py:20
  30.3 10.5 %collective-permute-done.1 = f32[260,128]{1,0:T(8,128)S(1)} collective-permute-done((f32[260,128]{1,0:T(8,128)S(1)}, f32[260,128]{1,0:T(8,128)S(1)}, u32[]{:S(2)}, u32[]{:S(2)}) %collective-permute-start.1) | collective-permute-done | bytes 133152 | tf_op jit(solution)/shard_map/ppermute | solution.py:20
  42.0 1.2 collective-permute-done.4.other_values
  43.2 2.2 %copy-done = bf16[256,8192]{1,0:T(8,128)(2,1)S(1)} copy-done((bf16[256,8192]{1,0:T(8,128)(2,1)S(1)}, bf16[256,8192]{1,0:T(8,128)(2,1)}, u32[]{:S(2)}) %copy-start) | copy-done | bytes 4194328
  45.4 2.0 %shard_map.101 = f32[2,256,256]{2,1,0:T(8,128)S(1)} custom-call(s32[2]{0:T(128)S(1)} %pad_add_fusion.blocks, bf16[256,256]{1,0:T(8,128)(2,1)S(1)} %multiply_convert_fusion.own_values, bf16[256,256]{1,0:T(8,128)(2,1)S(1)} %collective-permute-done.4.other_values, bf16[256,8192]{1,0:T(8,128)(2,1)S(1)} %copy-done, ...), custom_call_target="tpu_custom_call" | custom-call | flops 134217728 | bytes 1048576 | tf_op jit(solution)/shard_map/pallas_call | solution.py:56
  47.7 8.5 %collective-permute-start.6 = (bf16[256,256]{1,0:T(8,128)(2,1)S(1)}, bf16[256,256]{1,0:T(8,128)(2,1)S(1)}, u32[]{:S(2)}, u32[]{:S(2)}) collective-permute-start(bf16[256,256]{1,0:T(8,128)(2,1)S(1)} %get-tuple-element.44), channel_id=1, source_target_pairs={{0,120},{4,124},{8,0},{12,4},{16,8},{20,12},{24,16},{28,20},{32,24... | collective-permute-start | bytes 393224 | tf_op jit(solution)/shard_map/ppermute | solution.py:30
  56.2 2.2 %copy-done.1 = bf16[256,8192]{1,0:T(8,128)(2,1)S(1)} copy-done((bf16[256,8192]{1,0:T(8,128)(2,1)S(1)}, bf16[256,8192]{1,0:T(8,128)(2,1)}, u32[]{:S(2)}) %copy-start.1) | copy-done | bytes 4194328
  58.4 9.1 %shard_map.100 = f32[14,256,256]{2,1,0:T(8,128)S(1)} custom-call(s32[14]{0:T(128)S(1)} %stack.68.blocks, bf16[256,256]{1,0:T(8,128)(2,1)S(1)} %multiply_convert_fusion.own_values, bf16[256,256]{1,0:T(8,128)(2,1)S(1)} %collective-permute-done.4.other_values, bf16[256,8192]{1,0:T(8,128)(2,1)S(1)} %copy-done.1, ...), custom_call_target="tpu_custom_call" | custom-call | flops 939524096 | bytes 7340032 | tf_op jit(solution)/shard_map/pallas_call | solution.py:56
  67.7 6.5 %collective-permute-done.9 = bf16[256,256]{1,0:T(8,128)(2,1)S(1)} collective-permute-done((bf16[256,256]{1,0:T(8,128)(2,1)S(1)}, bf16[256,256]{1,0:T(8,128)(2,1)S(1)}, u32[]{:S(2)}, u32[]{:S(2)}) %collective-permute-start.9) | collective-permute-done | bytes 131104 | tf_op jit(solution)/shard_map/ppermute | solution.py:30
  74.9 4.5 %collective-permute-done.8 = bf16[256,256]{1,0:T(8,128)(2,1)S(1)} collective-permute-done((bf16[256,256]{1,0:T(8,128)(2,1)S(1)}, bf16[256,256]{1,0:T(8,128)(2,1)S(1)}, u32[]{:S(2)}, u32[]{:S(2)}) %collective-permute-start.8) | collective-permute-done | bytes 131104 | tf_op jit(solution)/shard_map/ppermute | solution.py:30
  79.3 6.2 %collective-permute-done.11 = bf16[256,256]{1,0:T(8,128)(2,1)S(1)} collective-permute-done((bf16[256,256]{1,0:T(8,128)(2,1)S(1)}, bf16[256,256]{1,0:T(8,128)(2,1)S(1)}, u32[]{:S(2)}, u32[]{:S(2)}) %collective-permute-start.11) | collective-permute-done | bytes 131104 | tf_op jit(solution)/shard_map/ppermute | solution.py:30
  86.2 4.5 %collective-permute-done.10 = bf16[256,256]{1,0:T(8,128)(2,1)S(1)} collective-permute-done((bf16[256,256]{1,0:T(8,128)(2,1)S(1)}, bf16[256,256]{1,0:T(8,128)(2,1)S(1)}, u32[]{:S(2)}, u32[]{:S(2)}) %collective-permute-start.10) | collective-permute-done | bytes 131104 | tf_op jit(solution)/shard_map/ppermute | solution.py:30
  90.7 6.2 %collective-permute-done.13 = bf16[256,256]{1,0:T(8,128)(2,1)S(1)} collective-permute-done((bf16[256,256]{1,0:T(8,128)(2,1)S(1)}, bf16[256,256]{1,0:T(8,128)(2,1)S(1)}, u32[]{:S(2)}, u32[]{:S(2)}) %collective-permute-start.13) | collective-permute-done | bytes 131104 | tf_op jit(solution)/shard_map/ppermute | solution.py:30
  97.5 4.5 %collective-permute-done.12 = bf16[256,256]{1,0:T(8,128)(2,1)S(1)} collective-permute-done((bf16[256,256]{1,0:T(8,128)(2,1)S(1)}, bf16[256,256]{1,0:T(8,128)(2,1)S(1)}, u32[]{:S(2)}, u32[]{:S(2)}) %collective-permute-start.12) | collective-permute-done | bytes 131104 | tf_op jit(solution)/shard_map/ppermute | solution.py:30
  102.0 6.2 %collective-permute-done.15 = bf16[256,256]{1,0:T(8,128)(2,1)S(1)} collective-permute-done((bf16[256,256]{1,0:T(8,128)(2,1)S(1)}, bf16[256,256]{1,0:T(8,128)(2,1)S(1)}, u32[]{:S(2)}, u32[]{:S(2)}) %collective-permute-start.15) | collective-permute-done | bytes 131104 | tf_op jit(solution)/shard_map/ppermute | solution.py:30
  108.8 5.4 %collective-permute-done.14 = bf16[256,256]{1,0:T(8,128)(2,1)S(1)} collective-permute-done((bf16[256,256]{1,0:T(8,128)(2,1)S(1)}, bf16[256,256]{1,0:T(8,128)(2,1)S(1)}, u32[]{:S(2)}, u32[]{:S(2)}) %collective-permute-start.14) | collective-permute-done | bytes 131104 | tf_op jit(solution)/shard_map/ppermute | solution.py:30
  114.2 6.9 %collective-permute-done.17 = bf16[256,256]{1,0:T(8,128)(2,1)S(1)} collective-permute-done((bf16[256,256]{1,0:T(8,128)(2,1)S(1)}, bf16[256,256]{1,0:T(8,128)(2,1)S(1)}, u32[]{:S(2)}, u32[]{:S(2)}) %collective-permute-start.17) | collective-permute-done | bytes 131104 | tf_op jit(solution)/shard_map/ppermute | solution.py:30
  121.8 4.5 %collective-permute-done.16 = bf16[256,256]{1,0:T(8,128)(2,1)S(1)} collective-permute-done((bf16[256,256]{1,0:T(8,128)(2,1)S(1)}, bf16[256,256]{1,0:T(8,128)(2,1)S(1)}, u32[]{:S(2)}, u32[]{:S(2)}) %collective-permute-start.16) | collective-permute-done | bytes 131104 | tf_op jit(solution)/shard_map/ppermute | solution.py:30
  126.3 6.2 %collective-permute-done.19 = bf16[256,256]{1,0:T(8,128)(2,1)S(1)} collective-permute-done((bf16[256,256]{1,0:T(8,128)(2,1)S(1)}, bf16[256,256]{1,0:T(8,128)(2,1)S(1)}, u32[]{:S(2)}, u32[]{:S(2)}) %collective-permute-start.19) | collective-permute-done | bytes 131104 | tf_op jit(solution)/shard_map/ppermute | solution.py:30
  133.1 1.5 %collective-permute-start.20 = (bf16[256,256]{1,0:T(8,128)(2,1)S(1)}, bf16[256,256]{1,0:T(8,128)(2,1)S(1)}, u32[]{:S(2)}, u32[]{:S(2)}) collective-permute-start(bf16[256,256]{1,0:T(8,128)(2,1)S(1)} %get-tuple-element.32), channel_id=1, source_target_pairs={{0,8},{4,12},{8,16},{12,20},{16,24},{20,28},{24,32},{28,36},{32,40... | collective-permute-start | bytes 393224 | tf_op jit(solution)/shard_map/ppermute | solution.py:30
  134.7 2.9 %collective-permute-done.18 = bf16[256,256]{1,0:T(8,128)(2,1)S(1)} collective-permute-done((bf16[256,256]{1,0:T(8,128)(2,1)S(1)}, bf16[256,256]{1,0:T(8,128)(2,1)S(1)}, u32[]{:S(2)}, u32[]{:S(2)}) %collective-permute-start.18) | collective-permute-done | bytes 131104 | tf_op jit(solution)/shard_map/ppermute | solution.py:30
  137.6 1.7 %collective-permute-done.20 = bf16[256,256]{1,0:T(8,128)(2,1)S(1)} collective-permute-done((bf16[256,256]{1,0:T(8,128)(2,1)S(1)}, bf16[256,256]{1,0:T(8,128)(2,1)S(1)}, u32[]{:S(2)}, u32[]{:S(2)}) %collective-permute-start.20) | collective-permute-done | bytes 131104 | tf_op jit(solution)/shard_map/ppermute | solution.py:30
  (75 shorter events, 11.4 us)
Async XLA Ops:
  1.4 22.3 %collective-permute-start = (bf16[3,512]{1,0:T(4,128)(2,1)S(1)}, bf16[3,512]{1,0:T(4,128)(2,1)S(1)}, u32[]{:S(2)}, u32[]{:S(2)}) collective-permute-start(bf16[3,512]{1,0:T(4,128)(2,1)S(1)} %pad_maximum_fusion.1), channel_id=1, source_target_pairs={{0,1},{1,2},{2,3},{4,5},{5,6},{6,7},{8,9},{9,10},{10,11},{12,13},{... | collective-permute-start | bytes 9224 | tf_op jit(solution)/shard_map/ppermute | solution.py:20
  5.0 38.3 %collective-permute-start.5 = (bf16[256,8192]{1,0:T(8,128)(2,1)}, bf16[256,8192]{1,0:T(8,128)(2,1)}, u32[]{:S(2)}, u32[]{:S(2)}) collective-permute-start(bf16[256,8192]{1,0:T(8,128)(2,1)} %own_weight.3), channel_id=1, source_target_pairs={{0,4},{4,0},{8,12},{12,8},{16,20},{20,16},{24,28},{28,24},{32,36},... | collective-permute-start | bytes 12582920 | tf_op jit(solution)/shard_map/ppermute | solution.py:25
  24.7 16.5 %copy-start.3 = (f32[4]{0:T(128)S(1)}, f32[4]{0:T(128)}, u32[]{:S(2)}) copy-start(f32[4]{0:T(128)} %param.15) | copy-start | bytes 52
  25.0 16.7 %copy-start.2 = (f32[256]{0:T(256)S(1)}, f32[256]{0:T(256)}, u32[]{:S(2)}) copy-start(f32[256]{0:T(256)} %param.18) | copy-start | bytes 3076
  25.6 4.6 %collective-permute-start.3 = (f32[260,128]{1,0:T(8,128)S(1)}, f32[260,128]{1,0:T(8,128)S(1)}, u32[]{:S(2)}, u32[]{:S(2)}) collective-permute-start(f32[260,128]{1,0:T(8,128)S(1)} %pad_maximum_fusion), channel_id=1, source_target_pairs={{0,3},{4,7},{8,11},{12,15},{16,19},{20,23},{24,27},{28,31},{32,35}... | collective-permute-start | bytes 399368 | tf_op jit(solution)/shard_map/ppermute | solution.py:20
  26.3 4.0 %collective-permute-start.2 = (f32[260,128]{1,0:T(8,128)S(1)}, f32[260,128]{1,0:T(8,128)S(1)}, u32[]{:S(2)}, u32[]{:S(2)}) collective-permute-start(f32[260,128]{1,0:T(8,128)S(1)} %pad_maximum_fusion), channel_id=1, source_target_pairs={{0,2},{1,3},{4,6},{5,7},{8,10},{9,11},{12,14},{13,15},{16,18},{17,... | collective-permute-start | bytes 399368 | tf_op jit(solution)/shard_map/ppermute | solution.py:20
  27.6 13.2 %collective-permute-start.1 = (f32[260,128]{1,0:T(8,128)S(1)}, f32[260,128]{1,0:T(8,128)S(1)}, u32[]{:S(2)}, u32[]{:S(2)}) collective-permute-start(f32[260,128]{1,0:T(8,128)S(1)} %pad_maximum_fusion), channel_id=1, source_target_pairs={{0,1},{1,2},{2,3},{4,5},{5,6},{6,7},{8,9},{9,10},{10,11},{12,13},{... | collective-permute-start | bytes 399368 | tf_op jit(solution)/shard_map/ppermute | solution.py:20
  41.7 1.5 %collective-permute-start.4 = (bf16[256,256]{1,0:T(8,128)(2,1)S(1)}, bf16[256,256]{1,0:T(8,128)(2,1)S(1)}, u32[]{:S(2)}, u32[]{:S(2)}) collective-permute-start(bf16[256,256]{1,0:T(8,128)(2,1)S(1)} %multiply_convert_fusion.own_values), channel_id=1, source_target_pairs={{0,4},{4,0},{8,12},{12,8},{16,20},{20,16},{24,28},{28,24},{32,36},... | collective-permute-start | bytes 393224 | tf_op jit(solution)/shard_map/ppermute | solution.py:25
  43.2 2.2 %copy-start = (bf16[256,8192]{1,0:T(8,128)(2,1)S(1)}, bf16[256,8192]{1,0:T(8,128)(2,1)}, u32[]{:S(2)}) copy-start(bf16[256,8192]{1,0:T(8,128)(2,1)} %own_weight.3) | copy-start | bytes 12582916
  47.5 20.1 %collective-permute-start.7 = (bf16[256,256]{1,0:T(8,128)(2,1)S(1)}, bf16[256,256]{1,0:T(8,128)(2,1)S(1)}, u32[]{:S(2)}, u32[]{:S(2)}) collective-permute-start(bf16[256,256]{1,0:T(8,128)(2,1)S(1)} %get-tuple-element.43), channel_id=1, source_target_pairs={{0,8},{4,12},{8,16},{12,20},{16,24},{20,28},{24,32},{28,36},{32,40... | collective-permute-start | bytes 393224 | tf_op jit(solution)/shard_map/ppermute | solution.py:30
  47.7 19.8 %collective-permute-start.6 = (bf16[256,256]{1,0:T(8,128)(2,1)S(1)}, bf16[256,256]{1,0:T(8,128)(2,1)S(1)}, u32[]{:S(2)}, u32[]{:S(2)}) collective-permute-start(bf16[256,256]{1,0:T(8,128)(2,1)S(1)} %get-tuple-element.44), channel_id=1, source_target_pairs={{0,120},{4,124},{8,0},{12,4},{16,8},{20,12},{24,16},{28,20},{32,24... | collective-permute-start | bytes 393224 | tf_op jit(solution)/shard_map/ppermute | solution.py:30
  56.2 2.2 %copy-start.1 = (bf16[256,8192]{1,0:T(8,128)(2,1)S(1)}, bf16[256,8192]{1,0:T(8,128)(2,1)}, u32[]{:S(2)}) copy-start(bf16[256,8192]{1,0:T(8,128)(2,1)} %own_weight.3) | copy-start | bytes 12582916
  67.6 6.6 %collective-permute-start.9 = (bf16[256,256]{1,0:T(8,128)(2,1)S(1)}, bf16[256,256]{1,0:T(8,128)(2,1)S(1)}, u32[]{:S(2)}, u32[]{:S(2)}) collective-permute-start(bf16[256,256]{1,0:T(8,128)(2,1)S(1)} %fusion.37), channel_id=1, source_target_pairs={{0,8},{4,12},{8,16},{12,20},{16,24},{20,28},{24,32},{28,36},{32,40... | collective-permute-start | bytes 393224 | tf_op jit(solution)/shard_map/ppermute | solution.py:30
  74.3 5.1 %collective-permute-start.8 = (bf16[256,256]{1,0:T(8,128)(2,1)S(1)}, bf16[256,256]{1,0:T(8,128)(2,1)S(1)}, u32[]{:S(2)}, u32[]{:S(2)}) collective-permute-start(bf16[256,256]{1,0:T(8,128)(2,1)S(1)} %get-tuple-element.42), channel_id=1, source_target_pairs={{0,120},{4,124},{8,0},{12,4},{16,8},{20,12},{24,16},{28,20},{32,24... | collective-permute-start | bytes 393224 | tf_op jit(solution)/shard_map/ppermute | solution.py:30
  79.3 6.2 %collective-permute-start.11 = (bf16[256,256]{1,0:T(8,128)(2,1)S(1)}, bf16[256,256]{1,0:T(8,128)(2,1)S(1)}, u32[]{:S(2)}, u32[]{:S(2)}) collective-permute-start(bf16[256,256]{1,0:T(8,128)(2,1)S(1)} %get-tuple-element.20), channel_id=1, source_target_pairs={{0,8},{4,12},{8,16},{12,20},{16,24},{20,28},{24,32},{28,36},{32,40... | collective-permute-start | bytes 393224 | tf_op jit(solution)/shard_map/ppermute | solution.py:30
  85.6 5.1 %collective-permute-start.10 = (bf16[256,256]{1,0:T(8,128)(2,1)S(1)}, bf16[256,256]{1,0:T(8,128)(2,1)S(1)}, u32[]{:S(2)}, u32[]{:S(2)}) collective-permute-start(bf16[256,256]{1,0:T(8,128)(2,1)S(1)} %get-tuple-element.40), channel_id=1, source_target_pairs={{0,120},{4,124},{8,0},{12,4},{16,8},{20,12},{24,16},{28,20},{32,24... | collective-permute-start | bytes 393224 | tf_op jit(solution)/shard_map/ppermute | solution.py:30
  90.7 6.2 %collective-permute-start.13 = (bf16[256,256]{1,0:T(8,128)(2,1)S(1)}, bf16[256,256]{1,0:T(8,128)(2,1)S(1)}, u32[]{:S(2)}, u32[]{:S(2)}) collective-permute-start(bf16[256,256]{1,0:T(8,128)(2,1)S(1)} %get-tuple-element.22), channel_id=1, source_target_pairs={{0,8},{4,12},{8,16},{12,20},{16,24},{20,28},{24,32},{28,36},{32,40... | collective-permute-start | bytes 393224 | tf_op jit(solution)/shard_map/ppermute | solution.py:30
  96.9 5.1 %collective-permute-start.12 = (bf16[256,256]{1,0:T(8,128)(2,1)S(1)}, bf16[256,256]{1,0:T(8,128)(2,1)S(1)}, u32[]{:S(2)}, u32[]{:S(2)}) collective-permute-start(bf16[256,256]{1,0:T(8,128)(2,1)S(1)} %get-tuple-element.38), channel_id=1, source_target_pairs={{0,120},{4,124},{8,0},{12,4},{16,8},{20,12},{24,16},{28,20},{32,24... | collective-permute-start | bytes 393224 | tf_op jit(solution)/shard_map/ppermute | solution.py:30
  102.0 6.2 %collective-permute-start.15 = (bf16[256,256]{1,0:T(8,128)(2,1)S(1)}, bf16[256,256]{1,0:T(8,128)(2,1)S(1)}, u32[]{:S(2)}, u32[]{:S(2)}) collective-permute-start(bf16[256,256]{1,0:T(8,128)(2,1)S(1)} %get-tuple-element.24), channel_id=1, source_target_pairs={{0,8},{4,12},{8,16},{12,20},{16,24},{20,28},{24,32},{28,36},{32,40... | collective-permute-start | bytes 393224 | tf_op jit(solution)/shard_map/ppermute | solution.py:30
  108.2 6.0 %collective-permute-start.14 = (bf16[256,256]{1,0:T(8,128)(2,1)S(1)}, bf16[256,256]{1,0:T(8,128)(2,1)S(1)}, u32[]{:S(2)}, u32[]{:S(2)}) collective-permute-start(bf16[256,256]{1,0:T(8,128)(2,1)S(1)} %get-tuple-element.36), channel_id=1, source_target_pairs={{0,120},{4,124},{8,0},{12,4},{16,8},{20,12},{24,16},{28,20},{32,24... | collective-permute-start | bytes 393224 | tf_op jit(solution)/shard_map/ppermute | solution.py:30
  114.2 6.9 %collective-permute-start.17 = (bf16[256,256]{1,0:T(8,128)(2,1)S(1)}, bf16[256,256]{1,0:T(8,128)(2,1)S(1)}, u32[]{:S(2)}, u32[]{:S(2)}) collective-permute-start(bf16[256,256]{1,0:T(8,128)(2,1)S(1)} %get-tuple-element.26), channel_id=1, source_target_pairs={{0,8},{4,12},{8,16},{12,20},{16,24},{20,28},{24,32},{28,36},{32,40... | collective-permute-start | bytes 393224 | tf_op jit(solution)/shard_map/ppermute | solution.py:30
  121.2 5.1 %collective-permute-start.16 = (bf16[256,256]{1,0:T(8,128)(2,1)S(1)}, bf16[256,256]{1,0:T(8,128)(2,1)S(1)}, u32[]{:S(2)}, u32[]{:S(2)}) collective-permute-start(bf16[256,256]{1,0:T(8,128)(2,1)S(1)} %get-tuple-element.34), channel_id=1, source_target_pairs={{0,120},{4,124},{8,0},{12,4},{16,8},{20,12},{24,16},{28,20},{32,24... | collective-permute-start | bytes 393224 | tf_op jit(solution)/shard_map/ppermute | solution.py:30
  126.3 6.2 %collective-permute-start.19 = (bf16[256,256]{1,0:T(8,128)(2,1)S(1)}, bf16[256,256]{1,0:T(8,128)(2,1)S(1)}, u32[]{:S(2)}, u32[]{:S(2)}) collective-permute-start(bf16[256,256]{1,0:T(8,128)(2,1)S(1)} %get-tuple-element.28), channel_id=1, source_target_pairs={{0,8},{4,12},{8,16},{12,20},{16,24},{20,28},{24,32},{28,36},{32,40... | collective-permute-start | bytes 393224 | tf_op jit(solution)/shard_map/ppermute | solution.py:30
  132.5 5.1 %collective-permute-start.18 = (bf16[256,256]{1,0:T(8,128)(2,1)S(1)}, bf16[256,256]{1,0:T(8,128)(2,1)S(1)}, u32[]{:S(2)}, u32[]{:S(2)}) collective-permute-start(bf16[256,256]{1,0:T(8,128)(2,1)S(1)} %get-tuple-element.31), channel_id=1, source_target_pairs={{0,120},{4,124},{8,0},{12,4},{16,8},{20,12},{24,16},{28,20},{32,24... | collective-permute-start | bytes 393224 | tf_op jit(solution)/shard_map/ppermute | solution.py:30
  133.1 6.2 %collective-permute-start.20 = (bf16[256,256]{1,0:T(8,128)(2,1)S(1)}, bf16[256,256]{1,0:T(8,128)(2,1)S(1)}, u32[]{:S(2)}, u32[]{:S(2)}) collective-permute-start(bf16[256,256]{1,0:T(8,128)(2,1)S(1)} %get-tuple-element.32), channel_id=1, source_target_pairs={{0,8},{4,12},{8,16},{12,20},{16,24},{20,28},{24,32},{28,36},{32,40... | collective-permute-start | bytes 393224 | tf_op jit(solution)/shard_map/ppermute | solution.py:30

commit v2 on v1

v2 whole, which is shorter than its diff:
```python
import functools

import jax
import jax.numpy as jnp
from jax import lax
from jax.experimental import pallas as pl
from jax.experimental.pallas import tpu as pltpu
from jax.sharding import PartitionSpec as P


CORES = 2
STREAMS = 2
LEAD = 16
F32 = jnp.float32
BF16 = jnp.bfloat16
PRECISE = lax.Precision.HIGHEST
VMEM = pl.BlockSpec(memory_space=pltpu.VMEM)
SMEM = pl.BlockSpec(memory_space=pltpu.SMEM)
HBM = pl.BlockSpec(memory_space=pltpu.HBM)


def shifted(shard, axis, by):
    devices = lax.axis_size(axis)
    pairs = [(i, i + by) for i in range(devices) if 0 <= i + by < devices]
    return lax.ppermute(shard, axis, pairs)


def to_other_core(shard):
    devices = lax.axis_size("tensor")
    return lax.ppermute(shard, "tensor", [(i, i ^ 1) for i in range(devices)])


def to_chip(shard, by):
    devices = lax.axis_size("tensor")
    return lax.ppermute(
        shard, "tensor", [(i, (i + CORES * by) % devices) for i in range(devices)]
    )


def call(body, specs, shapes, flops, scratch=()):
    return pl.pallas_call(
        body,
        in_specs=specs,
        out_specs=tuple(VMEM for _ in shapes),
        out_shape=tuple(jax.ShapeDtypeStruct(s, d) for s, d in shapes),
        scratch_shapes=list(scratch),
        compiler_params=pltpu.CompilerParams(vmem_limit_bytes=16 << 20),
        cost_estimate=pl.CostEstimate(flops=flops, bytes_accessed=1 << 20, transcendentals=0),
    )


def along(a, b, ca, cb, precision=None):
    return lax.dot_general(
        a, b, (((ca,), (cb,)), ((), ())), preferred_element_type=F32, precision=precision
    )


def halves(x):
    high = x.astype(BF16)
    return high, (x - high.astype(F32)).astype(BF16)


def silu(v):
    return v / (1.0 + jnp.exp(-v))


def per_head(columns, rows, width, head_dim):
    lane = lax.broadcasted_iota(jnp.int32, (rows, width), 1) // head_dim
    spread = jnp.broadcast_to(columns[:, 0:1], (rows, width))
    for head in range(1, width // head_dim):
        spread = jnp.where(lane == head, columns[:, head : head + 1], spread)
    return spread


def tail_body(mixer, maps, out, sems):
    tokens, width = mixer.shape
    rows = pl.ds(tokens - LEAD, LEAD)
    copies = [
        pltpu.make_async_copy(mixer.at[rows], out.at[:, pl.ds(0, width)], sems.at[0]),
        pltpu.make_async_copy(maps.at[rows], out.at[:, pl.ds(width, maps.shape[1])], sems.at[1]),
    ]
    for copy in copies:
        copy.start()
    for copy in copies:
        copy.wait()


def tail_of(mixer_input, state_maps):
    width = mixer_input.shape[1] + state_maps.shape[1]
    return call(
        tail_body, [HBM, HBM], [((LEAD, width), BF16)], 1000, [pltpu.SemaphoreType.DMA((2,))]
    )(mixer_input, state_maps)[0]


def decay_body(
    heads, head_dim, step_hbm, decay_hbm, skip_hbm, gate_hbm, mixer_hbm, maps_hbm, taps_hbm,
    map_taps_hbm, mix, tail, growth, ends, gated, skip, summed,
    raw, logs, gains, gate, mixer, maps, taps, map_taps, padded, sems
):
    pairs = [(decay_hbm, logs), (step_hbm, raw), (skip_hbm, gains), (gate_hbm, gate),
             (taps_hbm, taps), (map_taps_hbm, map_taps), (mixer_hbm, mixer), (maps_hbm, maps)]
    copies = [pltpu.make_async_copy(a, b, sems.at[i]) for i, (a, b) in enumerate(pairs)]
    for copy in copies:
        copy.start()
    tokens = raw.shape[1]
    width = heads * head_dim
    row = lax.broadcasted_iota(jnp.int32, (heads, tokens), 0)
    to = lax.broadcasted_iota(jnp.int32, (tokens, tokens), 0)
    since = lax.broadcasted_iota(jnp.int32, (tokens, tokens), 1)
    causal = to >= since
    ones = jnp.where(causal, 1.0, 0.0).astype(F32)
    same = jnp.where(to == since, 1.0, 0.0).astype(F32)
    for copy in copies[:3]:
        copy.wait()
    step = jnp.maximum(raw[...], 0.0) + jnp.log1p(jnp.exp(-jnp.abs(raw[...])))
    rates = jnp.broadcast_to(logs[:, 0:1], (heads, tokens))
    for head in range(1, heads):
        rates = jnp.where(row == head, logs[:, head : head + 1], rates)
    change = -jnp.exp(rates) * step
    across = along(change, ones, 1, 1, PRECISE)
    down = along(ones, change, 1, 1, PRECISE)
    step_down = along(same, step, 1, 1, PRECISE)
    for head in range(heads):
        spacing = jnp.where(causal, down[:, head : head + 1] - across[head : head + 1, :], -1e30)
        mix[head] = jnp.exp(spacing) * step[head : head + 1, :]
    last = down[tokens - 1 : tokens, :]
    tail[...] = per_head(jnp.exp(last - down) * step_down, tokens, width, head_dim)
    growth[...] = per_head(jnp.exp(down), tokens, width, head_dim)
    ends[...] = jnp.broadcast_to(jnp.exp(across[:, tokens - 1 : tokens]), ends.shape)
    skip[...] = per_head(gains[...], 1, width, head_dim)
    for copy in copies[3:]:
        copy.wait()
    gated[...] = silu(gate[...].astype(F32))
    for source, kernel, first in ((mixer, taps, 0), (maps, map_taps, width)):
        count = kernel.shape[0]
        columns = source.shape[1]
        padded[0:8, :columns] = jnp.zeros((8, columns), F32)
        padded[8 : 8 + tokens, :columns] = source[...].astype(F32)
        total = None
        for tap in range(count):
            at = 9 - count + tap
            term = kernel[tap : tap + 1, :].astype(F32) * padded[at : at + tokens, :columns]
            total = term if total is None else total + term
        summed[:, first : first + columns] = total


def decay(step_raw, decay_log, skip_gain, gate_input, mixer_input, state_maps, conv_input,
          conv_maps):
    heads, tokens = step_raw.shape
    channels = mixer_input.shape[1]
    square = (tokens, channels)
    width = channels + state_maps.shape[1]
    operands = (step_raw, decay_log.reshape(1, heads), skip_gain.reshape(1, heads), gate_input,
                mixer_input, state_maps, conv_input, conv_maps)
    return call(
        functools.partial(decay_body, heads, channels // heads),
        [HBM] * len(operands),
        [((heads, tokens, tokens), F32), (square, F32), (square, F32),
         ((heads, state_maps.shape[1] // 2), F32), (square, F32), ((1, channels), F32),
         ((tokens, width), F32)],
        10**8,
        [pltpu.VMEM(x.shape, x.dtype) for x in operands]
        + [pltpu.VMEM((tokens + 8, max(channels, state_maps.shape[1])), F32),
           pltpu.SemaphoreType.DMA((len(operands),))],
    )(*operands)


def conv_body(heads, summed, leading, conv_input, conv_maps, tail, ends, values, projected, sent):
    _, channels = values.shape
    state_dim = sent.shape[1]
    count = conv_input.shape[0]
    row = lax.broadcasted_iota(jnp.int32, (8, channels), 0)
    for out, kernel, first in ((values, conv_input, 0), (projected, conv_maps, channels)):
        columns = slice(first, first + out.shape[1])
        before = leading[:, columns].astype(F32)
        early = None
        for tap in range(count - 1):
            for at in range(count - 1 - tap):
                source = LEAD - (count - 1) + tap + at
                term = kernel[tap : tap + 1, :].astype(F32) * before[source : source + 1, :]
                term = jnp.where(row == at, term, 0.0)
                early = term if early is None else early + term
        out[...] = silu(summed[:, columns]).astype(BF16)
        fixed = silu(summed[0:8, columns] + early)
        fixed = jnp.concatenate([fixed, silu(summed[8:16, columns])], axis=0)
        out[0:16, :] = fixed.astype(BF16)
    high, low = halves(values[...].astype(F32) * tail[...])
    b_maps = projected[:, :state_dim]
    state = along(high, b_maps, 0, 0) + along(low, b_maps, 0, 0)
    sent[0:channels, :] = state.astype(BF16)
    end_high, end_low = halves(ends[...])
    rest = sent.shape[0] - channels - 2 * heads
    sent[channels:, :] = jnp.concatenate(
        [end_high.astype(F32), end_low.astype(F32), jnp.zeros((rest, state_dim), F32)], axis=0
    ).astype(BF16)


def inside_body(heads, head_dim, values, projected, mix, skip, out):
    tokens, _ = values.shape
    state_dim = projected.shape[1] // 2
    scores = along(projected[:, state_dim:], projected[:, :state_dim], 1, 1)
    pair = 128 // head_dim
    for first in range(0, heads, pair):
        columns = slice(first * head_dim, (first + pair) * head_dim)
        own = values[:, columns]
        lane = lax.broadcasted_iota(jnp.int32, (tokens, pair * head_dim), 1) // head_dim
        total = None
        for k in range(pair):
            weights = (scores * mix[first + k]).astype(BF16)
            part = along(weights, own, 1, 0)
            total = part if total is None else jnp.where(lane == k, part, total)
        out[:, columns] = total + skip[:, columns] * own.astype(F32)


def fetches(blocks, at, own_weight, other_weight, held, sems):
    width = held.shape[2]
    return [
        pltpu.make_async_copy(
            source.at[:, pl.ds(pl.multiple_of(blocks[2 * at + i] * width, width), width)],
            held.at[2 * k + i],
            sems.at[2 * k + i],
        )
        for k, source in enumerate((own_weight, other_weight))
        for i in range(2)
    ]


def norm_body(
    heads, head_dim, blocks, own_weight, other_weight, projected, inside, growth, gated, gain, *rest
):
    *messages, out, part, held, sems = rest
    copies = fetches(blocks, 0, own_weight, other_weight, held, sems)
    for copy in copies:
        copy.start()
    _, width = inside.shape
    state_dim = projected.shape[1] // 2
    pieces = []
    for head in range(heads):
        rows = slice(head * head_dim, (head + 1) * head_dim)
        carried = None
        for message in messages[::-1]:
            state = message[rows, :].astype(F32)
            if carried is not None:
                ends = message[width : width + 2 * heads, :].astype(F32)
                end = ends[head : head + 1, :] + ends[heads + head : heads + head + 1, :]
                state = end * carried + state
            carried = state
        pieces.append(carried)
    high, low = halves(jnp.concatenate(pieces, axis=0))
    c_maps = projected[:, state_dim:]
    carried_part = along(c_maps, high, 1, 1) + along(c_maps, low, 1, 1)
    value = (inside[...] + carried_part * growth[...]) * gated[...]
    row = lax.broadcasted_iota(jnp.int32, (width, width), 0) // head_dim
    column = lax.broadcasted_iota(jnp.int32, (width, width), 1) // head_dim
    alike = jnp.where(row == column, 1.0, 0.0).astype(BF16)
    high, low = halves(value * value)
    mean = (along(high, alike, 1, 0) + along(low, alike, 1, 0)) / head_dim
    out[...] = (value * lax.rsqrt(mean + 1e-05) * gain[...]).astype(BF16)
    for copy in copies:
        copy.wait()
    for i in range(2):
        part[i] = along(out[...], held[i], 1, 0)


def split(total, outs):
    rows = total.shape[0] // STREAMS
    for i in range(STREAMS):
        outs[i][...] = total[i * rows : (i + 1) * rows]


def first_body(other, part, held, *outs):
    for i in range(2):
        total = part[i] + along(other[...], held[2 + i], 1, 0)
        split(total.astype(BF16), outs[i * STREAMS : (i + 1) * STREAMS])


def product_body(at, blocks, own, other, own_weight, other_weight, *rest):
    *outs, held, sems = rest
    copies = fetches(blocks, at, own_weight, other_weight, held, sems)
    for copy in copies:
        copy.start()
    for copy in copies:
        copy.wait()
    for i in range(2):
        total = along(own[...], held[i], 1, 0) + along(other[...], held[2 + i], 1, 0)
        split(total, outs[i * STREAMS : (i + 1) * STREAMS])


def project(normed, part, held, out_weight, other_weight, blocks):
    devices = lax.axis_size("tensor")
    far = devices // CORES // 2
    width = out_weight.shape[1] // devices
    tokens, depth = normed.shape
    piece = (tokens // STREAMS, width)
    other = to_other_core(normed)
    work = 8 * tokens * depth * width
    parts = call(first_body, [VMEM] * 3, [(piece, BF16)] * (2 * STREAMS), work // 2)(
        other, part, held
    )
    ups, downs = list(parts[:STREAMS]), list(parts[STREAMS:])
    for step in range(1, far + 1):
        more = step < far
        if more:
            ups[0], normed, other = lax.optimization_barrier((ups[0], normed, other))
            parts = call(
                functools.partial(product_body, step),
                [SMEM, VMEM, VMEM, HBM, HBM],
                [(piece, F32)] * (2 * STREAMS),
                work,
                [pltpu.VMEM((4, depth, width), BF16), pltpu.SemaphoreType.DMA((4,))],
            )(blocks, normed, other, out_weight, other_weight)
        for i in range(STREAMS):
            ups[i] = to_chip(ups[i], 1)
            if more:
                ups[i] = (ups[i].astype(F32) + parts[i]).astype(BF16)
                downs[i] = to_chip(downs[i], -1).astype(F32) + parts[STREAMS + i]
                if step + 1 < far:
                    downs[i] = downs[i].astype(BF16)
    return jnp.concatenate(
        [(downs[i] + ups[i].astype(F32)).astype(BF16) for i in range(STREAMS)], axis=0
    )


def local(
    mixer_input,
    state_maps,
    gate_input,
    step_raw,
    decay_log,
    skip_gain,
    conv_input,
    conv_maps,
    norm_gain,
    out_weight,
):
    tokens, channels = mixer_input.shape
    heads = decay_log.shape[0]
    head_dim = channels // heads
    state_dim = state_maps.shape[1] // 2
    square = (tokens, channels)
    devices = lax.axis_size("tensor")
    chips = devices // CORES
    far = chips // 2
    steps = jnp.arange(far)
    offsets = jnp.stack([far - steps, jnp.where(steps < far - 1, steps + 1 - far, 0)], axis=1)
    blocks = lax.rem(
        lax.axis_index("tensor") + CORES * (offsets.reshape(-1) + chips), devices
    ).astype(jnp.int32)
    ending, step_raw = lax.optimization_barrier((tail_of(mixer_input, state_maps), step_raw))
    leading = shifted(ending, "seq", 1)
    mix, tail, growth, ends, gated, skip, summed = decay(
        step_raw, decay_log, skip_gain, gate_input, mixer_input, state_maps, conv_input,
        conv_maps,
    )
    gated, out_weight, blocks = lax.optimization_barrier((gated, out_weight, blocks))
    other_weight = to_other_core(out_weight)
    rows = channels + 16 * pl.cdiv(2 * heads, 16)
    values, projected, sent = call(
        functools.partial(conv_body, heads),
        [VMEM] * 6,
        [(square, BF16), (state_maps.shape, BF16), ((rows, state_dim), BF16)],
        10**8,
    )(summed, leading, conv_input, conv_maps, tail, ends)
    messages = [shifted(sent, "seq", by) for by in range(1, lax.axis_size("seq"))]
    (inside,) = call(
        functools.partial(inside_body, heads, head_dim), [VMEM] * 4, [(square, F32)], 10**9
    )(values, projected, mix, skip)
    width = out_weight.shape[1] // devices
    normed, part, held = call(
        functools.partial(norm_body, heads, head_dim),
        [SMEM, HBM, HBM] + [VMEM] * (5 + len(messages)),
        [(square, BF16), ((2, tokens, width), F32), ((4, channels, width), BF16)],
        10**8,
        [pltpu.SemaphoreType.DMA((4,))],
    )(blocks, out_weight, other_weight, projected, inside, growth, gated,
      norm_gain.reshape(1, channels), *messages)
    return project(normed, part, held, out_weight, other_weight, blocks)


def solution(mesh):
    placed = (
        P(("group", "seq"), "tensor"),
        P(("group", "seq"), None),
        P(("group", "seq"), "tensor"),
        P("tensor", ("group", "seq")),
        P("tensor"),
        P("tensor"),
        P(None, "tensor"),
        P(),
        P("tensor"),
        P("tensor", None),
    )

    return jax.shard_map(
        local, mesh=mesh, in_specs=placed, out_specs=P(("group", "seq"), "tensor"), check_vma=False
    )
```

time: 141 us -> 110 us (0.78)
  waiting for transfers between devices: 89.5 us -> 33.5 us
  starting transfers between devices: 21.7 us -> 54.3 us
  other arithmetic: 9.03 us -> 1.11 us
  local copies, waits for them, and re-layouts: 7.01 us -> 8.45 us
    ppermute x15 -> x30, waiting for transfers between devices: 66.1 us -> 9.65 us  [to_chip(): lax.ppermute(shard, 'tensor', [(i, (i + CORES * by) % devices) for i in r...]
    ppermute x15 -> x30, starting transfers between devices: 13.9 us -> 46.5 us  [to_chip(): lax.ppermute(shard, 'tensor', [(i, (i + CORES * by) % devices) for i in r...]
    unnamed x9 -> x24, local copies, waits for them, and re-layouts: 4.39 us -> 8.28 us
    mul x7 -> x0, other arithmetic: 3.58 us -> none  [the longest x2 1.68 us: causal_conv(): kernel[offset].astype(jnp.float32) * padded[offset:offset + values.shape[0]]]
    convert_element_type x12 -> x28, other arithmetic: 2.47 us -> 0.42 us  [the longest x14 0.2 us: project(): ups[i] = (ups[i].astype(F32) + parts[i]).astype(BF16)]
    slice x10 -> x0, local copies, waits for them, and re-layouts: 1.82 us -> none  [the longest x1 0.69 us: local(): mixer_input[tokens - lead_rows:]]
    pallas_call x2 -> x13, Pallas kernels: 11.1 us -> 11.7 us  [the longest x7 6.77 us: project(): call(functools.partial(product_body, step), [SMEM, VMEM, VMEM, HBM, HBM],...]
  transfers between devices with their start and end apart: 21 -> 36, of which waited for: 16 -> 6; matrix products, arithmetic and copies ran while one was open for 7% -> 0% of each run, Pallas kernels for 6% -> 7%
where the time goes in v2:
time: 110 us
  starting transfers between devices  54.3 us (49%)
  waiting for transfers between devices  33.5 us (30%)
  Pallas kernels  11.7 us (11%)
  local copies, waits for them, and re-layouts  8.45 us (8%)
  other arithmetic  1.11 us (1%)
    ppermute x30, starting transfers between devices, to_chip(): lax.ppermute(shard, 'tensor', [(i, (i + CORES * by) % devices) for i in r...  46.5 us
    ppermute x4, waiting for transfers between devices, shifted(): return lax.ppermute(shard, axis, pairs)  22.6 us
    ppermute x30, waiting for transfers between devices, to_chip(): lax.ppermute(shard, 'tensor', [(i, (i + CORES * by) % devices) for i in r...  9.65 us
    unnamed x24, local copies, waits for them, and re-layouts  8.28 us
    ppermute x4, starting transfers between devices, shifted(): return lax.ppermute(shard, axis, pairs)  7.49 us
    pallas_call x7, Pallas kernels, project(): call(functools.partial(product_body, step), [SMEM, VMEM, VMEM, HBM, HBM],...  6.77 us
    pallas_call x1, Pallas kernels, decay(): call(functools.partial(decay_body, heads, channels // heads), [HBM] * len...  2.37 us
  transfers between devices with their start and end apart: 36, of which 6 were waited for; matrix products, arithmetic and copies ran while one was open for 0% of the time, Pallas kernels for 7%

profile of v2, /device:TPU:34, one launch (start us, length us, event | category | flops | bytes accessed | tf_op | source)
XLA Modules:
  0.0 109.6 jit_solution(11393143310245735132)
XLA Ops:
  0.2 1.0 copy-done.1
  1.3 1.2 %copy-done.3 = bf16[256,256]{1,0:T(8,128)(2,1)S(1)} copy-done((bf16[256,256]{1,0:T(8,128)(2,1)S(1)}, bf16[256,256]{1,0:T(8,128)(2,1)}, u32[]{:S(2)}) %copy-start.3) | copy-done | bytes 131096
  8.5 2.4 %shard_map.101 = (f32[4,256,256]{2,1,0:T(8,128)S(1)}, f32[256,256]{1,0:T(8,128)S(1)}, f32[256,256]{1,0:T(8,128)S(1)}, f32[4,128]{1,0:T(4,128)S(1)}, f32[256,256]...) custom-call(f32[4,256]{1,0:T(4,128)S(1)} %copy-done.8, f32[1,4]{1,0:T(1,128)S(1)} %bitcast.4, ...), custom_call_target="tpu_custom_call" | custom-call | flops 100000000 | bytes 1048576 | tf_op jit(solution)/shard_map/pallas_call | solution.py:155
  11.1 3.6 %collective-permute-start.1 = (bf16[16,512]{1,0:T(8,128)(2,1)S(1)}, bf16[16,512]{1,0:T(8,128)(2,1)S(1)}, u32[]{:S(2)}, u32[]{:S(2)}) collective-permute-start(bf16[16,512]{1,0:T(8,128)(2,1)S(1)} %shard_map.100), channel_id=1, source_target_pairs={{0,1},{1,2},{2,3},{4,5},{5,6},{6,7},{8,9},{9,10},{10,11},{12,13},{... | collective-permute-start | bytes 49160 | tf_op jit(solution)/shard_map/ppermute | solution.py:25
  14.6 18.8 %collective-permute-done.1.leading = bf16[16,512]{1,0:T(8,128)(2,1)S(1)} collective-permute-done((bf16[16,512]{1,0:T(8,128)(2,1)S(1)}, bf16[16,512]{1,0:T(8,128)(2,1)S(1)}, u32[]{:S(2)}, u32[]{:S(2)}) %collective-permute-start.1) | collective-permute-done | bytes 16416 | tf_op jit(solution)/shard_map/ppermute | solution.py:25
  34.5 1.3 %collective-permute-start.3 = (bf16[272,128]{1,0:T(8,128)(2,1)S(1)}, bf16[272,128]{1,0:T(8,128)(2,1)S(1)}, u32[]{:S(2)}, u32[]{:S(2)}) collective-permute-start(bf16[272,128]{1,0:T(8,128)(2,1)S(1)} %get-tuple-element.90), channel_id=1, source_target_pairs={{0,2},{1,3},{4,6},{5,7},{8,10},{9,11},{12,14},{13,15},{16,18},{17,... | collective-permute-start | bytes 208904 | tf_op jit(solution)/shard_map/ppermute | solution.py:25
  35.9 2.0 %collective-permute-start.2 = (bf16[272,128]{1,0:T(8,128)(2,1)S(1)}, bf16[272,128]{1,0:T(8,128)(2,1)S(1)}, u32[]{:S(2)}, u32[]{:S(2)}) collective-permute-start(bf16[272,128]{1,0:T(8,128)(2,1)S(1)} %get-tuple-element.90), channel_id=1, source_target_pairs={{0,1},{1,2},{2,3},{4,5},{5,6},{6,7},{8,9},{9,10},{10,11},{12,13},{... | collective-permute-start | bytes 208904 | tf_op jit(solution)/shard_map/ppermute | solution.py:25
  38.3 3.8 %collective-permute-done.2.rest_0_ = bf16[272,128]{1,0:T(8,128)(2,1)S(1)} collective-permute-done((bf16[272,128]{1,0:T(8,128)(2,1)S(1)}, bf16[272,128]{1,0:T(8,128)(2,1)S(1)}, u32[]{:S(2)}, u32[]{:S(2)}) %collective-permute-start.2) | collective-permute-done | bytes 69664 | tf_op jit(solution)/shard_map/ppermute | solution.py:25
  42.1 1.4 %shard_map.104 = (bf16[256,256]{1,0:T(8,128)(2,1)S(1)}, f32[2,256,256]{2,1,0:T(8,128)S(1)}, bf16[4,256,256]{2,1,0:T(8,128)(2,1)S(1)}) custom-call(s32[16]{0:T(128)S(1)} %compare_select_fusion.blocks, bf16[256,8192]{1,0:T(8,128)(2,1)S(1)} %copy-done, bf16[256,8192]{1,0:T(8,128)(2,1)S(1)} %collective-permute-done.other_weight, ...), custom_call_target="tpu_custom_call" | custom-call | flops 100000000 | bytes 1048576 | tf_op jit(solution)/shard_map/pallas_call | solution.py:369
  43.7 1.3 %collective-permute-done.5.other = bf16[256,256]{1,0:T(8,128)(2,1)S(1)} collective-permute-done((bf16[256,256]{1,0:T(8,128)(2,1)S(1)}, bf16[256,256]{1,0:T(8,128)(2,1)S(1)}, u32[]{:S(2)}, u32[]{:S(2)}) %collective-permute-start.5) | collective-permute-done | bytes 131104 | tf_op jit(solution)/shard_map/ppermute | solution.py:30
  45.4 9.4 %collective-permute-start.6 = (bf16[128,256]{1,0:T(8,128)(2,1)S(1)}, bf16[128,256]{1,0:T(8,128)(2,1)S(1)}, u32[]{:S(2)}, u32[]{:S(2)}) collective-permute-start(bf16[128,256]{1,0:T(8,128)(2,1)S(1)} %get-tuple-element.94), channel_id=1, source_target_pairs={{0,120},{4,124},{8,0},{12,4},{16,8},{20,12},{24,16},{28,20},{32,24... | collective-permute-start | bytes 196616 | tf_op jit(solution)/shard_map/ppermute | solution.py:35
  54.8 1.9 %collective-permute-start.21 = (bf16[128,256]{1,0:T(8,128)(2,1)S(1)}, bf16[128,256]{1,0:T(8,128)(2,1)S(1)}, u32[]{:S(2)}, u32[]{:S(2)}) collective-permute-start(bf16[128,256]{1,0:T(8,128)(2,1)S(1)} %get-tuple-element.131), channel_id=1, source_target_pairs={{0,120},{4,124},{8,0},{12,4},{16,8},{20,12},{24,16},{28,20},{32,24... | collective-permute-start | bytes 196616 | tf_op jit(solution)/shard_map/ppermute | solution.py:35
  56.8 1.0 shard_map.106
  58.0 3.3 %collective-permute-start.7 = (bf16[128,256]{1,0:T(8,128)(2,1)S(1)}, bf16[128,256]{1,0:T(8,128)(2,1)S(1)}, u32[]{:S(2)}, u32[]{:S(2)}) collective-permute-start(bf16[128,256]{1,0:T(8,128)(2,1)S(1)} %add_convert_fusion.27), channel_id=1, source_target_pairs={{0,120},{4,124},{8,0},{12,4},{16,8},{20,12},{24,16},{28,20},{32,24... | collective-permute-start | bytes 196616 | tf_op jit(solution)/shard_map/ppermute | solution.py:35
  61.3 2.0 %collective-permute-start.22 = (bf16[128,256]{1,0:T(8,128)(2,1)S(1)}, bf16[128,256]{1,0:T(8,128)(2,1)S(1)}, u32[]{:S(2)}, u32[]{:S(2)}) collective-permute-start(bf16[128,256]{1,0:T(8,128)(2,1)S(1)} %add_convert_fusion.13), channel_id=1, source_target_pairs={{0,120},{4,124},{8,0},{12,4},{16,8},{20,12},{24,16},{28,20},{32,24... | collective-permute-start | bytes 196616 | tf_op jit(solution)/shard_map/ppermute | solution.py:35
  65.0 3.3 %collective-permute-start.9 = (bf16[128,256]{1,0:T(8,128)(2,1)S(1)}, bf16[128,256]{1,0:T(8,128)(2,1)S(1)}, u32[]{:S(2)}, u32[]{:S(2)}) collective-permute-start(bf16[128,256]{1,0:T(8,128)(2,1)S(1)} %add_convert_fusion.25), channel_id=1, source_target_pairs={{0,120},{4,124},{8,0},{12,4},{16,8},{20,12},{24,16},{28,20},{32,24... | collective-permute-start | bytes 196616 | tf_op jit(solution)/shard_map/ppermute | solution.py:35
  68.3 2.0 %collective-permute-start.23 = (bf16[128,256]{1,0:T(8,128)(2,1)S(1)}, bf16[128,256]{1,0:T(8,128)(2,1)S(1)}, u32[]{:S(2)}, u32[]{:S(2)}) collective-permute-start(bf16[128,256]{1,0:T(8,128)(2,1)S(1)} %add_convert_fusion.12), channel_id=1, source_target_pairs={{0,120},{4,124},{8,0},{12,4},{16,8},{20,12},{24,16},{28,20},{32,24... | collective-permute-start | bytes 196616 | tf_op jit(solution)/shard_map/ppermute | solution.py:35
  70.6 1.0 shard_map.108
  71.8 3.3 %collective-permute-start.11 = (bf16[128,256]{1,0:T(8,128)(2,1)S(1)}, bf16[128,256]{1,0:T(8,128)(2,1)S(1)}, u32[]{:S(2)}, u32[]{:S(2)}) collective-permute-start(bf16[128,256]{1,0:T(8,128)(2,1)S(1)} %add_convert_fusion.23), channel_id=1, source_target_pairs={{0,120},{4,124},{8,0},{12,4},{16,8},{20,12},{24,16},{28,20},{32,24... | collective-permute-start | bytes 196616 | tf_op jit(solution)/shard_map/ppermute | solution.py:35
  75.1 2.0 %collective-permute-start.24 = (bf16[128,256]{1,0:T(8,128)(2,1)S(1)}, bf16[128,256]{1,0:T(8,128)(2,1)S(1)}, u32[]{:S(2)}, u32[]{:S(2)}) collective-permute-start(bf16[128,256]{1,0:T(8,128)(2,1)S(1)} %add_convert_fusion.11), channel_id=1, source_target_pairs={{0,120},{4,124},{8,0},{12,4},{16,8},{20,12},{24,16},{28,20},{32,24... | collective-permute-start | bytes 196616 | tf_op jit(solution)/shard_map/ppermute | solution.py:35
  77.4 1.0 shard_map.109
  78.6 3.3 %collective-permute-start.13 = (bf16[128,256]{1,0:T(8,128)(2,1)S(1)}, bf16[128,256]{1,0:T(8,128)(2,1)S(1)}, u32[]{:S(2)}, u32[]{:S(2)}) collective-permute-start(bf16[128,256]{1,0:T(8,128)(2,1)S(1)} %add_convert_fusion.21), channel_id=1, source_target_pairs={{0,120},{4,124},{8,0},{12,4},{16,8},{20,12},{24,16},{28,20},{32,24... | collective-permute-start | bytes 196616 | tf_op jit(solution)/shard_map/ppermute | solution.py:35
  81.9 2.0 %collective-permute-start.25 = (bf16[128,256]{1,0:T(8,128)(2,1)S(1)}, bf16[128,256]{1,0:T(8,128)(2,1)S(1)}, u32[]{:S(2)}, u32[]{:S(2)}) collective-permute-start(bf16[128,256]{1,0:T(8,128)(2,1)S(1)} %add_convert_fusion.10), channel_id=1, source_target_pairs={{0,120},{4,124},{8,0},{12,4},{16,8},{20,12},{24,16},{28,20},{32,24... | collective-permute-start | bytes 196616 | tf_op jit(solution)/shard_map/ppermute | solution.py:35
  84.2 1.0 shard_map.110
  85.3 3.3 %collective-permute-start.15 = (bf16[128,256]{1,0:T(8,128)(2,1)S(1)}, bf16[128,256]{1,0:T(8,128)(2,1)S(1)}, u32[]{:S(2)}, u32[]{:S(2)}) collective-permute-start(bf16[128,256]{1,0:T(8,128)(2,1)S(1)} %add_convert_fusion.19), channel_id=1, source_target_pairs={{0,120},{4,124},{8,0},{12,4},{16,8},{20,12},{24,16},{28,20},{32,24... | collective-permute-start | bytes 196616 | tf_op jit(solution)/shard_map/ppermute | solution.py:35
  88.7 2.2 %collective-permute-start.26 = (bf16[128,256]{1,0:T(8,128)(2,1)S(1)}, bf16[128,256]{1,0:T(8,128)(2,1)S(1)}, u32[]{:S(2)}, u32[]{:S(2)}) collective-permute-start(bf16[128,256]{1,0:T(8,128)(2,1)S(1)} %add_convert_fusion.9), channel_id=1, source_target_pairs={{0,120},{4,124},{8,0},{12,4},{16,8},{20,12},{24,16},{28,20},{32,24... | collective-permute-start | bytes 196616 | tf_op jit(solution)/shard_map/ppermute | solution.py:35
  91.2 1.0 shard_map.111
  92.3 3.3 %collective-permute-start.17 = (bf16[128,256]{1,0:T(8,128)(2,1)S(1)}, bf16[128,256]{1,0:T(8,128)(2,1)S(1)}, u32[]{:S(2)}, u32[]{:S(2)}) collective-permute-start(bf16[128,256]{1,0:T(8,128)(2,1)S(1)} %add_convert_fusion.17), channel_id=1, source_target_pairs={{0,120},{4,124},{8,0},{12,4},{16,8},{20,12},{24,16},{28,20},{32,24... | collective-permute-start | bytes 196616 | tf_op jit(solution)/shard_map/ppermute | solution.py:35
  95.7 2.0 %collective-permute-start.27 = (bf16[128,256]{1,0:T(8,128)(2,1)S(1)}, bf16[128,256]{1,0:T(8,128)(2,1)S(1)}, u32[]{:S(2)}, u32[]{:S(2)}) collective-permute-start(bf16[128,256]{1,0:T(8,128)(2,1)S(1)} %add_convert_fusion.8), channel_id=1, source_target_pairs={{0,120},{4,124},{8,0},{12,4},{16,8},{20,12},{24,16},{28,20},{32,24... | collective-permute-start | bytes 196616 | tf_op jit(solution)/shard_map/ppermute | solution.py:35
  99.1 4.2 %collective-permute-done.34 = bf16[128,256]{1,0:T(8,128)(2,1)S(1)} collective-permute-done((bf16[128,256]{1,0:T(8,128)(2,1)S(1)}, bf16[128,256]{1,0:T(8,128)(2,1)S(1)}, u32[]{:S(2)}, u32[]{:S(2)}) %collective-permute-start.34) | collective-permute-done | bytes 65568 | tf_op jit(solution)/shard_map/ppermute | solution.py:35
  103.4 1.1 %collective-permute-done.20 = bf16[128,256]{1,0:T(8,128)(2,1)S(1)} collective-permute-done((bf16[128,256]{1,0:T(8,128)(2,1)S(1)}, bf16[128,256]{1,0:T(8,128)(2,1)S(1)}, u32[]{:S(2)}, u32[]{:S(2)}) %collective-permute-start.20) | collective-permute-done | bytes 65568 | tf_op jit(solution)/shard_map/ppermute | solution.py:35
  104.6 4.3 %collective-permute-done.35 = bf16[128,256]{1,0:T(8,128)(2,1)S(1)} collective-permute-done((bf16[128,256]{1,0:T(8,128)(2,1)S(1)}, bf16[128,256]{1,0:T(8,128)(2,1)S(1)}, u32[]{:S(2)}, u32[]{:S(2)}) %collective-permute-start.35) | collective-permute-done | bytes 65568 | tf_op jit(solution)/shard_map/ppermute | solution.py:35
  (111 shorter events, 14.6 us)
Async XLA Ops:
  10.9 31.2 %collective-permute-start = (bf16[256,8192]{1,0:T(8,128)(2,1)}, bf16[256,8192]{1,0:T(8,128)(2,1)S(1)}, u32[]{:S(2)}, u32[]{:S(2)}) collective-permute-start(bf16[256,8192]{1,0:T(8,128)(2,1)} %own_weight.7), channel_id=1, source_target_pairs={{0,4},{4,0},{8,12},{12,8},{16,20},{20,16},{24,28},{28,24},{32,36},... | collective-permute-start | bytes 12582920 | tf_op jit(solution)/shard_map/ppermute | solution.py:30
  11.1 22.4 %collective-permute-start.1 = (bf16[16,512]{1,0:T(8,128)(2,1)S(1)}, bf16[16,512]{1,0:T(8,128)(2,1)S(1)}, u32[]{:S(2)}, u32[]{:S(2)}) collective-permute-start(bf16[16,512]{1,0:T(8,128)(2,1)S(1)} %shard_map.100), channel_id=1, source_target_pairs={{0,1},{1,2},{2,3},{4,5},{5,6},{6,7},{8,9},{9,10},{10,11},{12,13},{... | collective-permute-start | bytes 49160 | tf_op jit(solution)/shard_map/ppermute | solution.py:25
  35.9 6.2 %collective-permute-start.2 = (bf16[272,128]{1,0:T(8,128)(2,1)S(1)}, bf16[272,128]{1,0:T(8,128)(2,1)S(1)}, u32[]{:S(2)}, u32[]{:S(2)}) collective-permute-start(bf16[272,128]{1,0:T(8,128)(2,1)S(1)} %get-tuple-element.90), channel_id=1, source_target_pairs={{0,1},{1,2},{2,3},{4,5},{5,6},{6,7},{8,9},{9,10},{10,11},{12,13},{... | collective-permute-start | bytes 208904 | tf_op jit(solution)/shard_map/ppermute | solution.py:25
  45.2 12.6 %collective-permute-start.8 = (bf16[128,256]{1,0:T(8,128)(2,1)S(1)}, bf16[128,256]{1,0:T(8,128)(2,1)S(1)}, u32[]{:S(2)}, u32[]{:S(2)}) collective-permute-start(bf16[128,256]{1,0:T(8,128)(2,1)S(1)} %get-tuple-element.99), channel_id=1, source_target_pairs={{0,8},{4,12},{8,16},{12,20},{16,24},{20,28},{24,32},{28,36},{32,40... | collective-permute-start | bytes 196616 | tf_op jit(solution)/shard_map/ppermute | solution.py:35
  45.4 12.6 %collective-permute-start.6 = (bf16[128,256]{1,0:T(8,128)(2,1)S(1)}, bf16[128,256]{1,0:T(8,128)(2,1)S(1)}, u32[]{:S(2)}, u32[]{:S(2)}) collective-permute-start(bf16[128,256]{1,0:T(8,128)(2,1)S(1)} %get-tuple-element.94), channel_id=1, source_target_pairs={{0,120},{4,124},{8,0},{12,4},{16,8},{20,12},{24,16},{28,20},{32,24... | collective-permute-start | bytes 196616 | tf_op jit(solution)/shard_map/ppermute | solution.py:35
  54.8 6.5 %collective-permute-start.21 = (bf16[128,256]{1,0:T(8,128)(2,1)S(1)}, bf16[128,256]{1,0:T(8,128)(2,1)S(1)}, u32[]{:S(2)}, u32[]{:S(2)}) collective-permute-start(bf16[128,256]{1,0:T(8,128)(2,1)S(1)} %get-tuple-element.131), channel_id=1, source_target_pairs={{0,120},{4,124},{8,0},{12,4},{16,8},{20,12},{24,16},{28,20},{32,24... | collective-permute-start | bytes 196616 | tf_op jit(solution)/shard_map/ppermute | solution.py:35
  56.7 6.7 %collective-permute-start.28 = (bf16[128,256]{1,0:T(8,128)(2,1)S(1)}, bf16[128,256]{1,0:T(8,128)(2,1)S(1)}, u32[]{:S(2)}, u32[]{:S(2)}) collective-permute-start(bf16[128,256]{1,0:T(8,128)(2,1)S(1)} %get-tuple-element.139), channel_id=1, source_target_pairs={{0,8},{4,12},{8,16},{12,20},{16,24},{20,28},{24,32},{28,36},{32,40... | collective-permute-start | bytes 196616 | tf_op jit(solution)/shard_map/ppermute | solution.py:35
  57.8 6.8 %collective-permute-start.10 = (bf16[128,256]{1,0:T(8,128)(2,1)S(1)}, bf16[128,256]{1,0:T(8,128)(2,1)S(1)}, u32[]{:S(2)}, u32[]{:S(2)}) collective-permute-start(bf16[128,256]{1,0:T(8,128)(2,1)S(1)} %add_convert_fusion.26), channel_id=1, source_target_pairs={{0,8},{4,12},{8,16},{12,20},{16,24},{20,28},{24,32},{28,36},{32,40... | collective-permute-start | bytes 196616 | tf_op jit(solution)/shard_map/ppermute | solution.py:35
  58.0 6.9 %collective-permute-start.7 = (bf16[128,256]{1,0:T(8,128)(2,1)S(1)}, bf16[128,256]{1,0:T(8,128)(2,1)S(1)}, u32[]{:S(2)}, u32[]{:S(2)}) collective-permute-start(bf16[128,256]{1,0:T(8,128)(2,1)S(1)} %add_convert_fusion.27), channel_id=1, source_target_pairs={{0,120},{4,124},{8,0},{12,4},{16,8},{20,12},{24,16},{28,20},{32,24... | collective-permute-start | bytes 196616 | tf_op jit(solution)/shard_map/ppermute | solution.py:35
  61.3 6.9 %collective-permute-start.22 = (bf16[128,256]{1,0:T(8,128)(2,1)S(1)}, bf16[128,256]{1,0:T(8,128)(2,1)S(1)}, u32[]{:S(2)}, u32[]{:S(2)}) collective-permute-start(bf16[128,256]{1,0:T(8,128)(2,1)S(1)} %add_convert_fusion.13), channel_id=1, source_target_pairs={{0,120},{4,124},{8,0},{12,4},{16,8},{20,12},{24,16},{28,20},{32,24... | collective-permute-start | bytes 196616 | tf_op jit(solution)/shard_map/ppermute | solution.py:35
  63.4 6.9 %collective-permute-start.29 = (bf16[128,256]{1,0:T(8,128)(2,1)S(1)}, bf16[128,256]{1,0:T(8,128)(2,1)S(1)}, u32[]{:S(2)}, u32[]{:S(2)}) collective-permute-start(bf16[128,256]{1,0:T(8,128)(2,1)S(1)} %add_convert_fusion.7), channel_id=1, source_target_pairs={{0,8},{4,12},{8,16},{12,20},{16,24},{20,28},{24,32},{28,36},{32,40... | collective-permute-start | bytes 196616 | tf_op jit(solution)/shard_map/ppermute | solution.py:35
  64.6 6.9 %collective-permute-start.12 = (bf16[128,256]{1,0:T(8,128)(2,1)S(1)}, bf16[128,256]{1,0:T(8,128)(2,1)S(1)}, u32[]{:S(2)}, u32[]{:S(2)}) collective-permute-start(bf16[128,256]{1,0:T(8,128)(2,1)S(1)} %add_convert_fusion.24), channel_id=1, source_target_pairs={{0,8},{4,12},{8,16},{12,20},{16,24},{20,28},{24,32},{28,36},{32,40... | collective-permute-start | bytes 196616 | tf_op jit(solution)/shard_map/ppermute | solution.py:35
  65.0 6.8 %collective-permute-start.9 = (bf16[128,256]{1,0:T(8,128)(2,1)S(1)}, bf16[128,256]{1,0:T(8,128)(2,1)S(1)}, u32[]{:S(2)}, u32[]{:S(2)}) collective-permute-start(bf16[128,256]{1,0:T(8,128)(2,1)S(1)} %add_convert_fusion.25), channel_id=1, source_target_pairs={{0,120},{4,124},{8,0},{12,4},{16,8},{20,12},{24,16},{28,20},{32,24... | collective-permute-start | bytes 196616 | tf_op jit(solution)/shard_map/ppermute | solution.py:35
  68.3 6.8 %collective-permute-start.23 = (bf16[128,256]{1,0:T(8,128)(2,1)S(1)}, bf16[128,256]{1,0:T(8,128)(2,1)S(1)}, u32[]{:S(2)}, u32[]{:S(2)}) collective-permute-start(bf16[128,256]{1,0:T(8,128)(2,1)S(1)} %add_convert_fusion.12), channel_id=1, source_target_pairs={{0,120},{4,124},{8,0},{12,4},{16,8},{20,12},{24,16},{28,20},{32,24... | collective-permute-start | bytes 196616 | tf_op jit(solution)/shard_map/ppermute | solution.py:35
  70.3 6.8 %collective-permute-start.30 = (bf16[128,256]{1,0:T(8,128)(2,1)S(1)}, bf16[128,256]{1,0:T(8,128)(2,1)S(1)}, u32[]{:S(2)}, u32[]{:S(2)}) collective-permute-start(bf16[128,256]{1,0:T(8,128)(2,1)S(1)} %add_convert_fusion.6), channel_id=1, source_target_pairs={{0,8},{4,12},{8,16},{12,20},{16,24},{20,28},{24,32},{28,36},{32,40... | collective-permute-start | bytes 196616 | tf_op jit(solution)/shard_map/ppermute | solution.py:35
  71.6 6.8 %collective-permute-start.14 = (bf16[128,256]{1,0:T(8,128)(2,1)S(1)}, bf16[128,256]{1,0:T(8,128)(2,1)S(1)}, u32[]{:S(2)}, u32[]{:S(2)}) collective-permute-start(bf16[128,256]{1,0:T(8,128)(2,1)S(1)} %add_convert_fusion.22), channel_id=1, source_target_pairs={{0,8},{4,12},{8,16},{12,20},{16,24},{20,28},{24,32},{28,36},{32,40... | collective-permute-start | bytes 196616 | tf_op jit(solution)/shard_map/ppermute | solution.py:35
  71.8 6.8 %collective-permute-start.11 = (bf16[128,256]{1,0:T(8,128)(2,1)S(1)}, bf16[128,256]{1,0:T(8,128)(2,1)S(1)}, u32[]{:S(2)}, u32[]{:S(2)}) collective-permute-start(bf16[128,256]{1,0:T(8,128)(2,1)S(1)} %add_convert_fusion.23), channel_id=1, source_target_pairs={{0,120},{4,124},{8,0},{12,4},{16,8},{20,12},{24,16},{28,20},{32,24... | collective-permute-start | bytes 196616 | tf_op jit(solution)/shard_map/ppermute | solution.py:35
  75.1 6.8 %collective-permute-start.24 = (bf16[128,256]{1,0:T(8,128)(2,1)S(1)}, bf16[128,256]{1,0:T(8,128)(2,1)S(1)}, u32[]{:S(2)}, u32[]{:S(2)}) collective-permute-start(bf16[128,256]{1,0:T(8,128)(2,1)S(1)} %add_convert_fusion.11), channel_id=1, source_target_pairs={{0,120},{4,124},{8,0},{12,4},{16,8},{20,12},{24,16},{28,20},{32,24... | collective-permute-start | bytes 196616 | tf_op jit(solution)/shard_map/ppermute | solution.py:35
  77.1 6.8 %collective-permute-start.31 = (bf16[128,256]{1,0:T(8,128)(2,1)S(1)}, bf16[128,256]{1,0:T(8,128)(2,1)S(1)}, u32[]{:S(2)}, u32[]{:S(2)}) collective-permute-start(bf16[128,256]{1,0:T(8,128)(2,1)S(1)} %add_convert_fusion.5), channel_id=1, source_target_pairs={{0,8},{4,12},{8,16},{12,20},{16,24},{20,28},{24,32},{28,36},{32,40... | collective-permute-start | bytes 196616 | tf_op jit(solution)/shard_map/ppermute | solution.py:35
  78.4 6.8 %collective-permute-start.16 = (bf16[128,256]{1,0:T(8,128)(2,1)S(1)}, bf16[128,256]{1,0:T(8,128)(2,1)S(1)}, u32[]{:S(2)}, u32[]{:S(2)}) collective-permute-start(bf16[128,256]{1,0:T(8,128)(2,1)S(1)} %add_convert_fusion.20), channel_id=1, source_target_pairs={{0,8},{4,12},{8,16},{12,20},{16,24},{20,28},{24,32},{28,36},{32,40... | collective-permute-start | bytes 196616 | tf_op jit(solution)/shard_map/ppermute | solution.py:35
  78.6 6.8 %collective-permute-start.13 = (bf16[128,256]{1,0:T(8,128)(2,1)S(1)}, bf16[128,256]{1,0:T(8,128)(2,1)S(1)}, u32[]{:S(2)}, u32[]{:S(2)}) collective-permute-start(bf16[128,256]{1,0:T(8,128)(2,1)S(1)} %add_convert_fusion.21), channel_id=1, source_target_pairs={{0,120},{4,124},{8,0},{12,4},{16,8},{20,12},{24,16},{28,20},{32,24... | collective-permute-start | bytes 196616 | tf_op jit(solution)/shard_map/ppermute | solution.py:35
  81.9 6.8 %collective-permute-start.25 = (bf16[128,256]{1,0:T(8,128)(2,1)S(1)}, bf16[128,256]{1,0:T(8,128)(2,1)S(1)}, u32[]{:S(2)}, u32[]{:S(2)}) collective-permute-start(bf16[128,256]{1,0:T(8,128)(2,1)S(1)} %add_convert_fusion.10), channel_id=1, source_target_pairs={{0,120},{4,124},{8,0},{12,4},{16,8},{20,12},{24,16},{28,20},{32,24... | collective-permute-start | bytes 196616 | tf_op jit(solution)/shard_map/ppermute | solution.py:35
  83.9 7.0 %collective-permute-start.32 = (bf16[128,256]{1,0:T(8,128)(2,1)S(1)}, bf16[128,256]{1,0:T(8,128)(2,1)S(1)}, u32[]{:S(2)}, u32[]{:S(2)}) collective-permute-start(bf16[128,256]{1,0:T(8,128)(2,1)S(1)} %add_convert_fusion.4), channel_id=1, source_target_pairs={{0,8},{4,12},{8,16},{12,20},{16,24},{20,28},{24,32},{28,36},{32,40... | collective-permute-start | bytes 196616 | tf_op jit(solution)/shard_map/ppermute | solution.py:35
  85.2 7.0 %collective-permute-start.18 = (bf16[128,256]{1,0:T(8,128)(2,1)S(1)}, bf16[128,256]{1,0:T(8,128)(2,1)S(1)}, u32[]{:S(2)}, u32[]{:S(2)}) collective-permute-start(bf16[128,256]{1,0:T(8,128)(2,1)S(1)} %add_convert_fusion.18), channel_id=1, source_target_pairs={{0,8},{4,12},{8,16},{12,20},{16,24},{20,28},{24,32},{28,36},{32,40... | collective-permute-start | bytes 196616 | tf_op jit(solution)/shard_map/ppermute | solution.py:35
  85.3 7.0 %collective-permute-start.15 = (bf16[128,256]{1,0:T(8,128)(2,1)S(1)}, bf16[128,256]{1,0:T(8,128)(2,1)S(1)}, u32[]{:S(2)}, u32[]{:S(2)}) collective-permute-start(bf16[128,256]{1,0:T(8,128)(2,1)S(1)} %add_convert_fusion.19), channel_id=1, source_target_pairs={{0,120},{4,124},{8,0},{12,4},{16,8},{20,12},{24,16},{28,20},{32,24... | collective-permute-start | bytes 196616 | tf_op jit(solution)/shard_map/ppermute | solution.py:35
  88.7 7.0 %collective-permute-start.26 = (bf16[128,256]{1,0:T(8,128)(2,1)S(1)}, bf16[128,256]{1,0:T(8,128)(2,1)S(1)}, u32[]{:S(2)}, u32[]{:S(2)}) collective-permute-start(bf16[128,256]{1,0:T(8,128)(2,1)S(1)} %add_convert_fusion.9), channel_id=1, source_target_pairs={{0,120},{4,124},{8,0},{12,4},{16,8},{20,12},{24,16},{28,20},{32,24... | collective-permute-start | bytes 196616 | tf_op jit(solution)/shard_map/ppermute | solution.py:35
  90.9 6.8 %collective-permute-start.33 = (bf16[128,256]{1,0:T(8,128)(2,1)S(1)}, bf16[128,256]{1,0:T(8,128)(2,1)S(1)}, u32[]{:S(2)}, u32[]{:S(2)}) collective-permute-start(bf16[128,256]{1,0:T(8,128)(2,1)S(1)} %add_convert_fusion.3), channel_id=1, source_target_pairs={{0,8},{4,12},{8,16},{12,20},{16,24},{20,28},{24,32},{28,36},{32,40... | collective-permute-start | bytes 196616 | tf_op jit(solution)/shard_map/ppermute | solution.py:35
  92.2 6.8 %collective-permute-start.19 = (bf16[128,256]{1,0:T(8,128)(2,1)S(1)}, bf16[128,256]{1,0:T(8,128)(2,1)S(1)}, u32[]{:S(2)}, u32[]{:S(2)}) collective-permute-start(bf16[128,256]{1,0:T(8,128)(2,1)S(1)} %add_convert_fusion.16), channel_id=1, source_target_pairs={{0,8},{4,12},{8,16},{12,20},{16,24},{20,28},{24,32},{28,36},{32,40... | collective-permute-start | bytes 196616 | tf_op jit(solution)/shard_map/ppermute | solution.py:35
  92.3 11.1 %collective-permute-start.17 = (bf16[128,256]{1,0:T(8,128)(2,1)S(1)}, bf16[128,256]{1,0:T(8,128)(2,1)S(1)}, u32[]{:S(2)}, u32[]{:S(2)}) collective-permute-start(bf16[128,256]{1,0:T(8,128)(2,1)S(1)} %add_convert_fusion.17), channel_id=1, source_target_pairs={{0,120},{4,124},{8,0},{12,4},{16,8},{20,12},{24,16},{28,20},{32,24... | collective-permute-start | bytes 196616 | tf_op jit(solution)/shard_map/ppermute | solution.py:35
  95.7 8.9 %collective-permute-start.27 = (bf16[128,256]{1,0:T(8,128)(2,1)S(1)}, bf16[128,256]{1,0:T(8,128)(2,1)S(1)}, u32[]{:S(2)}, u32[]{:S(2)}) collective-permute-start(bf16[128,256]{1,0:T(8,128)(2,1)S(1)} %add_convert_fusion.8), channel_id=1, source_target_pairs={{0,120},{4,124},{8,0},{12,4},{16,8},{20,12},{24,16},{28,20},{32,24... | collective-permute-start | bytes 196616 | tf_op jit(solution)/shard_map/ppermute | solution.py:35
  99.0 5.6 %collective-permute-start.20 = (bf16[128,256]{1,0:T(8,128)(2,1)S(1)}, bf16[128,256]{1,0:T(8,128)(2,1)S(1)}, u32[]{:S(2)}, u32[]{:S(2)}) collective-permute-start(bf16[128,256]{1,0:T(8,128)(2,1)S(1)} %add_convert_fusion.15), channel_id=1, source_target_pairs={{0,8},{4,12},{8,16},{12,20},{16,24},{20,28},{24,32},{28,36},{32,40... | collective-permute-start | bytes 196616 | tf_op jit(solution)/shard_map/ppermute | solution.py:35
  103.3 5.6 %collective-permute-start.35 = (bf16[128,256]{1,0:T(8,128)(2,1)S(1)}, bf16[128,256]{1,0:T(8,128)(2,1)S(1)}, u32[]{:S(2)}, u32[]{:S(2)}) collective-permute-start(bf16[128,256]{1,0:T(8,128)(2,1)S(1)} %add_convert_fusion.1), channel_id=1, source_target_pairs={{0,8},{4,12},{8,16},{12,20},{16,24},{20,28},{24,32},{28,36},{32,40... | collective-permute-start | bytes 196616 | tf_op jit(solution)/shard_map/ppermute | solution.py:35
  (16 other events, 107.6 us)

commit v3 on v2

--- a/solution.py
+++ b/solution.py
@@ -9,7 +9,6 @@
 
 
 CORES = 2
-STREAMS = 2
 LEAD = 16
 F32 = jnp.float32
 BF16 = jnp.bfloat16
@@ -30,21 +29,25 @@
     return lax.ppermute(shard, "tensor", [(i, i ^ 1) for i in range(devices)])
 
 
-def to_chip(shard, by):
+def to_chip(shard, by, core):
     devices = lax.axis_size("tensor")
-    return lax.ppermute(
-        shard, "tensor", [(i, (i + CORES * by) % devices) for i in range(devices)]
-    )
-
-
-def call(body, specs, shapes, flops, scratch=()):
+    first = CORES - 1
+    pairs = [(i, (i - first + CORES * by + core) % devices) for i in range(first, devices, CORES)]
+    return lax.ppermute(shard, "tensor", pairs)
+
+
+def in_hbm(x):
+    return pltpu.with_memory_space_constraint(x, pltpu.HBM)
+
+
+def call(body, specs, shapes, flops, scratch=(), grant=16 << 20):
     return pl.pallas_call(
         body,
         in_specs=specs,
         out_specs=tuple(VMEM for _ in shapes),
         out_shape=tuple(jax.ShapeDtypeStruct(s, d) for s, d in shapes),
         scratch_shapes=list(scratch),
-        compiler_params=pltpu.CompilerParams(vmem_limit_bytes=16 << 20),
+        compiler_params=pltpu.CompilerParams(vmem_limit_bytes=grant),
         cost_estimate=pl.CostEstimate(flops=flops, bytes_accessed=1 << 20, transcendentals=0),
     )
 
@@ -88,13 +91,13 @@
 def tail_of(mixer_input, state_maps):
     width = mixer_input.shape[1] + state_maps.shape[1]
     return call(
-        tail_body, [HBM, HBM], [((LEAD, width), BF16)], 1000, [pltpu.SemaphoreType.DMA((2,))]
-    )(mixer_input, state_maps)[0]
+        tail_body, [HBM, HBM], [((LEAD, width), BF16)], 1000, [pltpu.SemaphoreType.DMA((2,))],
+    )(in_hbm(mixer_input), in_hbm(state_maps))[0]
 
 
 def decay_body(
     heads, head_dim, step_hbm, decay_hbm, skip_hbm, gate_hbm, mixer_hbm, maps_hbm, taps_hbm,
-    map_taps_hbm, mix, tail, growth, ends, gated, skip, summed,
+    map_taps_hbm, mix, tail, growth, ends, gated, skip, summed, wide_taps,
     raw, logs, gains, gate, mixer, maps, taps, map_taps, padded, sems
 ):
     pairs = [(decay_hbm, logs), (step_hbm, raw), (skip_hbm, gains), (gate_hbm, gate),
@@ -136,10 +139,12 @@
         columns = source.shape[1]
         padded[0:8, :columns] = jnp.zeros((8, columns), F32)
         padded[8 : 8 + tokens, :columns] = source[...].astype(F32)
+        wide_taps[:, first : first + columns] = kernel[...].astype(F32)
         total = None
         for tap in range(count):
             at = 9 - count + tap
-            term = kernel[tap : tap + 1, :].astype(F32) * padded[at : at + tokens, :columns]
+            scale = wide_taps[tap : tap + 1, first : first + columns]
+            term = scale * padded[at : at + tokens, :columns]
             total = term if total is None else total + term
         summed[:, first : first + columns] = total
 
@@ -157,27 +162,27 @@
         [HBM] * len(operands),
         [((heads, tokens, tokens), F32), (square, F32), (square, F32),
          ((heads, state_maps.shape[1] // 2), F32), (square, F32), ((1, channels), F32),
-         ((tokens, width), F32)],
+         ((tokens, width), F32), ((conv_input.shape[0], width), F32)],
         10**8,
         [pltpu.VMEM(x.shape, x.dtype) for x in operands]
         + [pltpu.VMEM((tokens + 8, max(channels, state_maps.shape[1])), F32),
            pltpu.SemaphoreType.DMA((len(operands),))],
-    )(*operands)
-
-
-def conv_body(heads, summed, leading, conv_input, conv_maps, tail, ends, values, projected, sent):
+    )(*(in_hbm(x) for x in operands))
+
+
+def conv_body(heads, summed, leading, taps, tail, ends, values, projected, sent):
     _, channels = values.shape
     state_dim = sent.shape[1]
-    count = conv_input.shape[0]
+    count = taps.shape[0]
     row = lax.broadcasted_iota(jnp.int32, (8, channels), 0)
-    for out, kernel, first in ((values, conv_input, 0), (projected, conv_maps, channels)):
+    for out, first in ((values, 0), (projected, channels)):
         columns = slice(first, first + out.shape[1])
         before = leading[:, columns].astype(F32)
         early = None
         for tap in range(count - 1):
             for at in range(count - 1 - tap):
                 source = LEAD - (count - 1) + tap + at
-                term = kernel[tap : tap + 1, :].astype(F32) * before[source : source + 1, :]
+                term = taps[tap : tap + 1, columns] * before[source : source + 1, :]
                 term = jnp.where(row == at, term, 0.0)
                 early = term if early is None else early + term
         out[...] = silu(summed[:, columns]).astype(BF16)
@@ -212,24 +217,26 @@
         out[:, columns] = total + skip[:, columns] * own.astype(F32)
 
 
-def fetches(blocks, at, own_weight, other_weight, held, sems):
+def fetches(me, chips, bys, weights, held, sems):
     width = held.shape[2]
-    return [
-        pltpu.make_async_copy(
-            source.at[:, pl.ds(pl.multiple_of(blocks[2 * at + i] * width, width), width)],
-            held.at[2 * k + i],
-            sems.at[2 * k + i],
-        )
-        for k, source in enumerate((own_weight, other_weight))
-        for i in range(2)
-    ]
+    copies = []
+    for i, by in enumerate(bys):
+        chip = lax.rem(lax.div(me[0], CORES) + by + chips, chips)
+        at = pl.ds(pl.multiple_of(chip * width, width), width)
+        for k, weight in enumerate(weights):
+            place = len(weights) * i + k
+            copies.append(
+                pltpu.make_async_copy(weight.at[:, at], held.at[place], sems.at[place])
+            )
+    return copies
 
 
 def norm_body(
-    heads, head_dim, blocks, own_weight, other_weight, projected, inside, growth, gated, gain, *rest
+    heads, head_dim, chips, bys, me, position, own_weight, other_weight, projected, inside, growth,
+    gated, gain, *rest
 ):
-    *messages, out, part, held, sems = rest
-    copies = fetches(blocks, 0, own_weight, other_weight, held, sems)
+    *messages, out, held, sems = rest
+    copies = fetches(me, chips, bys, (own_weight, other_weight), held, sems)
     for copy in copies:
         copy.start()
     _, width = inside.shape
@@ -238,13 +245,14 @@
     for head in range(heads):
         rows = slice(head * head_dim, (head + 1) * head_dim)
         carried = None
-        for message in messages[::-1]:
+        for by in range(len(messages), 0, -1):
+            message = messages[by - 1]
             state = message[rows, :].astype(F32)
             if carried is not None:
                 ends = message[width : width + 2 * heads, :].astype(F32)
                 end = ends[head : head + 1, :] + ends[heads + head : heads + head + 1, :]
                 state = end * carried + state
-            carried = state
+            carried = jnp.where(position[0] >= by, state, 0.0)
         pieces.append(carried)
     high, low = halves(jnp.concatenate(pieces, axis=0))
     c_maps = projected[:, state_dim:]
@@ -258,67 +266,87 @@
     out[...] = (value * lax.rsqrt(mean + 1e-05) * gain[...]).astype(BF16)
     for copy in copies:
         copy.wait()
-    for i in range(2):
-        part[i] = along(out[...], held[i], 1, 0)
-
-
-def split(total, outs):
-    rows = total.shape[0] // STREAMS
-    for i in range(STREAMS):
-        outs[i][...] = total[i * rows : (i + 1) * rows]
-
-
-def first_body(other, part, held, *outs):
-    for i in range(2):
-        total = part[i] + along(other[...], held[2 + i], 1, 0)
-        split(total.astype(BF16), outs[i * STREAMS : (i + 1) * STREAMS])
-
-
-def product_body(at, blocks, own, other, own_weight, other_weight, *rest):
-    *outs, held, sems = rest
-    copies = fetches(blocks, at, own_weight, other_weight, held, sems)
+
+
+def own_body(own, held, *parts):
+    for i, part in enumerate(parts):
+        part[...] = along(own[...], held[2 * i], 1, 0)
+
+
+def first_body(other, held, *rest):
+    count = len(rest) // (1 + CORES)
+    for i, part in enumerate(rest[:count]):
+        total = part[...] + along(other[...], held[2 * i + 1], 1, 0)
+        outs = rest[count + CORES * i : count + CORES * (i + 1)]
+        width = total.shape[1] // CORES
+        for core, out in enumerate(outs):
+            out[...] = total[:, core * width : (core + 1) * width].astype(BF16)
+
+
+def rest_body(chips, bys, me, own, other, own_weight, other_weight, *rest):
+    *outs, held, mine, sems, mine_sems = rest
+    weights = (own_weight, other_weight)
+    width = outs[-1].shape[1]
+    copies = fetches(me, chips, bys, weights, held, sems)
+    at = pl.ds(pl.multiple_of(me[0] * width, width), width)
+    for k, weight in enumerate(weights):
+        copies.append(pltpu.make_async_copy(weight.at[:, at], mine.at[k], mine_sems.at[k]))
     for copy in copies:
         copy.start()
-    for copy in copies:
+    for i in range(len(bys)):
+        for copy in copies[2 * i : 2 * i + 2]:
+            copy.wait()
+        total = along(own[...], held[2 * i], 1, 0) + along(other[...], held[2 * i + 1], 1, 0)
+        for core in range(CORES):
+            outs[CORES * i + core][...] = total[:, core * width : (core + 1) * width]
+    for copy in copies[-2:]:
         copy.wait()
-    for i in range(2):
-        total = along(own[...], held[i], 1, 0) + along(other[...], held[2 + i], 1, 0)
-        split(total, outs[i * STREAMS : (i + 1) * STREAMS])
-
-
-def project(normed, part, held, out_weight, other_weight, blocks):
+    outs[-1][...] = along(own[...], mine[0], 1, 0) + along(other[...], mine[1], 1, 0)
+
+
+def project(normed, held, out_weight, other_weight, me, bys):
     devices = lax.axis_size("tensor")
-    far = devices // CORES // 2
+    chips = devices // CORES
+    far = chips // 2
     width = out_weight.shape[1] // devices
     tokens, depth = normed.shape
-    piece = (tokens // STREAMS, width)
+    piece = (tokens, width)
+    work = 2 * tokens * depth * width * CORES
+    own = call(
+        own_body, [VMEM] * 2, [((tokens, CORES * width), F32)] * len(bys), work * len(bys)
+    )(normed, held)
     other = to_other_core(normed)
-    work = 8 * tokens * depth * width
-    parts = call(first_body, [VMEM] * 3, [(piece, BF16)] * (2 * STREAMS), work // 2)(
-        other, part, held
-    )
-    ups, downs = list(parts[:STREAMS]), list(parts[STREAMS:])
+    parts = call(
+        first_body, [VMEM] * (2 + len(bys)), [(piece, BF16)] * (CORES * len(bys)), work * len(bys)
+    )(other, held, *own)
+    ups, downs = list(parts[:CORES]), list(parts[CORES:])
+    left = []
+    for step in range(1, far):
+        left += [far - step] + ([step + 1 - far] if step + 1 < far else [])
+    ups[0], normed, other = lax.optimization_barrier((ups[0], normed, other))
+    parts = call(
+        functools.partial(rest_body, chips, left),
+        [SMEM, VMEM, VMEM, HBM, HBM],
+        [(piece, F32)] * (CORES * len(left) + 1),
+        2 * work * len(left),
+        [pltpu.VMEM((2 * len(left), depth, CORES * width), BF16),
+         pltpu.VMEM((2, depth, width), BF16),
+         pltpu.SemaphoreType.DMA((2 * len(left),)), pltpu.SemaphoreType.DMA((2,))],
+    )(me, normed, other, in_hbm(out_weight), in_hbm(other_weight))
+    part = {(by, core): parts[CORES * i + core] for i, by in enumerate(left) for core in range(CORES)}
     for step in range(1, far + 1):
-        more = step < far
-        if more:
-            ups[0], normed, other = lax.optimization_barrier((ups[0], normed, other))
-            parts = call(
-                functools.partial(product_body, step),
-                [SMEM, VMEM, VMEM, HBM, HBM],
-                [(piece, F32)] * (2 * STREAMS),
-                work,
-                [pltpu.VMEM((4, depth, width), BF16), pltpu.SemaphoreType.DMA((4,))],
-            )(blocks, normed, other, out_weight, other_weight)
-        for i in range(STREAMS):
-            ups[i] = to_chip(ups[i], 1)
-            if more:
-                ups[i] = (ups[i].astype(F32) + parts[i]).astype(BF16)
-                downs[i] = to_chip(downs[i], -1).astype(F32) + parts[STREAMS + i]
-                if step + 1 < far:
-                    downs[i] = downs[i].astype(BF16)
-    return jnp.concatenate(
-        [(downs[i] + ups[i].astype(F32)).astype(BF16) for i in range(STREAMS)], axis=0
-    )
+        for core in range(CORES):
+            ups[core] = to_chip(ups[core], 1, core if step == far else CORES - 1)
+            if step < far:
+                ups[core] = (ups[core].astype(F32) + part[far - step, core]).astype(BF16)
+                by = step + 1 - far
+                downs[core] = to_chip(downs[core], -1, CORES - 1 if by else core)
+                if by:
+                    downs[core] = (downs[core].astype(F32) + part[by, core]).astype(BF16)
+    total = parts[-1]
+    for arrived in downs + ups:
+        total = total + arrived.astype(F32)
+    return total.astype(BF16)
 
 
 def local(
@@ -338,43 +366,45 @@
     head_dim = channels // heads
     state_dim = state_maps.shape[1] // 2
     square = (tokens, channels)
-    devices = lax.axis_size("tensor")
-    chips = devices // CORES
-    far = chips // 2
-    steps = jnp.arange(far)
-    offsets = jnp.stack([far - steps, jnp.where(steps < far - 1, steps + 1 - far, 0)], axis=1)
-    blocks = lax.rem(
-        lax.axis_index("tensor") + CORES * (offsets.reshape(-1) + chips), devices
-    ).astype(jnp.int32)
+    me = lax.axis_index("tensor").reshape(1)
+    position = lax.axis_index("seq").reshape(1)
     ending, step_raw = lax.optimization_barrier((tail_of(mixer_input, state_maps), step_raw))
     leading = shifted(ending, "seq", 1)
-    mix, tail, growth, ends, gated, skip, summed = decay(
+    mix, tail, growth, ends, gated, skip, summed, taps = decay(
         step_raw, decay_log, skip_gain, gate_input, mixer_input, state_maps, conv_input,
         conv_maps,
     )
-    gated, out_weight, blocks = lax.optimization_barrier((gated, out_weight, blocks))
+    gated, out_weight = lax.optimization_barrier((gated, out_weight))
     other_weight = to_other_core(out_weight)
     rows = channels + 16 * pl.cdiv(2 * heads, 16)
     values, projected, sent = call(
         functools.partial(conv_body, heads),
-        [VMEM] * 6,
+        [VMEM] * 5,
         [(square, BF16), (state_maps.shape, BF16), ((rows, state_dim), BF16)],
         10**8,
-    )(summed, leading, conv_input, conv_maps, tail, ends)
-    messages = [shifted(sent, "seq", by) for by in range(1, lax.axis_size("seq"))]
+    )(summed, leading, taps, tail, ends)
+    pieces = lax.axis_size("seq")
+    messages = [
+        lax.ppermute(sent, "seq", [(i, (i + by) % pieces) for i in range(pieces)])
+        for by in range(1, pieces)
+    ]
     (inside,) = call(
         functools.partial(inside_body, heads, head_dim), [VMEM] * 4, [(square, F32)], 10**9
     )(values, projected, mix, skip)
-    width = out_weight.shape[1] // devices
-    normed, part, held = call(
-        functools.partial(norm_body, heads, head_dim),
-        [SMEM, HBM, HBM] + [VMEM] * (5 + len(messages)),
-        [(square, BF16), ((2, tokens, width), F32), ((4, channels, width), BF16)],
+    devices = lax.axis_size("tensor")
+    chips = devices // CORES
+    width = out_weight.shape[1] // chips
+    bys = (chips // 2, 1 - chips // 2)
+    count = CORES * len(bys)
+    normed, held = call(
+        functools.partial(norm_body, heads, head_dim, chips, bys),
+        [SMEM, SMEM, HBM, HBM] + [VMEM] * (5 + len(messages)),
+        [(square, BF16), ((count, channels, width), BF16)],
         10**8,
-        [pltpu.SemaphoreType.DMA((4,))],
-    )(blocks, out_weight, other_weight, projected, inside, growth, gated,
+        [pltpu.SemaphoreType.DMA((count,))],
+    )(me, position, in_hbm(out_weight), in_hbm(other_weight), projected, inside, growth, gated,
       norm_gain.reshape(1, channels), *messages)
-    return project(normed, part, held, out_weight, other_weight, blocks)
+    return project(normed, held, out_weight, other_weight, me, bys)
 
 
 def solution(mesh):

time: 110 us -> 145 us (1.32)
  the two profiles are of different devices: /device:TPU:34 before, /device:TPU:33 now
where the time goes in v3:
time: 145 us; the launch traced here: 144 us
  starting transfers between devices  116 us (80%)
  waiting for transfers between devices  14.1 us (10%)
  Pallas kernels  11.9 us (8%)
  other arithmetic  1.48 us (1%)
    ppermute x30, starting transfers between devices, to_chip(): return lax.ppermute(shard, 'tensor', pairs)  87.7 us
    ppermute x2, starting transfers between devices, to_other_core(): return lax.ppermute(shard, 'tensor', [(i, i ^ 1) for i in range(devices)])  23.3 us
    ppermute x30, waiting for transfers between devices, to_chip(): return lax.ppermute(shard, 'tensor', pairs)  8.68 us
    pallas_call x1, Pallas kernels, project(): call(functools.partial(rest_body, chips, left), [SMEM, VMEM, VMEM, HBM, H...  5.63 us
    ppermute x3, waiting for transfers between devices, local(): lax.ppermute(sent, 'seq', [(i, (i + by) % pieces) for i in range(pieces)])  3.87 us
    ppermute x3, starting transfers between devices, local(): lax.ppermute(sent, 'seq', [(i, (i + by) % pieces) for i in range(pieces)])  3.61 us
  transfers between devices with their start and end apart: 36, of which 7 were waited for; matrix products, arithmetic and copies ran while one was open for 1% of the time, Pallas kernels for 5%

profile of v3, /device:TPU:33, one launch (start us, length us, event | category | flops | bytes accessed | tf_op | source)
XLA Modules:
  0.0 144.1 jit_solution(12015019767307887863)
XLA Ops:
  0.8 2.5 %shard_map.101 = (f32[4,256,256]{2,1,0:T(8,128)S(1)}, f32[256,256]{1,0:T(8,128)S(1)}, f32[256,256]{1,0:T(8,128)S(1)}, f32[4,128]{1,0:T(4,128)S(1)}, f32[256,256]...) custom-call(f32[4,256]{1,0:T(4,128)} %step_hbm, f32[1,4]{1,0:T(1,128)} %bitcast.6, ...), custom_call_target="tpu_custom_call" | custom-call | flops 100000000 | bytes 1048576 | tf_op jit(solution)/shard_map/pallas_call | solution.py:160
  3.3 20.5 %collective-permute-start = (bf16[256,8192]{1,0:T(8,128)(2,1)}, bf16[256,8192]{1,0:T(8,128)(2,1)}, u32[]{:S(2)}, u32[]{:S(2)}) collective-permute-start(bf16[256,8192]{1,0:T(8,128)(2,1)} %own_weight.1), channel_id=1, source_target_pairs={{0,4},{4,0},{8,12},{12,8},{16,20},{20,16},{24,28},{28,24},{32,36},... | collective-permute-start | bytes 12582920 | tf_op jit(solution)/shard_map/ppermute | solution.py:29
  26.5 3.5 %collective-permute-start.3 = (bf16[272,128]{1,0:T(8,128)(2,1)S(1)}, bf16[272,128]{1,0:T(8,128)(2,1)S(1)}, u32[]{:S(2)}, u32[]{:S(2)}) collective-permute-start(bf16[272,128]{1,0:T(8,128)(2,1)S(1)} %get-tuple-element.72), channel_id=1, source_target_pairs={{0,2},{1,3},{2,0},{3,1},{4,6},{5,7},{6,4},{7,5},{8,10},{9,11},{10,... | collective-permute-start | bytes 208904 | tf_op jit(solution)/shard_map/ppermute | solution.py:388
  31.7 2.7 %collective-permute-done.2.rest_0_ = bf16[272,128]{1,0:T(8,128)(2,1)S(1)} collective-permute-done((bf16[272,128]{1,0:T(8,128)(2,1)S(1)}, bf16[272,128]{1,0:T(8,128)(2,1)S(1)}, u32[]{:S(2)}, u32[]{:S(2)}) %collective-permute-start.2) | collective-permute-done | bytes 69664 | tf_op jit(solution)/shard_map/ppermute | solution.py:388
  36.0 2.7 %collective-permute-start.5 = (bf16[256,256]{1,0:T(8,128)(2,1)S(1)}, bf16[256,256]{1,0:T(8,128)(2,1)S(1)}, u32[]{:S(2)}, u32[]{:S(2)}) collective-permute-start(bf16[256,256]{1,0:T(8,128)(2,1)S(1)} %get-tuple-element.78.own), channel_id=1, source_target_pairs={{0,4},{4,0},{8,12},{12,8},{16,20},{20,16},{24,28},{28,24},{32,36},... | collective-permute-start | bytes 393224 | tf_op jit(solution)/shard_map/ppermute | solution.py:29
  40.0 2.0 %collective-permute-start.20 = (bf16[256,256]{1,0:T(8,128)(2,1)S(1)}, bf16[256,256]{1,0:T(8,128)(2,1)S(1)}, u32[]{:S(2)}, u32[]{:S(2)}) collective-permute-start(bf16[256,256]{1,0:T(8,128)(2,1)S(1)} %get-tuple-element.95), channel_id=1, source_target_pairs={{4,12},{12,20},{20,28},{28,36},{36,44},{44,52},{52,60},{60,68},{68... | collective-permute-start | bytes 393224 | tf_op jit(solution)/shard_map/ppermute | solution.py:36
  41.9 7.8 %collective-permute-start.6 = (bf16[256,256]{1,0:T(8,128)(2,1)S(1)}, bf16[256,256]{1,0:T(8,128)(2,1)S(1)}, u32[]{:S(2)}, u32[]{:S(2)}) collective-permute-start(bf16[256,256]{1,0:T(8,128)(2,1)S(1)} %get-tuple-element.81), channel_id=1, source_target_pairs={{4,124},{12,4},{20,12},{28,20},{36,28},{44,36},{52,44},{60,52},{68... | collective-permute-start | bytes 393224 | tf_op jit(solution)/shard_map/ppermute | solution.py:36
  49.8 3.4 %collective-permute-start.13 = (bf16[256,256]{1,0:T(8,128)(2,1)S(1)}, bf16[256,256]{1,0:T(8,128)(2,1)S(1)}, u32[]{:S(2)}, u32[]{:S(2)}) collective-permute-start(bf16[256,256]{1,0:T(8,128)(2,1)S(1)} %get-tuple-element.88), channel_id=1, source_target_pairs={{4,124},{12,4},{20,12},{28,20},{36,28},{44,36},{52,44},{60,52},{68... | collective-permute-start | bytes 393224 | tf_op jit(solution)/shard_map/ppermute | solution.py:36
  53.2 2.0 %collective-permute-start.28 = (bf16[256,256]{1,0:T(8,128)(2,1)S(1)}, bf16[256,256]{1,0:T(8,128)(2,1)S(1)}, u32[]{:S(2)}, u32[]{:S(2)}) collective-permute-start(bf16[256,256]{1,0:T(8,128)(2,1)S(1)} %get-tuple-element.103), channel_id=1, source_target_pairs={{4,12},{12,20},{20,28},{28,36},{36,44},{44,52},{52,60},{60,68},{68... | collective-permute-start | bytes 393224 | tf_op jit(solution)/shard_map/ppermute | solution.py:36
  55.1 5.6 %shard_map.107 = (f32[256,256]{1,0:T(8,128)S(1)}, f32[256,256]{1,0:T(8,128)S(1)}, f32[256,256]{1,0:T(8,128)S(1)}, f32[256,256]{1,0:T(8,128)S(1)}, f32[256,256]{1...) custom-call(s32[1]{0:T(128)} %bitcast.me, ...), custom_call_target="tpu_custom_call" | custom-call | flops 1744830464 | bytes 1048576 | tf_op jit(solution)/shard_map/pallas_call | solution.py:327
  60.8 4.6 %collective-permute-start.7 = (bf16[256,256]{1,0:T(8,128)(2,1)S(1)}, bf16[256,256]{1,0:T(8,128)(2,1)S(1)}, u32[]{:S(2)}, u32[]{:S(2)}) collective-permute-start(bf16[256,256]{1,0:T(8,128)(2,1)S(1)} %add_convert_fusion.26), channel_id=1, source_target_pairs={{4,124},{12,4},{20,12},{28,20},{36,28},{44,36},{52,44},{60,52},{68... | collective-permute-start | bytes 393224 | tf_op jit(solution)/shard_map/ppermute | solution.py:36
  65.5 2.0 %collective-permute-start.14 = (bf16[256,256]{1,0:T(8,128)(2,1)S(1)}, bf16[256,256]{1,0:T(8,128)(2,1)S(1)}, u32[]{:S(2)}, u32[]{:S(2)}) collective-permute-start(bf16[256,256]{1,0:T(8,128)(2,1)S(1)} %add_convert_fusion.20), channel_id=1, source_target_pairs={{4,124},{12,4},{20,12},{28,20},{36,28},{44,36},{52,44},{60,52},{68... | collective-permute-start | bytes 393224 | tf_op jit(solution)/shard_map/ppermute | solution.py:36
  67.5 3.4 %collective-permute-start.21 = (bf16[256,256]{1,0:T(8,128)(2,1)S(1)}, bf16[256,256]{1,0:T(8,128)(2,1)S(1)}, u32[]{:S(2)}, u32[]{:S(2)}) collective-permute-start(bf16[256,256]{1,0:T(8,128)(2,1)S(1)} %add_convert_fusion.14), channel_id=1, source_target_pairs={{4,12},{12,20},{20,28},{28,36},{36,44},{44,52},{52,60},{60,68},{68... | collective-permute-start | bytes 393224 | tf_op jit(solution)/shard_map/ppermute | solution.py:36
  70.9 2.0 %collective-permute-start.29 = (bf16[256,256]{1,0:T(8,128)(2,1)S(1)}, bf16[256,256]{1,0:T(8,128)(2,1)S(1)}, u32[]{:S(2)}, u32[]{:S(2)}) collective-permute-start(bf16[256,256]{1,0:T(8,128)(2,1)S(1)} %add_convert_fusion.7), channel_id=1, source_target_pairs={{4,12},{12,20},{20,28},{28,36},{36,44},{44,52},{52,60},{60,68},{68... | collective-permute-start | bytes 393224 | tf_op jit(solution)/shard_map/ppermute | solution.py:36
  72.9 4.6 %collective-permute-start.8 = (bf16[256,256]{1,0:T(8,128)(2,1)S(1)}, bf16[256,256]{1,0:T(8,128)(2,1)S(1)}, u32[]{:S(2)}, u32[]{:S(2)}) collective-permute-start(bf16[256,256]{1,0:T(8,128)(2,1)S(1)} %add_convert_fusion.25), channel_id=1, source_target_pairs={{4,124},{12,4},{20,12},{28,20},{36,28},{44,36},{52,44},{60,52},{68... | collective-permute-start | bytes 393224 | tf_op jit(solution)/shard_map/ppermute | solution.py:36
  77.6 2.0 %collective-permute-start.15 = (bf16[256,256]{1,0:T(8,128)(2,1)S(1)}, bf16[256,256]{1,0:T(8,128)(2,1)S(1)}, u32[]{:S(2)}, u32[]{:S(2)}) collective-permute-start(bf16[256,256]{1,0:T(8,128)(2,1)S(1)} %add_convert_fusion.19), channel_id=1, source_target_pairs={{4,124},{12,4},{20,12},{28,20},{36,28},{44,36},{52,44},{60,52},{68... | collective-permute-start | bytes 393224 | tf_op jit(solution)/shard_map/ppermute | solution.py:36
  79.6 3.4 %collective-permute-start.22 = (bf16[256,256]{1,0:T(8,128)(2,1)S(1)}, bf16[256,256]{1,0:T(8,128)(2,1)S(1)}, u32[]{:S(2)}, u32[]{:S(2)}) collective-permute-start(bf16[256,256]{1,0:T(8,128)(2,1)S(1)} %add_convert_fusion.13), channel_id=1, source_target_pairs={{4,12},{12,20},{20,28},{28,36},{36,44},{44,52},{52,60},{60,68},{68... | collective-permute-start | bytes 393224 | tf_op jit(solution)/shard_map/ppermute | solution.py:36
  85.0 4.6 %collective-permute-start.9 = (bf16[256,256]{1,0:T(8,128)(2,1)S(1)}, bf16[256,256]{1,0:T(8,128)(2,1)S(1)}, u32[]{:S(2)}, u32[]{:S(2)}) collective-permute-start(bf16[256,256]{1,0:T(8,128)(2,1)S(1)} %add_convert_fusion.24), channel_id=1, source_target_pairs={{4,124},{12,4},{20,12},{28,20},{36,28},{44,36},{52,44},{60,52},{68... | collective-permute-start | bytes 393224 | tf_op jit(solution)/shard_map/ppermute | solution.py:36
  89.7 2.0 %collective-permute-start.16 = (bf16[256,256]{1,0:T(8,128)(2,1)S(1)}, bf16[256,256]{1,0:T(8,128)(2,1)S(1)}, u32[]{:S(2)}, u32[]{:S(2)}) collective-permute-start(bf16[256,256]{1,0:T(8,128)(2,1)S(1)} %add_convert_fusion.18), channel_id=1, source_target_pairs={{4,124},{12,4},{20,12},{28,20},{36,28},{44,36},{52,44},{60,52},{68... | collective-permute-start | bytes 393224 | tf_op jit(solution)/shard_map/ppermute | solution.py:36
  91.7 3.4 %collective-permute-start.23 = (bf16[256,256]{1,0:T(8,128)(2,1)S(1)}, bf16[256,256]{1,0:T(8,128)(2,1)S(1)}, u32[]{:S(2)}, u32[]{:S(2)}) collective-permute-start(bf16[256,256]{1,0:T(8,128)(2,1)S(1)} %add_convert_fusion.12), channel_id=1, source_target_pairs={{4,12},{12,20},{20,28},{28,36},{36,44},{44,52},{52,60},{60,68},{68... | collective-permute-start | bytes 393224 | tf_op jit(solution)/shard_map/ppermute | solution.py:36
  97.2 4.6 %collective-permute-start.10 = (bf16[256,256]{1,0:T(8,128)(2,1)S(1)}, bf16[256,256]{1,0:T(8,128)(2,1)S(1)}, u32[]{:S(2)}, u32[]{:S(2)}) collective-permute-start(bf16[256,256]{1,0:T(8,128)(2,1)S(1)} %add_convert_fusion.23), channel_id=1, source_target_pairs={{4,124},{12,4},{20,12},{28,20},{36,28},{44,36},{52,44},{60,52},{68... | collective-permute-start | bytes 393224 | tf_op jit(solution)/shard_map/ppermute | solution.py:36
  101.8 2.0 %collective-permute-start.17 = (bf16[256,256]{1,0:T(8,128)(2,1)S(1)}, bf16[256,256]{1,0:T(8,128)(2,1)S(1)}, u32[]{:S(2)}, u32[]{:S(2)}) collective-permute-start(bf16[256,256]{1,0:T(8,128)(2,1)S(1)} %add_convert_fusion.17), channel_id=1, source_target_pairs={{4,124},{12,4},{20,12},{28,20},{36,28},{44,36},{52,44},{60,52},{68... | collective-permute-start | bytes 393224 | tf_op jit(solution)/shard_map/ppermute | solution.py:36
  103.8 3.4 %collective-permute-start.24 = (bf16[256,256]{1,0:T(8,128)(2,1)S(1)}, bf16[256,256]{1,0:T(8,128)(2,1)S(1)}, u32[]{:S(2)}, u32[]{:S(2)}) collective-permute-start(bf16[256,256]{1,0:T(8,128)(2,1)S(1)} %add_convert_fusion.11), channel_id=1, source_target_pairs={{4,12},{12,20},{20,28},{28,36},{36,44},{44,52},{52,60},{60,68},{68... | collective-permute-start | bytes 393224 | tf_op jit(solution)/shard_map/ppermute | solution.py:36
  109.3 4.6 %collective-permute-start.11 = (bf16[256,256]{1,0:T(8,128)(2,1)S(1)}, bf16[256,256]{1,0:T(8,128)(2,1)S(1)}, u32[]{:S(2)}, u32[]{:S(2)}) collective-permute-start(bf16[256,256]{1,0:T(8,128)(2,1)S(1)} %add_convert_fusion.22), channel_id=1, source_target_pairs={{4,124},{12,4},{20,12},{28,20},{36,28},{44,36},{52,44},{60,52},{68... | collective-permute-start | bytes 393224 | tf_op jit(solution)/shard_map/ppermute | solution.py:36
  113.9 2.0 %collective-permute-start.18 = (bf16[256,256]{1,0:T(8,128)(2,1)S(1)}, bf16[256,256]{1,0:T(8,128)(2,1)S(1)}, u32[]{:S(2)}, u32[]{:S(2)}) collective-permute-start(bf16[256,256]{1,0:T(8,128)(2,1)S(1)} %add_convert_fusion.16), channel_id=1, source_target_pairs={{4,124},{12,4},{20,12},{28,20},{36,28},{44,36},{52,44},{60,52},{68... | collective-permute-start | bytes 393224 | tf_op jit(solution)/shard_map/ppermute | solution.py:36
  115.9 3.4 %collective-permute-start.25 = (bf16[256,256]{1,0:T(8,128)(2,1)S(1)}, bf16[256,256]{1,0:T(8,128)(2,1)S(1)}, u32[]{:S(2)}, u32[]{:S(2)}) collective-permute-start(bf16[256,256]{1,0:T(8,128)(2,1)S(1)} %add_convert_fusion.10), channel_id=1, source_target_pairs={{4,12},{12,20},{20,28},{28,36},{36,44},{44,52},{52,60},{60,68},{68... | collective-permute-start | bytes 393224 | tf_op jit(solution)/shard_map/ppermute | solution.py:36
  119.4 2.0 %collective-permute-start.33 = (bf16[256,256]{1,0:T(8,128)(2,1)S(1)}, bf16[256,256]{1,0:T(8,128)(2,1)S(1)}, u32[]{:S(2)}, u32[]{:S(2)}) collective-permute-start(bf16[256,256]{1,0:T(8,128)(2,1)S(1)} %add_convert_fusion.3), channel_id=1, source_target_pairs={{4,12},{12,20},{20,28},{28,36},{36,44},{44,52},{52,60},{60,68},{68... | collective-permute-start | bytes 393224 | tf_op jit(solution)/shard_map/ppermute | solution.py:36
  122.8 4.6 %collective-permute-start.19 = (bf16[256,256]{1,0:T(8,128)(2,1)S(1)}, bf16[256,256]{1,0:T(8,128)(2,1)S(1)}, u32[]{:S(2)}, u32[]{:S(2)}) collective-permute-start(bf16[256,256]{1,0:T(8,128)(2,1)S(1)} %add_convert_fusion.15), channel_id=1, source_target_pairs={{4,124},{12,4},{20,12},{28,20},{36,28},{44,36},{52,44},{60,52},{68... | collective-permute-start | bytes 393224 | tf_op jit(solution)/shard_map/ppermute | solution.py:36
  129.4 2.0 %collective-permute-start.34 = (bf16[256,256]{1,0:T(8,128)(2,1)S(1)}, bf16[256,256]{1,0:T(8,128)(2,1)S(1)}, u32[]{:S(2)}, u32[]{:S(2)}) collective-permute-start(bf16[256,256]{1,0:T(8,128)(2,1)S(1)} %add_convert_fusion.2), channel_id=1, source_target_pairs={{4,12},{12,20},{20,28},{28,36},{36,44},{44,52},{52,60},{60,68},{68... | collective-permute-start | bytes 393224 | tf_op jit(solution)/shard_map/ppermute | solution.py:36
  131.4 3.0 %collective-permute-done.26 = bf16[256,256]{1,0:T(8,128)(2,1)S(1)} collective-permute-done((bf16[256,256]{1,0:T(8,128)(2,1)S(1)}, bf16[256,256]{1,0:T(8,128)(2,1)S(1)}, u32[]{:S(2)}, u32[]{:S(2)}) %collective-permute-start.26) | collective-permute-done | bytes 131104 | tf_op jit(solution)/shard_map/ppermute | solution.py:36
  136.4 2.0 %collective-permute-start.35 = (bf16[256,256]{1,0:T(8,128)(2,1)S(1)}, bf16[256,256]{1,0:T(8,128)(2,1)S(1)}, u32[]{:S(2)}, u32[]{:S(2)}) collective-permute-start(bf16[256,256]{1,0:T(8,128)(2,1)S(1)} %add_convert_fusion.1), channel_id=1, source_target_pairs={{4,12},{12,20},{20,28},{28,36},{36,44},{44,52},{52,60},{60,68},{68... | collective-permute-start | bytes 393224 | tf_op jit(solution)/shard_map/ppermute | solution.py:36
  138.4 5.0 %collective-permute-done.35 = bf16[256,256]{1,0:T(8,128)(2,1)S(1)} collective-permute-done((bf16[256,256]{1,0:T(8,128)(2,1)S(1)}, bf16[256,256]{1,0:T(8,128)(2,1)S(1)}, u32[]{:S(2)}, u32[]{:S(2)}) %collective-permute-start.35) | collective-permute-done | bytes 131104 | tf_op jit(solution)/shard_map/ppermute | solution.py:36
  (77 shorter events, 20.6 us)
Async XLA Ops:
  3.3 31.1 %collective-permute-start = (bf16[256,8192]{1,0:T(8,128)(2,1)}, bf16[256,8192]{1,0:T(8,128)(2,1)}, u32[]{:S(2)}, u32[]{:S(2)}) collective-permute-start(bf16[256,8192]{1,0:T(8,128)(2,1)} %own_weight.1), channel_id=1, source_target_pairs={{0,4},{4,0},{8,12},{12,8},{16,20},{20,16},{24,28},{28,24},{32,36},... | collective-permute-start | bytes 12582920 | tf_op jit(solution)/shard_map/ppermute | solution.py:29
  26.5 5.2 %collective-permute-start.3 = (bf16[272,128]{1,0:T(8,128)(2,1)S(1)}, bf16[272,128]{1,0:T(8,128)(2,1)S(1)}, u32[]{:S(2)}, u32[]{:S(2)}) collective-permute-start(bf16[272,128]{1,0:T(8,128)(2,1)S(1)} %get-tuple-element.72), channel_id=1, source_target_pairs={{0,2},{1,3},{2,0},{3,1},{4,6},{5,7},{6,4},{7,5},{8,10},{9,11},{10,... | collective-permute-start | bytes 208904 | tf_op jit(solution)/shard_map/ppermute | solution.py:388
  30.0 4.4 %collective-permute-start.2 = (bf16[272,128]{1,0:T(8,128)(2,1)S(1)}, bf16[272,128]{1,0:T(8,128)(2,1)S(1)}, u32[]{:S(2)}, u32[]{:S(2)}) collective-permute-start(bf16[272,128]{1,0:T(8,128)(2,1)S(1)} %get-tuple-element.72), channel_id=1, source_target_pairs={{0,1},{1,2},{2,3},{3,0},{4,5},{5,6},{6,7},{7,4},{8,9},{9,10},{10,1... | collective-permute-start | bytes 208904 | tf_op jit(solution)/shard_map/ppermute | solution.py:388
  40.0 27.4 %collective-permute-start.20 = (bf16[256,256]{1,0:T(8,128)(2,1)S(1)}, bf16[256,256]{1,0:T(8,128)(2,1)S(1)}, u32[]{:S(2)}, u32[]{:S(2)}) collective-permute-start(bf16[256,256]{1,0:T(8,128)(2,1)S(1)} %get-tuple-element.95), channel_id=1, source_target_pairs={{4,12},{12,20},{20,28},{28,36},{36,44},{44,52},{52,60},{60,68},{68... | collective-permute-start | bytes 393224 | tf_op jit(solution)/shard_map/ppermute | solution.py:36
  41.9 18.8 %collective-permute-start.6 = (bf16[256,256]{1,0:T(8,128)(2,1)S(1)}, bf16[256,256]{1,0:T(8,128)(2,1)S(1)}, u32[]{:S(2)}, u32[]{:S(2)}) collective-permute-start(bf16[256,256]{1,0:T(8,128)(2,1)S(1)} %get-tuple-element.81), channel_id=1, source_target_pairs={{4,124},{12,4},{20,12},{28,20},{36,28},{44,36},{52,44},{60,52},{68... | collective-permute-start | bytes 393224 | tf_op jit(solution)/shard_map/ppermute | solution.py:36
  49.8 15.7 %collective-permute-start.13 = (bf16[256,256]{1,0:T(8,128)(2,1)S(1)}, bf16[256,256]{1,0:T(8,128)(2,1)S(1)}, u32[]{:S(2)}, u32[]{:S(2)}) collective-permute-start(bf16[256,256]{1,0:T(8,128)(2,1)S(1)} %get-tuple-element.88), channel_id=1, source_target_pairs={{4,124},{12,4},{20,12},{28,20},{36,28},{44,36},{52,44},{60,52},{68... | collective-permute-start | bytes 393224 | tf_op jit(solution)/shard_map/ppermute | solution.py:36
  53.2 17.7 %collective-permute-start.28 = (bf16[256,256]{1,0:T(8,128)(2,1)S(1)}, bf16[256,256]{1,0:T(8,128)(2,1)S(1)}, u32[]{:S(2)}, u32[]{:S(2)}) collective-permute-start(bf16[256,256]{1,0:T(8,128)(2,1)S(1)} %get-tuple-element.103), channel_id=1, source_target_pairs={{4,12},{12,20},{20,28},{28,36},{36,44},{44,52},{52,60},{60,68},{68... | collective-permute-start | bytes 393224 | tf_op jit(solution)/shard_map/ppermute | solution.py:36
  60.8 12.1 %collective-permute-start.7 = (bf16[256,256]{1,0:T(8,128)(2,1)S(1)}, bf16[256,256]{1,0:T(8,128)(2,1)S(1)}, u32[]{:S(2)}, u32[]{:S(2)}) collective-permute-start(bf16[256,256]{1,0:T(8,128)(2,1)S(1)} %add_convert_fusion.26), channel_id=1, source_target_pairs={{4,124},{12,4},{20,12},{28,20},{36,28},{44,36},{52,44},{60,52},{68... | collective-permute-start | bytes 393224 | tf_op jit(solution)/shard_map/ppermute | solution.py:36
  65.5 12.1 %collective-permute-start.14 = (bf16[256,256]{1,0:T(8,128)(2,1)S(1)}, bf16[256,256]{1,0:T(8,128)(2,1)S(1)}, u32[]{:S(2)}, u32[]{:S(2)}) collective-permute-start(bf16[256,256]{1,0:T(8,128)(2,1)S(1)} %add_convert_fusion.20), channel_id=1, source_target_pairs={{4,124},{12,4},{20,12},{28,20},{36,28},{44,36},{52,44},{60,52},{68... | collective-permute-start | bytes 393224 | tf_op jit(solution)/shard_map/ppermute | solution.py:36
  67.5 12.1 %collective-permute-start.21 = (bf16[256,256]{1,0:T(8,128)(2,1)S(1)}, bf16[256,256]{1,0:T(8,128)(2,1)S(1)}, u32[]{:S(2)}, u32[]{:S(2)}) collective-permute-start(bf16[256,256]{1,0:T(8,128)(2,1)S(1)} %add_convert_fusion.14), channel_id=1, source_target_pairs={{4,12},{12,20},{20,28},{28,36},{36,44},{44,52},{52,60},{60,68},{68... | collective-permute-start | bytes 393224 | tf_op jit(solution)/shard_map/ppermute | solution.py:36
  70.9 12.1 %collective-permute-start.29 = (bf16[256,256]{1,0:T(8,128)(2,1)S(1)}, bf16[256,256]{1,0:T(8,128)(2,1)S(1)}, u32[]{:S(2)}, u32[]{:S(2)}) collective-permute-start(bf16[256,256]{1,0:T(8,128)(2,1)S(1)} %add_convert_fusion.7), channel_id=1, source_target_pairs={{4,12},{12,20},{20,28},{28,36},{36,44},{44,52},{52,60},{60,68},{68... | collective-permute-start | bytes 393224 | tf_op jit(solution)/shard_map/ppermute | solution.py:36
  72.9 12.1 %collective-permute-start.8 = (bf16[256,256]{1,0:T(8,128)(2,1)S(1)}, bf16[256,256]{1,0:T(8,128)(2,1)S(1)}, u32[]{:S(2)}, u32[]{:S(2)}) collective-permute-start(bf16[256,256]{1,0:T(8,128)(2,1)S(1)} %add_convert_fusion.25), channel_id=1, source_target_pairs={{4,124},{12,4},{20,12},{28,20},{36,28},{44,36},{52,44},{60,52},{68... | collective-permute-start | bytes 393224 | tf_op jit(solution)/shard_map/ppermute | solution.py:36
  77.6 12.1 %collective-permute-start.15 = (bf16[256,256]{1,0:T(8,128)(2,1)S(1)}, bf16[256,256]{1,0:T(8,128)(2,1)S(1)}, u32[]{:S(2)}, u32[]{:S(2)}) collective-permute-start(bf16[256,256]{1,0:T(8,128)(2,1)S(1)} %add_convert_fusion.19), channel_id=1, source_target_pairs={{4,124},{12,4},{20,12},{28,20},{36,28},{44,36},{52,44},{60,52},{68... | collective-permute-start | bytes 393224 | tf_op jit(solution)/shard_map/ppermute | solution.py:36
  79.6 12.1 %collective-permute-start.22 = (bf16[256,256]{1,0:T(8,128)(2,1)S(1)}, bf16[256,256]{1,0:T(8,128)(2,1)S(1)}, u32[]{:S(2)}, u32[]{:S(2)}) collective-permute-start(bf16[256,256]{1,0:T(8,128)(2,1)S(1)} %add_convert_fusion.13), channel_id=1, source_target_pairs={{4,12},{12,20},{20,28},{28,36},{36,44},{44,52},{52,60},{60,68},{68... | collective-permute-start | bytes 393224 | tf_op jit(solution)/shard_map/ppermute | solution.py:36
  83.0 12.1 %collective-permute-start.30 = (bf16[256,256]{1,0:T(8,128)(2,1)S(1)}, bf16[256,256]{1,0:T(8,128)(2,1)S(1)}, u32[]{:S(2)}, u32[]{:S(2)}) collective-permute-start(bf16[256,256]{1,0:T(8,128)(2,1)S(1)} %add_convert_fusion.6), channel_id=1, source_target_pairs={{4,12},{12,20},{20,28},{28,36},{36,44},{44,52},{52,60},{60,68},{68... | collective-permute-start | bytes 393224 | tf_op jit(solution)/shard_map/ppermute | solution.py:36
  85.0 12.1 %collective-permute-start.9 = (bf16[256,256]{1,0:T(8,128)(2,1)S(1)}, bf16[256,256]{1,0:T(8,128)(2,1)S(1)}, u32[]{:S(2)}, u32[]{:S(2)}) collective-permute-start(bf16[256,256]{1,0:T(8,128)(2,1)S(1)} %add_convert_fusion.24), channel_id=1, source_target_pairs={{4,124},{12,4},{20,12},{28,20},{36,28},{44,36},{52,44},{60,52},{68... | collective-permute-start | bytes 393224 | tf_op jit(solution)/shard_map/ppermute | solution.py:36
  89.7 12.1 %collective-permute-start.16 = (bf16[256,256]{1,0:T(8,128)(2,1)S(1)}, bf16[256,256]{1,0:T(8,128)(2,1)S(1)}, u32[]{:S(2)}, u32[]{:S(2)}) collective-permute-start(bf16[256,256]{1,0:T(8,128)(2,1)S(1)} %add_convert_fusion.18), channel_id=1, source_target_pairs={{4,124},{12,4},{20,12},{28,20},{36,28},{44,36},{52,44},{60,52},{68... | collective-permute-start | bytes 393224 | tf_op jit(solution)/shard_map/ppermute | solution.py:36
  91.7 12.1 %collective-permute-start.23 = (bf16[256,256]{1,0:T(8,128)(2,1)S(1)}, bf16[256,256]{1,0:T(8,128)(2,1)S(1)}, u32[]{:S(2)}, u32[]{:S(2)}) collective-permute-start(bf16[256,256]{1,0:T(8,128)(2,1)S(1)} %add_convert_fusion.12), channel_id=1, source_target_pairs={{4,12},{12,20},{20,28},{28,36},{36,44},{44,52},{52,60},{60,68},{68... | collective-permute-start | bytes 393224 | tf_op jit(solution)/shard_map/ppermute | solution.py:36
  95.2 12.1 %collective-permute-start.31 = (bf16[256,256]{1,0:T(8,128)(2,1)S(1)}, bf16[256,256]{1,0:T(8,128)(2,1)S(1)}, u32[]{:S(2)}, u32[]{:S(2)}) collective-permute-start(bf16[256,256]{1,0:T(8,128)(2,1)S(1)} %add_convert_fusion.5), channel_id=1, source_target_pairs={{4,12},{12,20},{20,28},{28,36},{36,44},{44,52},{52,60},{60,68},{68... | collective-permute-start | bytes 393224 | tf_op jit(solution)/shard_map/ppermute | solution.py:36
  97.2 12.1 %collective-permute-start.10 = (bf16[256,256]{1,0:T(8,128)(2,1)S(1)}, bf16[256,256]{1,0:T(8,128)(2,1)S(1)}, u32[]{:S(2)}, u32[]{:S(2)}) collective-permute-start(bf16[256,256]{1,0:T(8,128)(2,1)S(1)} %add_convert_fusion.23), channel_id=1, source_target_pairs={{4,124},{12,4},{20,12},{28,20},{36,28},{44,36},{52,44},{60,52},{68... | collective-permute-start | bytes 393224 | tf_op jit(solution)/shard_map/ppermute | solution.py:36
  101.8 12.1 %collective-permute-start.17 = (bf16[256,256]{1,0:T(8,128)(2,1)S(1)}, bf16[256,256]{1,0:T(8,128)(2,1)S(1)}, u32[]{:S(2)}, u32[]{:S(2)}) collective-permute-start(bf16[256,256]{1,0:T(8,128)(2,1)S(1)} %add_convert_fusion.17), channel_id=1, source_target_pairs={{4,124},{12,4},{20,12},{28,20},{36,28},{44,36},{52,44},{60,52},{68... | collective-permute-start | bytes 393224 | tf_op jit(solution)/shard_map/ppermute | solution.py:36
  103.8 12.1 %collective-permute-start.24 = (bf16[256,256]{1,0:T(8,128)(2,1)S(1)}, bf16[256,256]{1,0:T(8,128)(2,1)S(1)}, u32[]{:S(2)}, u32[]{:S(2)}) collective-permute-start(bf16[256,256]{1,0:T(8,128)(2,1)S(1)} %add_convert_fusion.11), channel_id=1, source_target_pairs={{4,12},{12,20},{20,28},{28,36},{36,44},{44,52},{52,60},{60,68},{68... | collective-permute-start | bytes 393224 | tf_op jit(solution)/shard_map/ppermute | solution.py:36
  107.3 12.1 %collective-permute-start.32 = (bf16[256,256]{1,0:T(8,128)(2,1)S(1)}, bf16[256,256]{1,0:T(8,128)(2,1)S(1)}, u32[]{:S(2)}, u32[]{:S(2)}) collective-permute-start(bf16[256,256]{1,0:T(8,128)(2,1)S(1)} %add_convert_fusion.4), channel_id=1, source_target_pairs={{4,12},{12,20},{20,28},{28,36},{36,44},{44,52},{52,60},{60,68},{68... | collective-permute-start | bytes 393224 | tf_op jit(solution)/shard_map/ppermute | solution.py:36
  109.3 12.1 %collective-permute-start.11 = (bf16[256,256]{1,0:T(8,128)(2,1)S(1)}, bf16[256,256]{1,0:T(8,128)(2,1)S(1)}, u32[]{:S(2)}, u32[]{:S(2)}) collective-permute-start(bf16[256,256]{1,0:T(8,128)(2,1)S(1)} %add_convert_fusion.22), channel_id=1, source_target_pairs={{4,124},{12,4},{20,12},{28,20},{36,28},{44,36},{52,44},{60,52},{68... | collective-permute-start | bytes 393224 | tf_op jit(solution)/shard_map/ppermute | solution.py:36
  113.9 8.8 %collective-permute-start.18 = (bf16[256,256]{1,0:T(8,128)(2,1)S(1)}, bf16[256,256]{1,0:T(8,128)(2,1)S(1)}, u32[]{:S(2)}, u32[]{:S(2)}) collective-permute-start(bf16[256,256]{1,0:T(8,128)(2,1)S(1)} %add_convert_fusion.16), channel_id=1, source_target_pairs={{4,124},{12,4},{20,12},{28,20},{36,28},{44,36},{52,44},{60,52},{68... | collective-permute-start | bytes 393224 | tf_op jit(solution)/shard_map/ppermute | solution.py:36
  115.9 11.4 %collective-permute-start.25 = (bf16[256,256]{1,0:T(8,128)(2,1)S(1)}, bf16[256,256]{1,0:T(8,128)(2,1)S(1)}, u32[]{:S(2)}, u32[]{:S(2)}) collective-permute-start(bf16[256,256]{1,0:T(8,128)(2,1)S(1)} %add_convert_fusion.10), channel_id=1, source_target_pairs={{4,12},{12,20},{20,28},{28,36},{36,44},{44,52},{52,60},{60,68},{68... | collective-permute-start | bytes 393224 | tf_op jit(solution)/shard_map/ppermute | solution.py:36
  119.4 10.0 %collective-permute-start.33 = (bf16[256,256]{1,0:T(8,128)(2,1)S(1)}, bf16[256,256]{1,0:T(8,128)(2,1)S(1)}, u32[]{:S(2)}, u32[]{:S(2)}) collective-permute-start(bf16[256,256]{1,0:T(8,128)(2,1)S(1)} %add_convert_fusion.3), channel_id=1, source_target_pairs={{4,12},{12,20},{20,28},{28,36},{36,44},{44,52},{52,60},{60,68},{68... | collective-permute-start | bytes 393224 | tf_op jit(solution)/shard_map/ppermute | solution.py:36
  121.4 17.0 %collective-permute-start.12 = (bf16[256,256]{1,0:T(8,128)(2,1)S(1)}, bf16[256,256]{1,0:T(8,128)(2,1)S(1)}, u32[]{:S(2)}, u32[]{:S(2)}) collective-permute-start(bf16[256,256]{1,0:T(8,128)(2,1)S(1)} %add_convert_fusion.21), channel_id=1, source_target_pairs={{4,120},{12,0},{20,8},{28,16},{36,24},{44,32},{52,40},{60,48},{68,... | collective-permute-start | bytes 393224 | tf_op jit(solution)/shard_map/ppermute | solution.py:36
  122.8 15.6 %collective-permute-start.19 = (bf16[256,256]{1,0:T(8,128)(2,1)S(1)}, bf16[256,256]{1,0:T(8,128)(2,1)S(1)}, u32[]{:S(2)}, u32[]{:S(2)}) collective-permute-start(bf16[256,256]{1,0:T(8,128)(2,1)S(1)} %add_convert_fusion.15), channel_id=1, source_target_pairs={{4,124},{12,4},{20,12},{28,20},{36,28},{44,36},{52,44},{60,52},{68... | collective-permute-start | bytes 393224 | tf_op jit(solution)/shard_map/ppermute | solution.py:36
  127.4 7.0 %collective-permute-start.26 = (bf16[256,256]{1,0:T(8,128)(2,1)S(1)}, bf16[256,256]{1,0:T(8,128)(2,1)S(1)}, u32[]{:S(2)}, u32[]{:S(2)}) collective-permute-start(bf16[256,256]{1,0:T(8,128)(2,1)S(1)} %add_convert_fusion.9), channel_id=1, source_target_pairs={{4,12},{12,20},{20,28},{28,36},{36,44},{44,52},{52,60},{60,68},{68... | collective-permute-start | bytes 393224 | tf_op jit(solution)/shard_map/ppermute | solution.py:36
  129.4 7.0 %collective-permute-start.34 = (bf16[256,256]{1,0:T(8,128)(2,1)S(1)}, bf16[256,256]{1,0:T(8,128)(2,1)S(1)}, u32[]{:S(2)}, u32[]{:S(2)}) collective-permute-start(bf16[256,256]{1,0:T(8,128)(2,1)S(1)} %add_convert_fusion.2), channel_id=1, source_target_pairs={{4,12},{12,20},{20,28},{28,36},{36,44},{44,52},{52,60},{60,68},{68... | collective-permute-start | bytes 393224 | tf_op jit(solution)/shard_map/ppermute | solution.py:36
  136.4 7.0 %collective-permute-start.35 = (bf16[256,256]{1,0:T(8,128)(2,1)S(1)}, bf16[256,256]{1,0:T(8,128)(2,1)S(1)}, u32[]{:S(2)}, u32[]{:S(2)}) collective-permute-start(bf16[256,256]{1,0:T(8,128)(2,1)S(1)} %add_convert_fusion.1), channel_id=1, source_target_pairs={{4,12},{12,20},{20,28},{28,36},{36,44},{44,52},{52,60},{60,68},{68... | collective-permute-start | bytes 393224 | tf_op jit(solution)/shard_map/ppermute | solution.py:36
  (5 other events, 48.4 us)

commit v4 on v3

--- a/solution.py
+++ b/solution.py
@@ -10,6 +10,7 @@
 
 CORES = 2
 LEAD = 16
+STREAMS = 2
 F32 = jnp.float32
 BF16 = jnp.bfloat16
 PRECISE = lax.Precision.HIGHEST
@@ -29,11 +30,11 @@
     return lax.ppermute(shard, "tensor", [(i, i ^ 1) for i in range(devices)])
 
 
-def to_chip(shard, by, core):
+def to_chip(shard, by):
     devices = lax.axis_size("tensor")
-    first = CORES - 1
-    pairs = [(i, (i - first + CORES * by + core) % devices) for i in range(first, devices, CORES)]
-    return lax.ppermute(shard, "tensor", pairs)
+    return lax.ppermute(
+        shard, "tensor", [(i, (i + CORES * by) % devices) for i in range(devices)]
+    )
 
 
 def in_hbm(x):
@@ -95,45 +96,43 @@
     )(in_hbm(mixer_input), in_hbm(state_maps))[0]
 
 
+def spread_over(vectors, tokens):
+    heads = vectors.shape[1]
+    row = lax.broadcasted_iota(jnp.int32, (heads, tokens), 0)
+    spread = jnp.broadcast_to(vectors[:, 0:1], (heads, tokens))
+    for head in range(1, heads):
+        spread = jnp.where(row == head, vectors[:, head : head + 1], spread)
+    return spread
+
+
 def decay_body(
-    heads, head_dim, step_hbm, decay_hbm, skip_hbm, gate_hbm, mixer_hbm, maps_hbm, taps_hbm,
-    map_taps_hbm, mix, tail, growth, ends, gated, skip, summed, wide_taps,
-    raw, logs, gains, gate, mixer, maps, taps, map_taps, padded, sems
+    head_dim, step_hbm, decay_hbm, taps_hbm, map_taps_hbm, mixer_hbm, maps_hbm,
+    tail, ends, summed, wide_taps, across, down, step,
+    raw, logs, taps, map_taps, mixer, maps, padded, sems
 ):
-    pairs = [(decay_hbm, logs), (step_hbm, raw), (skip_hbm, gains), (gate_hbm, gate),
-             (taps_hbm, taps), (map_taps_hbm, map_taps), (mixer_hbm, mixer), (maps_hbm, maps)]
+    pairs = [(decay_hbm, logs), (step_hbm, raw), (taps_hbm, taps), (map_taps_hbm, map_taps),
+             (mixer_hbm, mixer), (maps_hbm, maps)]
     copies = [pltpu.make_async_copy(a, b, sems.at[i]) for i, (a, b) in enumerate(pairs)]
     for copy in copies:
         copy.start()
-    tokens = raw.shape[1]
+    heads, tokens = raw.shape
     width = heads * head_dim
-    row = lax.broadcasted_iota(jnp.int32, (heads, tokens), 0)
     to = lax.broadcasted_iota(jnp.int32, (tokens, tokens), 0)
     since = lax.broadcasted_iota(jnp.int32, (tokens, tokens), 1)
-    causal = to >= since
-    ones = jnp.where(causal, 1.0, 0.0).astype(F32)
+    ones = jnp.where(to >= since, 1.0, 0.0).astype(F32)
     same = jnp.where(to == since, 1.0, 0.0).astype(F32)
-    for copy in copies[:3]:
+    for copy in copies[:2]:
         copy.wait()
-    step = jnp.maximum(raw[...], 0.0) + jnp.log1p(jnp.exp(-jnp.abs(raw[...])))
-    rates = jnp.broadcast_to(logs[:, 0:1], (heads, tokens))
-    for head in range(1, heads):
-        rates = jnp.where(row == head, logs[:, head : head + 1], rates)
-    change = -jnp.exp(rates) * step
-    across = along(change, ones, 1, 1, PRECISE)
-    down = along(ones, change, 1, 1, PRECISE)
-    step_down = along(same, step, 1, 1, PRECISE)
-    for head in range(heads):
-        spacing = jnp.where(causal, down[:, head : head + 1] - across[head : head + 1, :], -1e30)
-        mix[head] = jnp.exp(spacing) * step[head : head + 1, :]
+    step[...] = jnp.maximum(raw[...], 0.0) + jnp.log1p(jnp.exp(-jnp.abs(raw[...])))
+    change = -jnp.exp(spread_over(logs[...], tokens)) * step[...]
+    across[...] = along(change, ones, 1, 1, PRECISE)
+    down[...] = along(ones, change, 1, 1, PRECISE)
+    step_down = along(same, step[...], 1, 1, PRECISE)
     last = down[tokens - 1 : tokens, :]
-    tail[...] = per_head(jnp.exp(last - down) * step_down, tokens, width, head_dim)
-    growth[...] = per_head(jnp.exp(down), tokens, width, head_dim)
+    tail[...] = per_head(jnp.exp(last - down[...]) * step_down, tokens, width, head_dim)
     ends[...] = jnp.broadcast_to(jnp.exp(across[:, tokens - 1 : tokens]), ends.shape)
-    skip[...] = per_head(gains[...], 1, width, head_dim)
-    for copy in copies[3:]:
+    for copy in copies[2:]:
         copy.wait()
-    gated[...] = silu(gate[...].astype(F32))
     for source, kernel, first in ((mixer, taps, 0), (maps, map_taps, width)):
         count = kernel.shape[0]
         columns = source.shape[1]
@@ -149,22 +148,21 @@
         summed[:, first : first + columns] = total
 
 
-def decay(step_raw, decay_log, skip_gain, gate_input, mixer_input, state_maps, conv_input,
-          conv_maps):
+def decay(step_raw, decay_log, mixer_input, state_maps, conv_input, conv_maps):
     heads, tokens = step_raw.shape
     channels = mixer_input.shape[1]
-    square = (tokens, channels)
     width = channels + state_maps.shape[1]
-    operands = (step_raw, decay_log.reshape(1, heads), skip_gain.reshape(1, heads), gate_input,
-                mixer_input, state_maps, conv_input, conv_maps)
+    operands = (step_raw, decay_log.reshape(1, heads), conv_input, conv_maps, mixer_input,
+                state_maps)
+    scratch = (step_raw, operands[1], conv_input, conv_maps, mixer_input, state_maps)
     return call(
-        functools.partial(decay_body, heads, channels // heads),
+        functools.partial(decay_body, channels // heads),
         [HBM] * len(operands),
-        [((heads, tokens, tokens), F32), (square, F32), (square, F32),
-         ((heads, state_maps.shape[1] // 2), F32), (square, F32), ((1, channels), F32),
-         ((tokens, width), F32), ((conv_input.shape[0], width), F32)],
+        [((tokens, channels), F32), ((heads, state_maps.shape[1] // 2), F32),
+         ((tokens, width), F32), ((conv_input.shape[0], width), F32),
+         ((heads, tokens), F32), ((tokens, heads), F32), ((heads, tokens), F32)],
         10**8,
-        [pltpu.VMEM(x.shape, x.dtype) for x in operands]
+        [pltpu.VMEM(x.shape, x.dtype) for x in scratch]
         + [pltpu.VMEM((tokens + 8, max(channels, state_maps.shape[1])), F32),
            pltpu.SemaphoreType.DMA((len(operands),))],
     )(*(in_hbm(x) for x in operands))
@@ -200,10 +198,25 @@
     ).astype(BF16)
 
 
-def inside_body(heads, head_dim, values, projected, mix, skip, out):
-    tokens, _ = values.shape
+def inside_body(
+    heads, head_dim, values, projected, across, down, step, gate_hbm, skip_hbm, out, growth, gated,
+    gate, gains, sems
+):
+    copies = [pltpu.make_async_copy(gate_hbm, gate, sems.at[0]),
+              pltpu.make_async_copy(skip_hbm, gains, sems.at[1])]
+    for copy in copies:
+        copy.start()
+    tokens, width = values.shape
     state_dim = projected.shape[1] // 2
     scores = along(projected[:, state_dim:], projected[:, :state_dim], 1, 1)
+    to = lax.broadcasted_iota(jnp.int32, (tokens, tokens), 0)
+    since = lax.broadcasted_iota(jnp.int32, (tokens, tokens), 1)
+    causal = to >= since
+    growth[...] = per_head(jnp.exp(down[...]), tokens, width, head_dim)
+    for copy in copies:
+        copy.wait()
+    gated[...] = silu(gate[...].astype(F32))
+    skip = per_head(gains[...], 1, width, head_dim)
     pair = 128 // head_dim
     for first in range(0, heads, pair):
         columns = slice(first * head_dim, (first + pair) * head_dim)
@@ -211,18 +224,20 @@
         lane = lax.broadcasted_iota(jnp.int32, (tokens, pair * head_dim), 1) // head_dim
         total = None
         for k in range(pair):
-            weights = (scores * mix[first + k]).astype(BF16)
+            head = slice(first + k, first + k + 1)
+            spacing = jnp.where(causal, down[:, head] - across[head, :], -1e30)
+            weights = (scores * (jnp.exp(spacing) * step[head, :])).astype(BF16)
             part = along(weights, own, 1, 0)
             total = part if total is None else jnp.where(lane == k, part, total)
         out[:, columns] = total + skip[:, columns] * own.astype(F32)
 
 
-def fetches(me, chips, bys, weights, held, sems):
+def fetches(me, devices, bys, weights, held, sems):
     width = held.shape[2]
     copies = []
     for i, by in enumerate(bys):
-        chip = lax.rem(lax.div(me[0], CORES) + by + chips, chips)
-        at = pl.ds(pl.multiple_of(chip * width, width), width)
+        block = lax.rem(me[0] + CORES * by + devices, devices)
+        at = pl.ds(pl.multiple_of(block * width, width), width)
         for k, weight in enumerate(weights):
             place = len(weights) * i + k
             copies.append(
@@ -232,11 +247,11 @@
 
 
 def norm_body(
-    heads, head_dim, chips, bys, me, position, own_weight, other_weight, projected, inside, growth,
+    heads, head_dim, devices, bys, me, position, own_weight, other_weight, projected, inside, growth,
     gated, gain, *rest
 ):
     *messages, out, held, sems = rest
-    copies = fetches(me, chips, bys, (own_weight, other_weight), held, sems)
+    copies = fetches(me, devices, bys, (own_weight, other_weight), held, sems)
     for copy in copies:
         copy.start()
     _, width = inside.shape
@@ -273,80 +288,69 @@
         part[...] = along(own[...], held[2 * i], 1, 0)
 
 
+def split(total, outs):
+    rows = total.shape[0] // len(outs)
+    for i, out in enumerate(outs):
+        out[...] = total[i * rows : (i + 1) * rows].astype(out.dtype)
+
+
 def first_body(other, held, *rest):
-    count = len(rest) // (1 + CORES)
+    count = len(rest) // (1 + STREAMS)
     for i, part in enumerate(rest[:count]):
         total = part[...] + along(other[...], held[2 * i + 1], 1, 0)
-        outs = rest[count + CORES * i : count + CORES * (i + 1)]
-        width = total.shape[1] // CORES
-        for core, out in enumerate(outs):
-            out[...] = total[:, core * width : (core + 1) * width].astype(BF16)
-
-
-def rest_body(chips, bys, me, own, other, own_weight, other_weight, *rest):
-    *outs, held, mine, sems, mine_sems = rest
-    weights = (own_weight, other_weight)
-    width = outs[-1].shape[1]
-    copies = fetches(me, chips, bys, weights, held, sems)
-    at = pl.ds(pl.multiple_of(me[0] * width, width), width)
-    for k, weight in enumerate(weights):
-        copies.append(pltpu.make_async_copy(weight.at[:, at], mine.at[k], mine_sems.at[k]))
-    for copy in copies:
-        copy.start()
-    for i in range(len(bys)):
-        for copy in copies[2 * i : 2 * i + 2]:
-            copy.wait()
-        total = along(own[...], held[2 * i], 1, 0) + along(other[...], held[2 * i + 1], 1, 0)
-        for core in range(CORES):
-            outs[CORES * i + core][...] = total[:, core * width : (core + 1) * width]
-    for copy in copies[-2:]:
-        copy.wait()
-    outs[-1][...] = along(own[...], mine[0], 1, 0) + along(other[...], mine[1], 1, 0)
+        split(total, rest[count + STREAMS * i : count + STREAMS * (i + 1)])
+
+
+def rest_body(devices, bys, me, own, other, own_weight, other_weight, *outs):
+    width = outs[0].shape[1]
+    for i, by in enumerate(bys):
+        block = lax.rem(me[0] + CORES * by + devices, devices)
+        at = pl.ds(pl.multiple_of(block * width, width), width)
+        total = along(own[...], own_weight[:, at], 1, 0)
+        total = total + along(other[...], other_weight[:, at], 1, 0)
+        split(total, outs[STREAMS * i : STREAMS * (i + 1)])
 
 
 def project(normed, held, out_weight, other_weight, me, bys):
     devices = lax.axis_size("tensor")
-    chips = devices // CORES
-    far = chips // 2
+    far = devices // CORES // 2
     width = out_weight.shape[1] // devices
     tokens, depth = normed.shape
-    piece = (tokens, width)
-    work = 2 * tokens * depth * width * CORES
-    own = call(
-        own_body, [VMEM] * 2, [((tokens, CORES * width), F32)] * len(bys), work * len(bys)
-    )(normed, held)
+    piece = (tokens // STREAMS, width)
+    work = 2 * tokens * depth * width
+    own = call(own_body, [VMEM] * 2, [((tokens, width), F32)] * len(bys), work * len(bys))(
+        normed, held
+    )
     other = to_other_core(normed)
     parts = call(
-        first_body, [VMEM] * (2 + len(bys)), [(piece, BF16)] * (CORES * len(bys)), work * len(bys)
+        first_body, [VMEM] * (2 + len(bys)), [(piece, BF16)] * (STREAMS * len(bys)),
+        work * len(bys),
     )(other, held, *own)
-    ups, downs = list(parts[:CORES]), list(parts[CORES:])
+    ups, downs = list(parts[:STREAMS]), list(parts[STREAMS:])
     left = []
     for step in range(1, far):
-        left += [far - step] + ([step + 1 - far] if step + 1 < far else [])
+        left += [far - step, step + 1 - far]
     ups[0], normed, other = lax.optimization_barrier((ups[0], normed, other))
     parts = call(
-        functools.partial(rest_body, chips, left),
-        [SMEM, VMEM, VMEM, HBM, HBM],
-        [(piece, F32)] * (CORES * len(left) + 1),
+        functools.partial(rest_body, devices, left),
+        [SMEM] + [VMEM] * 4,
+        [(piece, F32)] * (STREAMS * len(left)),
         2 * work * len(left),
-        [pltpu.VMEM((2 * len(left), depth, CORES * width), BF16),
-         pltpu.VMEM((2, depth, width), BF16),
-         pltpu.SemaphoreType.DMA((2 * len(left),)), pltpu.SemaphoreType.DMA((2,))],
-    )(me, normed, other, in_hbm(out_weight), in_hbm(other_weight))
-    part = {(by, core): parts[CORES * i + core] for i, by in enumerate(left) for core in range(CORES)}
+    )(me, normed, other, out_weight, other_weight)
+    part = {
+        (by, i): parts[STREAMS * k + i] for k, by in enumerate(left) for i in range(STREAMS)
+    }
     for step in range(1, far + 1):
-        for core in range(CORES):
-            ups[core] = to_chip(ups[core], 1, core if step == far else CORES - 1)
+        for i in range(STREAMS):
+            ups[i] = to_chip(ups[i], 1)
             if step < far:
-                ups[core] = (ups[core].astype(F32) + part[far - step, core]).astype(BF16)
-                by = step + 1 - far
-                downs[core] = to_chip(downs[core], -1, CORES - 1 if by else core)
-                if by:
-                    downs[core] = (downs[core].astype(F32) + part[by, core]).astype(BF16)
-    total = parts[-1]
-    for arrived in downs + ups:
-        total = total + arrived.astype(F32)
-    return total.astype(BF16)
+                ups[i] = (ups[i].astype(F32) + part[far - step, i]).astype(BF16)
+                downs[i] = to_chip(downs[i], -1).astype(F32) + part[step + 1 - far, i]
+                if step + 1 < far:
+                    downs[i] = downs[i].astype(BF16)
+    return jnp.concatenate(
+        [(downs[i] + ups[i].astype(F32)).astype(BF16) for i in range(STREAMS)], axis=0
+    )
 
 
 def local(
@@ -370,11 +374,10 @@
     position = lax.axis_index("seq").reshape(1)
     ending, step_raw = lax.optimization_barrier((tail_of(mixer_input, state_maps), step_raw))
     leading = shifted(ending, "seq", 1)
-    mix, tail, growth, ends, gated, skip, summed, taps = decay(
-        step_raw, decay_log, skip_gain, gate_input, mixer_input, state_maps, conv_input,
-        conv_maps,
-    )
-    gated, out_weight = lax.optimization_barrier((gated, out_weight))
+    tail, ends, summed, taps, across, down, step = decay(
+        step_raw, decay_log, mixer_input, state_maps, conv_input, conv_maps
+    )
+    step, out_weight = lax.optimization_barrier((step, out_weight))
     other_weight = to_other_core(out_weight)
     rows = channels + 16 * pl.cdiv(2 * heads, 16)
     values, projected, sent = call(
@@ -388,16 +391,20 @@
         lax.ppermute(sent, "seq", [(i, (i + by) % pieces) for i in range(pieces)])
         for by in range(1, pieces)
     ]
-    (inside,) = call(
-        functools.partial(inside_body, heads, head_dim), [VMEM] * 4, [(square, F32)], 10**9
-    )(values, projected, mix, skip)
+    inside, growth, gated = call(
+        functools.partial(inside_body, heads, head_dim),
+        [VMEM] * 5 + [HBM] * 2,
+        [(square, F32)] * 3,
+        10**9,
+        [pltpu.VMEM(square, BF16), pltpu.VMEM((1, heads), F32), pltpu.SemaphoreType.DMA((2,))],
+    )(values, projected, across, down, step, in_hbm(gate_input), in_hbm(skip_gain.reshape(1, heads)))
     devices = lax.axis_size("tensor")
-    chips = devices // CORES
-    width = out_weight.shape[1] // chips
-    bys = (chips // 2, 1 - chips // 2)
-    count = CORES * len(bys)
+    width = out_weight.shape[1] // devices
+    far = devices // CORES // 2
+    bys = (far, 1 - far)
+    count = 2 * len(bys)
     normed, held = call(
-        functools.partial(norm_body, heads, head_dim, chips, bys),
+        functools.partial(norm_body, heads, head_dim, devices, bys),
         [SMEM, SMEM, HBM, HBM] + [VMEM] * (5 + len(messages)),
         [(square, BF16), ((count, channels, width), BF16)],
         10**8,

time: 145 us -> 98.2 us (0.68)
  the two profiles are of different devices: /device:TPU:33 before, /device:TPU:40 now
where the time goes in v4:
time: 98.2 us; the launch traced here: 98 us
  starting transfers between devices  68.7 us (70%)
  waiting for transfers between devices  18 us (18%)
  Pallas kernels  9.87 us (10%)
  other arithmetic  1.08 us (1%)
    ppermute x30, starting transfers between devices, to_chip(): lax.ppermute(shard, 'tensor', [(i, (i + CORES * by) % devices) for i in r...  59.4 us
    ppermute x30, waiting for transfers between devices, to_chip(): lax.ppermute(shard, 'tensor', [(i, (i + CORES * by) % devices) for i in r...  11.9 us
    ppermute x3, starting transfers between devices, local(): lax.ppermute(sent, 'seq', [(i, (i + by) % pieces) for i in range(pieces)])  5.5 us
    ppermute x3, waiting for transfers between devices, local(): lax.ppermute(sent, 'seq', [(i, (i + by) % pieces) for i in range(pieces)])  3.61 us
    ppermute x1, starting transfers between devices, shifted(): return lax.ppermute(shard, axis, pairs)  3.56 us
    pallas_call x1, Pallas kernels, project(): call(functools.partial(rest_body, devices, left), [SMEM] + [VMEM] * 4, [(...  3.33 us
    pallas_call x1, Pallas kernels, decay(): call(functools.partial(decay_body, channels // heads), [HBM] * len(operan...  2.17 us
  transfers between devices with their start and end apart: 36, of which 12 were waited for; matrix products, arithmetic and copies ran while one was open for 0% of the time, Pallas kernels for 5%

profile of v4, /device:TPU:40, one launch (start us, length us, event | category | flops | bytes accessed | tf_op | source)
XLA Modules:
  0.0 98.0 jit_solution(8128545032919658585)
XLA Ops:
  0.0 0.7 shard_map.100
  0.8 2.2 %shard_map.101 = (f32[256,256]{1,0:T(8,128)S(1)}, f32[4,128]{1,0:T(4,128)S(1)}, f32[256,512]{1,0:T(8,128)S(1)}, f32[4,512]{1,0:T(4,128)S(1)}, f32[4,256]{1,0:T(4...) custom-call(f32[4,256]{1,0:T(4,128)} %step_hbm, f32[1,4]{1,0:T(1,128)} %bitcast.6, bf16[4,256]{1,0:T(4,128)(2,1)} %taps_hbm.1, ...), custom_call_target="tpu_custom_call" | custom-call | flops 100000000 | bytes 1048576 | tf_op jit(solution)/shard_map/pallas_call | solution.py:158
  3.1 3.6 %collective-permute-start.1 = (bf16[16,512]{1,0:T(8,128)(2,1)S(1)}, bf16[16,512]{1,0:T(8,128)(2,1)S(1)}, u32[]{:S(2)}, u32[]{:S(2)}) collective-permute-start(bf16[16,512]{1,0:T(8,128)(2,1)S(1)} %shard_map.100), channel_id=1, source_target_pairs={{0,1},{1,2},{2,3},{4,5},{5,6},{6,7},{8,9},{9,10},{10,11},{12,13},{... | collective-permute-start | bytes 49160 | tf_op jit(solution)/shard_map/ppermute | solution.py:25
  6.7 1.4 %collective-permute-done.1.leading = bf16[16,512]{1,0:T(8,128)(2,1)S(1)} collective-permute-done((bf16[16,512]{1,0:T(8,128)(2,1)S(1)}, bf16[16,512]{1,0:T(8,128)(2,1)S(1)}, u32[]{:S(2)}, u32[]{:S(2)}) %collective-permute-start.1) | collective-permute-done | bytes 16416 | tf_op jit(solution)/shard_map/ppermute | solution.py:25
  8.5 3.9 %collective-permute-start.4 = (bf16[272,128]{1,0:T(8,128)(2,1)S(1)}, bf16[272,128]{1,0:T(8,128)(2,1)S(1)}, u32[]{:S(2)}, u32[]{:S(2)}) collective-permute-start(bf16[272,128]{1,0:T(8,128)(2,1)S(1)} %get-tuple-element.77), channel_id=1, source_target_pairs={{0,3},{1,0},{2,1},{3,2},{4,7},{5,4},{6,5},{7,6},{8,11},{9,8},{10,9... | collective-permute-start | bytes 208904 | tf_op jit(solution)/shard_map/ppermute | solution.py:391
  13.0 1.0 %collective-permute-start.2 = (bf16[272,128]{1,0:T(8,128)(2,1)S(1)}, bf16[272,128]{1,0:T(8,128)(2,1)S(1)}, u32[]{:S(2)}, u32[]{:S(2)}) collective-permute-start(bf16[272,128]{1,0:T(8,128)(2,1)S(1)} %get-tuple-element.77), channel_id=1, source_target_pairs={{0,1},{1,2},{2,3},{3,0},{4,5},{5,6},{6,7},{7,4},{8,9},{9,10},{10,1... | collective-permute-start | bytes 208904 | tf_op jit(solution)/shard_map/ppermute | solution.py:391
  14.0 1.4 %shard_map.103 = (f32[256,256]{1,0:T(8,128)S(1)}, f32[256,256]{1,0:T(8,128)S(1)}, f32[256,256]{1,0:T(8,128)S(1)}) custom-call(bf16[256,256]{1,0:T(8,128)(2,1)S(1)} %get-tuple-element.70.values, bf16[256,256]{1,0:T(8,128)(2,1)S(1)} %get-tuple-element.69.projected, f32[4,256]{1,0:T(4,128)S(1)} %get-tuple-element.71.across, ...), custom_call_target="tpu_custom_call" | custom-call | flops 1000000000 | bytes 1048576 | tf_op jit(solution)/shard_map/pallas_call | solution.py:394
  15.4 2.9 %collective-permute-done.3.rest_1_ = bf16[272,128]{1,0:T(8,128)(2,1)S(1)} collective-permute-done((bf16[272,128]{1,0:T(8,128)(2,1)S(1)}, bf16[272,128]{1,0:T(8,128)(2,1)S(1)}, u32[]{:S(2)}, u32[]{:S(2)}) %collective-permute-start.3) | collective-permute-done | bytes 69664 | tf_op jit(solution)/shard_map/ppermute | solution.py:391
  19.0 1.4 %shard_map.104 = (bf16[256,256]{1,0:T(8,128)(2,1)S(1)}, bf16[4,256,256]{2,1,0:T(8,128)(2,1)S(1)}) custom-call(s32[1]{0:T(128)} %bitcast.me, s32[1]{0:T(128)} %bitcast.1.position, bf16[256,8192]{1,0:T(8,128)(2,1)} %own_weight.1, bf16[256,8192]{1,0:T(8,128)(2,1)} %collective-permute-done.other_weight, bf16[256,256]{1,0:T(8,128)(2,1)S(1)} %get-tuple-element.69.projected, ...), custom_call_target="tpu_custom_call" | custom-call | flops 100000000 | bytes 1048576 | tf_op jit(solution)/shard_map/pallas_call | solution.py:406
  20.8 1.1 %collective-permute-done.5.other = bf16[256,256]{1,0:T(8,128)(2,1)S(1)} collective-permute-done((bf16[256,256]{1,0:T(8,128)(2,1)S(1)}, bf16[256,256]{1,0:T(8,128)(2,1)S(1)}, u32[]{:S(2)}, u32[]{:S(2)}) %collective-permute-start.5) | collective-permute-done | bytes 131104 | tf_op jit(solution)/shard_map/ppermute | solution.py:30
  22.1 2.9 %collective-permute-start.13 = (bf16[128,256]{1,0:T(8,128)(2,1)S(1)}, bf16[128,256]{1,0:T(8,128)(2,1)S(1)}, u32[]{:S(2)}, u32[]{:S(2)}) collective-permute-start(bf16[128,256]{1,0:T(8,128)(2,1)S(1)} %get-tuple-element.93), channel_id=1, source_target_pairs={{0,8},{4,12},{8,16},{12,20},{16,24},{20,28},{24,32},{28,36},{32,40... | collective-permute-start | bytes 196616 | tf_op jit(solution)/shard_map/ppermute | solution.py:35
  25.0 19.7 %collective-permute-start.6 = (bf16[128,256]{1,0:T(8,128)(2,1)S(1)}, bf16[128,256]{1,0:T(8,128)(2,1)S(1)}, u32[]{:S(2)}, u32[]{:S(2)}) collective-permute-start(bf16[128,256]{1,0:T(8,128)(2,1)S(1)} %get-tuple-element.82), channel_id=1, source_target_pairs={{0,120},{4,124},{8,0},{12,4},{16,8},{20,12},{24,16},{28,20},{32,24... | collective-permute-start | bytes 196616 | tf_op jit(solution)/shard_map/ppermute | solution.py:35
  44.8 1.9 %collective-permute-start.21 = (bf16[128,256]{1,0:T(8,128)(2,1)S(1)}, bf16[128,256]{1,0:T(8,128)(2,1)S(1)}, u32[]{:S(2)}, u32[]{:S(2)}) collective-permute-start(bf16[128,256]{1,0:T(8,128)(2,1)S(1)} %get-tuple-element.101), channel_id=1, source_target_pairs={{0,120},{4,124},{8,0},{12,4},{16,8},{20,12},{24,16},{28,20},{32,24... | collective-permute-start | bytes 196616 | tf_op jit(solution)/shard_map/ppermute | solution.py:35
  46.8 3.3 %shard_map.107 = (f32[128,256]{1,0:T(8,128)S(1)}, f32[128,256]{1,0:T(8,128)S(1)}, f32[128,256]{1,0:T(8,128)S(1)}, f32[128,256]{1,0:T(8,128)S(1)}, f32[128,256]{1...) custom-call(s32[1]{0:T(128)} %bitcast.me, ...), custom_call_target="tpu_custom_call" | custom-call | flops 939524096 | bytes 1048576 | tf_op jit(solution)/shard_map/pallas_call | solution.py:334
  50.3 3.5 %collective-permute-start.7 = (bf16[128,256]{1,0:T(8,128)(2,1)S(1)}, bf16[128,256]{1,0:T(8,128)(2,1)S(1)}, u32[]{:S(2)}, u32[]{:S(2)}) collective-permute-start(bf16[128,256]{1,0:T(8,128)(2,1)S(1)} %add_convert_fusion.27), channel_id=1, source_target_pairs={{0,120},{4,124},{8,0},{12,4},{16,8},{20,12},{24,16},{28,20},{32,24... | collective-permute-start | bytes 196616 | tf_op jit(solution)/shard_map/ppermute | solution.py:35
  53.8 2.0 %collective-permute-start.22 = (bf16[128,256]{1,0:T(8,128)(2,1)S(1)}, bf16[128,256]{1,0:T(8,128)(2,1)S(1)}, u32[]{:S(2)}, u32[]{:S(2)}) collective-permute-start(bf16[128,256]{1,0:T(8,128)(2,1)S(1)} %add_convert_fusion.13), channel_id=1, source_target_pairs={{0,120},{4,124},{8,0},{12,4},{16,8},{20,12},{24,16},{28,20},{32,24... | collective-permute-start | bytes 196616 | tf_op jit(solution)/shard_map/ppermute | solution.py:35
  56.3 3.3 %collective-permute-start.8 = (bf16[128,256]{1,0:T(8,128)(2,1)S(1)}, bf16[128,256]{1,0:T(8,128)(2,1)S(1)}, u32[]{:S(2)}, u32[]{:S(2)}) collective-permute-start(bf16[128,256]{1,0:T(8,128)(2,1)S(1)} %add_convert_fusion.26), channel_id=1, source_target_pairs={{0,120},{4,124},{8,0},{12,4},{16,8},{20,12},{24,16},{28,20},{32,24... | collective-permute-start | bytes 196616 | tf_op jit(solution)/shard_map/ppermute | solution.py:35
  59.7 2.0 %collective-permute-start.23 = (bf16[128,256]{1,0:T(8,128)(2,1)S(1)}, bf16[128,256]{1,0:T(8,128)(2,1)S(1)}, u32[]{:S(2)}, u32[]{:S(2)}) collective-permute-start(bf16[128,256]{1,0:T(8,128)(2,1)S(1)} %add_convert_fusion.12), channel_id=1, source_target_pairs={{0,120},{4,124},{8,0},{12,4},{16,8},{20,12},{24,16},{28,20},{32,24... | collective-permute-start | bytes 196616 | tf_op jit(solution)/shard_map/ppermute | solution.py:35
  62.3 3.3 %collective-permute-start.9 = (bf16[128,256]{1,0:T(8,128)(2,1)S(1)}, bf16[128,256]{1,0:T(8,128)(2,1)S(1)}, u32[]{:S(2)}, u32[]{:S(2)}) collective-permute-start(bf16[128,256]{1,0:T(8,128)(2,1)S(1)} %add_convert_fusion.25), channel_id=1, source_target_pairs={{0,120},{4,124},{8,0},{12,4},{16,8},{20,12},{24,16},{28,20},{32,24... | collective-permute-start | bytes 196616 | tf_op jit(solution)/shard_map/ppermute | solution.py:35
  65.7 2.1 %collective-permute-start.24 = (bf16[128,256]{1,0:T(8,128)(2,1)S(1)}, bf16[128,256]{1,0:T(8,128)(2,1)S(1)}, u32[]{:S(2)}, u32[]{:S(2)}) collective-permute-start(bf16[128,256]{1,0:T(8,128)(2,1)S(1)} %add_convert_fusion.11), channel_id=1, source_target_pairs={{0,120},{4,124},{8,0},{12,4},{16,8},{20,12},{24,16},{28,20},{32,24... | collective-permute-start | bytes 196616 | tf_op jit(solution)/shard_map/ppermute | solution.py:35
  68.5 3.3 %collective-permute-start.10 = (bf16[128,256]{1,0:T(8,128)(2,1)S(1)}, bf16[128,256]{1,0:T(8,128)(2,1)S(1)}, u32[]{:S(2)}, u32[]{:S(2)}) collective-permute-start(bf16[128,256]{1,0:T(8,128)(2,1)S(1)} %add_convert_fusion.24), channel_id=1, source_target_pairs={{0,120},{4,124},{8,0},{12,4},{16,8},{20,12},{24,16},{28,20},{32,24... | collective-permute-start | bytes 196616 | tf_op jit(solution)/shard_map/ppermute | solution.py:35
  71.8 2.2 %collective-permute-start.25 = (bf16[128,256]{1,0:T(8,128)(2,1)S(1)}, bf16[128,256]{1,0:T(8,128)(2,1)S(1)}, u32[]{:S(2)}, u32[]{:S(2)}) collective-permute-start(bf16[128,256]{1,0:T(8,128)(2,1)S(1)} %add_convert_fusion.10), channel_id=1, source_target_pairs={{0,120},{4,124},{8,0},{12,4},{16,8},{20,12},{24,16},{28,20},{32,24... | collective-permute-start | bytes 196616 | tf_op jit(solution)/shard_map/ppermute | solution.py:35
  74.2 1.0 %collective-permute-done.17 = bf16[128,256]{1,0:T(8,128)(2,1)S(1)} collective-permute-done((bf16[128,256]{1,0:T(8,128)(2,1)S(1)}, bf16[128,256]{1,0:T(8,128)(2,1)S(1)}, u32[]{:S(2)}, u32[]{:S(2)}) %collective-permute-start.17) | collective-permute-done | bytes 65568 | tf_op jit(solution)/shard_map/ppermute | solution.py:35
  75.4 3.5 %collective-permute-start.11 = (bf16[128,256]{1,0:T(8,128)(2,1)S(1)}, bf16[128,256]{1,0:T(8,128)(2,1)S(1)}, u32[]{:S(2)}, u32[]{:S(2)}) collective-permute-start(bf16[128,256]{1,0:T(8,128)(2,1)S(1)} %add_convert_fusion.23), channel_id=1, source_target_pairs={{0,120},{4,124},{8,0},{12,4},{16,8},{20,12},{24,16},{28,20},{32,24... | collective-permute-start | bytes 196616 | tf_op jit(solution)/shard_map/ppermute | solution.py:35
  79.0 1.1 %collective-permute-start.26 = (bf16[128,256]{1,0:T(8,128)(2,1)S(1)}, bf16[128,256]{1,0:T(8,128)(2,1)S(1)}, u32[]{:S(2)}, u32[]{:S(2)}) collective-permute-start(bf16[128,256]{1,0:T(8,128)(2,1)S(1)} %add_convert_fusion.9), channel_id=1, source_target_pairs={{0,120},{4,124},{8,0},{12,4},{16,8},{20,12},{24,16},{28,20},{32,24... | collective-permute-start | bytes 196616 | tf_op jit(solution)/shard_map/ppermute | solution.py:35
  80.3 0.9 collective-permute-start.33
  81.4 3.3 %collective-permute-start.12 = (bf16[128,256]{1,0:T(8,128)(2,1)S(1)}, bf16[128,256]{1,0:T(8,128)(2,1)S(1)}, u32[]{:S(2)}, u32[]{:S(2)}) collective-permute-start(bf16[128,256]{1,0:T(8,128)(2,1)S(1)} %add_convert_fusion.22), channel_id=1, source_target_pairs={{0,120},{4,124},{8,0},{12,4},{16,8},{20,12},{24,16},{28,20},{32,24... | collective-permute-start | bytes 196616 | tf_op jit(solution)/shard_map/ppermute | solution.py:35
  84.8 1.3 %collective-permute-start.27 = (bf16[128,256]{1,0:T(8,128)(2,1)S(1)}, bf16[128,256]{1,0:T(8,128)(2,1)S(1)}, u32[]{:S(2)}, u32[]{:S(2)}) collective-permute-start(bf16[128,256]{1,0:T(8,128)(2,1)S(1)} %add_convert_fusion.8), channel_id=1, source_target_pairs={{0,120},{4,124},{8,0},{12,4},{16,8},{20,12},{24,16},{28,20},{32,24... | collective-permute-start | bytes 196616 | tf_op jit(solution)/shard_map/ppermute | solution.py:35
  86.1 0.9 collective-permute-start.34
  87.2 4.5 %collective-permute-done.34 = bf16[128,256]{1,0:T(8,128)(2,1)S(1)} collective-permute-done((bf16[128,256]{1,0:T(8,128)(2,1)S(1)}, bf16[128,256]{1,0:T(8,128)(2,1)S(1)}, u32[]{:S(2)}, u32[]{:S(2)}) %collective-permute-start.34) | collective-permute-done | bytes 65568 | tf_op jit(solution)/shard_map/ppermute | solution.py:35
  91.9 0.8 collective-permute-done.20
  92.7 4.6 %collective-permute-done.35 = bf16[128,256]{1,0:T(8,128)(2,1)S(1)} collective-permute-done((bf16[128,256]{1,0:T(8,128)(2,1)S(1)}, bf16[128,256]{1,0:T(8,128)(2,1)S(1)}, u32[]{:S(2)}, u32[]{:S(2)}) %collective-permute-start.35) | collective-permute-done | bytes 65568 | tf_op jit(solution)/shard_map/ppermute | solution.py:35
  (81 shorter events, 6.5 us)
Async XLA Ops:
  2.9 16.1 %collective-permute-start = (bf16[256,8192]{1,0:T(8,128)(2,1)}, bf16[256,8192]{1,0:T(8,128)(2,1)}, u32[]{:S(2)}, u32[]{:S(2)}) collective-permute-start(bf16[256,8192]{1,0:T(8,128)(2,1)} %own_weight.1), channel_id=1, source_target_pairs={{0,4},{4,0},{8,12},{12,8},{16,20},{20,16},{24,28},{28,24},{32,36},... | collective-permute-start | bytes 12582920 | tf_op jit(solution)/shard_map/ppermute | solution.py:30
  8.5 6.9 %collective-permute-start.4 = (bf16[272,128]{1,0:T(8,128)(2,1)S(1)}, bf16[272,128]{1,0:T(8,128)(2,1)S(1)}, u32[]{:S(2)}, u32[]{:S(2)}) collective-permute-start(bf16[272,128]{1,0:T(8,128)(2,1)S(1)} %get-tuple-element.77), channel_id=1, source_target_pairs={{0,3},{1,0},{2,1},{3,2},{4,7},{5,4},{6,5},{7,6},{8,11},{9,8},{10,9... | collective-permute-start | bytes 208904 | tf_op jit(solution)/shard_map/ppermute | solution.py:391
  12.4 5.9 %collective-permute-start.3 = (bf16[272,128]{1,0:T(8,128)(2,1)S(1)}, bf16[272,128]{1,0:T(8,128)(2,1)S(1)}, u32[]{:S(2)}, u32[]{:S(2)}) collective-permute-start(bf16[272,128]{1,0:T(8,128)(2,1)S(1)} %get-tuple-element.77), channel_id=1, source_target_pairs={{0,2},{1,3},{2,0},{3,1},{4,6},{5,7},{6,4},{7,5},{8,10},{9,11},{10,... | collective-permute-start | bytes 208904 | tf_op jit(solution)/shard_map/ppermute | solution.py:391
  13.0 6.0 %collective-permute-start.2 = (bf16[272,128]{1,0:T(8,128)(2,1)S(1)}, bf16[272,128]{1,0:T(8,128)(2,1)S(1)}, u32[]{:S(2)}, u32[]{:S(2)}) collective-permute-start(bf16[272,128]{1,0:T(8,128)(2,1)S(1)} %get-tuple-element.77), channel_id=1, source_target_pairs={{0,1},{1,2},{2,3},{3,0},{4,5},{5,6},{6,7},{7,4},{8,9},{9,10},{10,1... | collective-permute-start | bytes 208904 | tf_op jit(solution)/shard_map/ppermute | solution.py:391
  22.1 28.0 %collective-permute-start.13 = (bf16[128,256]{1,0:T(8,128)(2,1)S(1)}, bf16[128,256]{1,0:T(8,128)(2,1)S(1)}, u32[]{:S(2)}, u32[]{:S(2)}) collective-permute-start(bf16[128,256]{1,0:T(8,128)(2,1)S(1)} %get-tuple-element.93), channel_id=1, source_target_pairs={{0,8},{4,12},{8,16},{12,20},{16,24},{20,28},{24,32},{28,36},{32,40... | collective-permute-start | bytes 196616 | tf_op jit(solution)/shard_map/ppermute | solution.py:35
  25.0 25.3 %collective-permute-start.6 = (bf16[128,256]{1,0:T(8,128)(2,1)S(1)}, bf16[128,256]{1,0:T(8,128)(2,1)S(1)}, u32[]{:S(2)}, u32[]{:S(2)}) collective-permute-start(bf16[128,256]{1,0:T(8,128)(2,1)S(1)} %get-tuple-element.82), channel_id=1, source_target_pairs={{0,120},{4,124},{8,0},{12,4},{16,8},{20,12},{24,16},{28,20},{32,24... | collective-permute-start | bytes 196616 | tf_op jit(solution)/shard_map/ppermute | solution.py:35
  44.8 9.1 %collective-permute-start.21 = (bf16[128,256]{1,0:T(8,128)(2,1)S(1)}, bf16[128,256]{1,0:T(8,128)(2,1)S(1)}, u32[]{:S(2)}, u32[]{:S(2)}) collective-permute-start(bf16[128,256]{1,0:T(8,128)(2,1)S(1)} %get-tuple-element.101), channel_id=1, source_target_pairs={{0,120},{4,124},{8,0},{12,4},{16,8},{20,12},{24,16},{28,20},{32,24... | collective-permute-start | bytes 196616 | tf_op jit(solution)/shard_map/ppermute | solution.py:35
  46.6 9.2 %collective-permute-start.28 = (bf16[128,256]{1,0:T(8,128)(2,1)S(1)}, bf16[128,256]{1,0:T(8,128)(2,1)S(1)}, u32[]{:S(2)}, u32[]{:S(2)}) collective-permute-start(bf16[128,256]{1,0:T(8,128)(2,1)S(1)} %get-tuple-element.109), channel_id=1, source_target_pairs={{0,8},{4,12},{8,16},{12,20},{16,24},{20,28},{24,32},{28,36},{32,40... | collective-permute-start | bytes 196616 | tf_op jit(solution)/shard_map/ppermute | solution.py:35
  50.2 6.0 %collective-permute-start.14 = (bf16[128,256]{1,0:T(8,128)(2,1)S(1)}, bf16[128,256]{1,0:T(8,128)(2,1)S(1)}, u32[]{:S(2)}, u32[]{:S(2)}) collective-permute-start(bf16[128,256]{1,0:T(8,128)(2,1)S(1)} %add_convert_fusion.21), channel_id=1, source_target_pairs={{0,8},{4,12},{8,16},{12,20},{16,24},{20,28},{24,32},{28,36},{32,40... | collective-permute-start | bytes 196616 | tf_op jit(solution)/shard_map/ppermute | solution.py:35
  50.3 6.0 %collective-permute-start.7 = (bf16[128,256]{1,0:T(8,128)(2,1)S(1)}, bf16[128,256]{1,0:T(8,128)(2,1)S(1)}, u32[]{:S(2)}, u32[]{:S(2)}) collective-permute-start(bf16[128,256]{1,0:T(8,128)(2,1)S(1)} %add_convert_fusion.27), channel_id=1, source_target_pairs={{0,120},{4,124},{8,0},{12,4},{16,8},{20,12},{24,16},{28,20},{32,24... | collective-permute-start | bytes 196616 | tf_op jit(solution)/shard_map/ppermute | solution.py:35
  53.8 5.8 %collective-permute-start.22 = (bf16[128,256]{1,0:T(8,128)(2,1)S(1)}, bf16[128,256]{1,0:T(8,128)(2,1)S(1)}, u32[]{:S(2)}, u32[]{:S(2)}) collective-permute-start(bf16[128,256]{1,0:T(8,128)(2,1)S(1)} %add_convert_fusion.13), channel_id=1, source_target_pairs={{0,120},{4,124},{8,0},{12,4},{16,8},{20,12},{24,16},{28,20},{32,24... | collective-permute-start | bytes 196616 | tf_op jit(solution)/shard_map/ppermute | solution.py:35
  55.9 5.8 %collective-permute-start.29 = (bf16[128,256]{1,0:T(8,128)(2,1)S(1)}, bf16[128,256]{1,0:T(8,128)(2,1)S(1)}, u32[]{:S(2)}, u32[]{:S(2)}) collective-permute-start(bf16[128,256]{1,0:T(8,128)(2,1)S(1)} %add_convert_fusion.7), channel_id=1, source_target_pairs={{0,8},{4,12},{8,16},{12,20},{16,24},{20,28},{24,32},{28,36},{32,40... | collective-permute-start | bytes 196616 | tf_op jit(solution)/shard_map/ppermute | solution.py:35
  56.1 6.0 %collective-permute-start.15 = (bf16[128,256]{1,0:T(8,128)(2,1)S(1)}, bf16[128,256]{1,0:T(8,128)(2,1)S(1)}, u32[]{:S(2)}, u32[]{:S(2)}) collective-permute-start(bf16[128,256]{1,0:T(8,128)(2,1)S(1)} %add_convert_fusion.20), channel_id=1, source_target_pairs={{0,8},{4,12},{8,16},{12,20},{16,24},{20,28},{24,32},{28,36},{32,40... | collective-permute-start | bytes 196616 | tf_op jit(solution)/shard_map/ppermute | solution.py:35
  56.3 6.0 %collective-permute-start.8 = (bf16[128,256]{1,0:T(8,128)(2,1)S(1)}, bf16[128,256]{1,0:T(8,128)(2,1)S(1)}, u32[]{:S(2)}, u32[]{:S(2)}) collective-permute-start(bf16[128,256]{1,0:T(8,128)(2,1)S(1)} %add_convert_fusion.26), channel_id=1, source_target_pairs={{0,120},{4,124},{8,0},{12,4},{16,8},{20,12},{24,16},{28,20},{32,24... | collective-permute-start | bytes 196616 | tf_op jit(solution)/shard_map/ppermute | solution.py:35
  59.7 6.0 %collective-permute-start.23 = (bf16[128,256]{1,0:T(8,128)(2,1)S(1)}, bf16[128,256]{1,0:T(8,128)(2,1)S(1)}, u32[]{:S(2)}, u32[]{:S(2)}) collective-permute-start(bf16[128,256]{1,0:T(8,128)(2,1)S(1)} %add_convert_fusion.12), channel_id=1, source_target_pairs={{0,120},{4,124},{8,0},{12,4},{16,8},{20,12},{24,16},{28,20},{32,24... | collective-permute-start | bytes 196616 | tf_op jit(solution)/shard_map/ppermute | solution.py:35
  61.7 6.1 %collective-permute-start.30 = (bf16[128,256]{1,0:T(8,128)(2,1)S(1)}, bf16[128,256]{1,0:T(8,128)(2,1)S(1)}, u32[]{:S(2)}, u32[]{:S(2)}) collective-permute-start(bf16[128,256]{1,0:T(8,128)(2,1)S(1)} %add_convert_fusion.6), channel_id=1, source_target_pairs={{0,8},{4,12},{8,16},{12,20},{16,24},{20,28},{24,32},{28,36},{32,40... | collective-permute-start | bytes 196616 | tf_op jit(solution)/shard_map/ppermute | solution.py:35
  62.2 6.1 %collective-permute-start.16 = (bf16[128,256]{1,0:T(8,128)(2,1)S(1)}, bf16[128,256]{1,0:T(8,128)(2,1)S(1)}, u32[]{:S(2)}, u32[]{:S(2)}) collective-permute-start(bf16[128,256]{1,0:T(8,128)(2,1)S(1)} %add_convert_fusion.19), channel_id=1, source_target_pairs={{0,8},{4,12},{8,16},{12,20},{16,24},{20,28},{24,32},{28,36},{32,40... | collective-permute-start | bytes 196616 | tf_op jit(solution)/shard_map/ppermute | solution.py:35
  62.3 6.1 %collective-permute-start.9 = (bf16[128,256]{1,0:T(8,128)(2,1)S(1)}, bf16[128,256]{1,0:T(8,128)(2,1)S(1)}, u32[]{:S(2)}, u32[]{:S(2)}) collective-permute-start(bf16[128,256]{1,0:T(8,128)(2,1)S(1)} %add_convert_fusion.25), channel_id=1, source_target_pairs={{0,120},{4,124},{8,0},{12,4},{16,8},{20,12},{24,16},{28,20},{32,24... | collective-permute-start | bytes 196616 | tf_op jit(solution)/shard_map/ppermute | solution.py:35
  65.7 6.1 %collective-permute-start.24 = (bf16[128,256]{1,0:T(8,128)(2,1)S(1)}, bf16[128,256]{1,0:T(8,128)(2,1)S(1)}, u32[]{:S(2)}, u32[]{:S(2)}) collective-permute-start(bf16[128,256]{1,0:T(8,128)(2,1)S(1)} %add_convert_fusion.11), channel_id=1, source_target_pairs={{0,120},{4,124},{8,0},{12,4},{16,8},{20,12},{24,16},{28,20},{32,24... | collective-permute-start | bytes 196616 | tf_op jit(solution)/shard_map/ppermute | solution.py:35
  67.8 6.3 %collective-permute-start.31 = (bf16[128,256]{1,0:T(8,128)(2,1)S(1)}, bf16[128,256]{1,0:T(8,128)(2,1)S(1)}, u32[]{:S(2)}, u32[]{:S(2)}) collective-permute-start(bf16[128,256]{1,0:T(8,128)(2,1)S(1)} %add_convert_fusion.5), channel_id=1, source_target_pairs={{0,8},{4,12},{8,16},{12,20},{16,24},{20,28},{24,32},{28,36},{32,40... | collective-permute-start | bytes 196616 | tf_op jit(solution)/shard_map/ppermute | solution.py:35
  68.3 6.9 %collective-permute-start.17 = (bf16[128,256]{1,0:T(8,128)(2,1)S(1)}, bf16[128,256]{1,0:T(8,128)(2,1)S(1)}, u32[]{:S(2)}, u32[]{:S(2)}) collective-permute-start(bf16[128,256]{1,0:T(8,128)(2,1)S(1)} %add_convert_fusion.18), channel_id=1, source_target_pairs={{0,8},{4,12},{8,16},{12,20},{16,24},{20,28},{24,32},{28,36},{32,40... | collective-permute-start | bytes 196616 | tf_op jit(solution)/shard_map/ppermute | solution.py:35
  68.5 6.9 %collective-permute-start.10 = (bf16[128,256]{1,0:T(8,128)(2,1)S(1)}, bf16[128,256]{1,0:T(8,128)(2,1)S(1)}, u32[]{:S(2)}, u32[]{:S(2)}) collective-permute-start(bf16[128,256]{1,0:T(8,128)(2,1)S(1)} %add_convert_fusion.24), channel_id=1, source_target_pairs={{0,120},{4,124},{8,0},{12,4},{16,8},{20,12},{24,16},{28,20},{32,24... | collective-permute-start | bytes 196616 | tf_op jit(solution)/shard_map/ppermute | solution.py:35
  71.8 7.1 %collective-permute-start.25 = (bf16[128,256]{1,0:T(8,128)(2,1)S(1)}, bf16[128,256]{1,0:T(8,128)(2,1)S(1)}, u32[]{:S(2)}, u32[]{:S(2)}) collective-permute-start(bf16[128,256]{1,0:T(8,128)(2,1)S(1)} %add_convert_fusion.10), channel_id=1, source_target_pairs={{0,120},{4,124},{8,0},{12,4},{16,8},{20,12},{24,16},{28,20},{32,24... | collective-permute-start | bytes 196616 | tf_op jit(solution)/shard_map/ppermute | solution.py:35
  74.1 6.2 %collective-permute-start.32 = (bf16[128,256]{1,0:T(8,128)(2,1)S(1)}, bf16[128,256]{1,0:T(8,128)(2,1)S(1)}, u32[]{:S(2)}, u32[]{:S(2)}) collective-permute-start(bf16[128,256]{1,0:T(8,128)(2,1)S(1)} %add_convert_fusion.4), channel_id=1, source_target_pairs={{0,8},{4,12},{8,16},{12,20},{16,24},{20,28},{24,32},{28,36},{32,40... | collective-permute-start | bytes 196616 | tf_op jit(solution)/shard_map/ppermute | solution.py:35
  75.2 6.0 %collective-permute-start.18 = (bf16[128,256]{1,0:T(8,128)(2,1)S(1)}, bf16[128,256]{1,0:T(8,128)(2,1)S(1)}, u32[]{:S(2)}, u32[]{:S(2)}) collective-permute-start(bf16[128,256]{1,0:T(8,128)(2,1)S(1)} %add_convert_fusion.17), channel_id=1, source_target_pairs={{0,8},{4,12},{8,16},{12,20},{16,24},{20,28},{24,32},{28,36},{32,40... | collective-permute-start | bytes 196616 | tf_op jit(solution)/shard_map/ppermute | solution.py:35
  75.4 6.0 %collective-permute-start.11 = (bf16[128,256]{1,0:T(8,128)(2,1)S(1)}, bf16[128,256]{1,0:T(8,128)(2,1)S(1)}, u32[]{:S(2)}, u32[]{:S(2)}) collective-permute-start(bf16[128,256]{1,0:T(8,128)(2,1)S(1)} %add_convert_fusion.23), channel_id=1, source_target_pairs={{0,120},{4,124},{8,0},{12,4},{16,8},{20,12},{24,16},{28,20},{32,24... | collective-permute-start | bytes 196616 | tf_op jit(solution)/shard_map/ppermute | solution.py:35
  79.0 5.8 %collective-permute-start.26 = (bf16[128,256]{1,0:T(8,128)(2,1)S(1)}, bf16[128,256]{1,0:T(8,128)(2,1)S(1)}, u32[]{:S(2)}, u32[]{:S(2)}) collective-permute-start(bf16[128,256]{1,0:T(8,128)(2,1)S(1)} %add_convert_fusion.9), channel_id=1, source_target_pairs={{0,120},{4,124},{8,0},{12,4},{16,8},{20,12},{24,16},{28,20},{32,24... | collective-permute-start | bytes 196616 | tf_op jit(solution)/shard_map/ppermute | solution.py:35
  80.3 5.8 %collective-permute-start.33 = (bf16[128,256]{1,0:T(8,128)(2,1)S(1)}, bf16[128,256]{1,0:T(8,128)(2,1)S(1)}, u32[]{:S(2)}, u32[]{:S(2)}) collective-permute-start(bf16[128,256]{1,0:T(8,128)(2,1)S(1)} %add_convert_fusion.3), channel_id=1, source_target_pairs={{0,8},{4,12},{8,16},{12,20},{16,24},{20,28},{24,32},{28,36},{32,40... | collective-permute-start | bytes 196616 | tf_op jit(solution)/shard_map/ppermute | solution.py:35
  81.3 5.8 %collective-permute-start.19 = (bf16[128,256]{1,0:T(8,128)(2,1)S(1)}, bf16[128,256]{1,0:T(8,128)(2,1)S(1)}, u32[]{:S(2)}, u32[]{:S(2)}) collective-permute-start(bf16[128,256]{1,0:T(8,128)(2,1)S(1)} %add_convert_fusion.16), channel_id=1, source_target_pairs={{0,8},{4,12},{8,16},{12,20},{16,24},{20,28},{24,32},{28,36},{32,40... | collective-permute-start | bytes 196616 | tf_op jit(solution)/shard_map/ppermute | solution.py:35
  81.4 10.5 %collective-permute-start.12 = (bf16[128,256]{1,0:T(8,128)(2,1)S(1)}, bf16[128,256]{1,0:T(8,128)(2,1)S(1)}, u32[]{:S(2)}, u32[]{:S(2)}) collective-permute-start(bf16[128,256]{1,0:T(8,128)(2,1)S(1)} %add_convert_fusion.22), channel_id=1, source_target_pairs={{0,120},{4,124},{8,0},{12,4},{16,8},{20,12},{24,16},{28,20},{32,24... | collective-permute-start | bytes 196616 | tf_op jit(solution)/shard_map/ppermute | solution.py:35
  84.8 7.9 %collective-permute-start.27 = (bf16[128,256]{1,0:T(8,128)(2,1)S(1)}, bf16[128,256]{1,0:T(8,128)(2,1)S(1)}, u32[]{:S(2)}, u32[]{:S(2)}) collective-permute-start(bf16[128,256]{1,0:T(8,128)(2,1)S(1)} %add_convert_fusion.8), channel_id=1, source_target_pairs={{0,120},{4,124},{8,0},{12,4},{16,8},{20,12},{24,16},{28,20},{32,24... | collective-permute-start | bytes 196616 | tf_op jit(solution)/shard_map/ppermute | solution.py:35
  87.1 5.6 %collective-permute-start.20 = (bf16[128,256]{1,0:T(8,128)(2,1)S(1)}, bf16[128,256]{1,0:T(8,128)(2,1)S(1)}, u32[]{:S(2)}, u32[]{:S(2)}) collective-permute-start(bf16[128,256]{1,0:T(8,128)(2,1)S(1)} %add_convert_fusion.15), channel_id=1, source_target_pairs={{0,8},{4,12},{8,16},{12,20},{16,24},{20,28},{24,32},{28,36},{32,40... | collective-permute-start | bytes 196616 | tf_op jit(solution)/shard_map/ppermute | solution.py:35
  (6 other events, 64.4 us)
